TPU v7x, 256 devices: a 8x8x2 block of a 8x8x16 slice. The times are simulated.
256 devices in a mesh: replica: 2 (over z), expert: 64 (over y, x), sub: 2 (over core).
Axes of the slice: x: 8, y: 8, z: 2, core: 2. Of those that a mesh axis runs over, the one named last changes fastest.
The devices are a block of a 8x8x16 slice.
Arguments:
- tokens: bfloat16 [2048, 7168], P(('replica', 'expert', 'sub')), parts along dimension 0, may hold values from -6 to 6
- expert_ids: int32 [2048, 8], P(('replica', 'expert', 'sub')), parts along dimension 0, may hold values from 0 to 31, all different within a row; in each aligned block of 8 rows (0 to 7, 8 to 15, ...) at most 3 rows name the same one
- route_levels: int32 [2048, 8], P(('replica', 'expert', 'sub')), parts along dimension 0, may hold values from 1 to 255
- gate_proj: bfloat16 [64, 7168, 512], P('expert', None, 'sub'), may hold values from -0.0625 to 0.0625
- up_proj: bfloat16 [64, 7168, 512], P('expert', None, 'sub'), may hold values from -0.0625 to 0.0625
- down_proj: bfloat16 [64, 512, 7168], P('expert', 'sub'), may hold values from -0.1875 to 0.1875
Outputs:
- moe_out: bfloat16 [2048, 7168], P(('replica', 'expert', 'sub')), parts along dimension 0
There are 2 independent parts, one for each index of `replica`. A program takes and returns all parts, laid end to end along the dimension named above; an argument that names none is the same for every part. Nothing has to cross between parts.
Inputs may be any that keep to these rules, and one draw needn't show every extreme that they name: `expert_ids`: each row names 8 different experts; among the 8 rows of one device no expert is named more than 3 times, and in some devices' rows one is named exactly 3 times.
All inputs are finite; a program needn't handle non-finite values.
Results may differ from a plain program's by a relative error of at most 0.013.
Values may be sent and summed in bfloat16 or wider, within the bound.
No kernel may reach another device: no remote copies, remote signals or barrier semaphores. Data moves between devices by JAX's collectives and lax.ppermute only.
A program may use at most 448 MiB of HBM per device.

v0:
```python
import jax
import jax.numpy as jnp
from jax import lax
from jax.sharding import PartitionSpec as P


def cut_along(x, dim, length):
    before, after = (x.shape[:dim], x.shape[dim + 1 :])
    return jnp.moveaxis(x.reshape(*before, length, -1, *after), dim, 0)


def summed_on_arrival(x, axis, dim):
    tiles = cut_along(x, dim, lax.axis_size(axis))
    arrived = lax.all_to_all(tiles, axis, split_axis=0, concat_axis=0, tiled=True)
    return arrived.astype(jnp.float32).sum(axis=0)


def partner_2(block, axis, stride):
    count = lax.axis_size(axis)
    route = []
    for low in range(count):
        high = low | 1 << stride
        if high != low and high < count:
            route += [(low, high), (high, low)]
    return lax.ppermute(block, axis, route)


def laid_out(tiles, dim):
    tiles = jnp.moveaxis(tiles, 0, dim)
    lengths = tiles.shape
    return tiles.reshape(*lengths[:dim], lengths[dim] * lengths[dim + 1], *lengths[dim + 2 :])


def sent_to_all(x, axis):
    length = lax.axis_size(axis)
    return lax.all_to_all(jnp.broadcast_to(x[None], (length, *x.shape)), axis, 0, 0, tiled=True)


def collect(x, axis, dim):
    return laid_out(sent_to_all(x, axis), dim)


def local(tokens, expert_ids, route_levels, gate_proj, up_proj, down_proj):
    rows_here, width = tokens.shape
    picks = expert_ids.shape[1]
    experts = lax.axis_size("expert") * lax.axis_size("sub") // 4
    capacity = rows_here * picks * 3 // (experts * 2)
    pair_count = rows_here * picks
    flat_ids = expert_ids.reshape(pair_count)
    onehot = (flat_ids[:, None] == jnp.arange(experts, dtype=jnp.int32)[None, :]).astype(jnp.int32)
    before = jnp.cumsum(onehot, axis=0, dtype=jnp.int32) - onehot
    slot_of = jnp.sum(before * onehot, axis=1)
    position = flat_ids * capacity + slot_of
    placed = (position[:, None] == jnp.arange(experts * capacity, dtype=jnp.int32)[None, :]).astype(
        jnp.float32
    )
    shares = route_levels.astype(jnp.float32)
    shares = shares / jnp.sum(shares, axis=1, keepdims=True)
    owner_rows = (
        jnp.arange(pair_count, dtype=jnp.int32)[None, :] // picks
        == jnp.arange(rows_here, dtype=jnp.int32)[:, None]
    ).astype(jnp.float32)
    sender = jnp.dot(owner_rows, placed, precision=lax.Precision.HIGHEST)
    weighting = jnp.dot(
        owner_rows * shares.reshape(1, pair_count), placed, precision=lax.Precision.HIGHEST
    )
    outgoing = jnp.dot(sender.T.astype(jnp.bfloat16), tokens, preferred_element_type=jnp.float32)
    outgoing = outgoing.astype(jnp.bfloat16).reshape(experts, 1, capacity, width)
    gate_local = gate_proj[0]
    up_local = up_proj[0]
    down_local = down_proj[0]
    parity = lax.axis_index("expert") % 2
    half_cols = width // 2
    buffer = outgoing.reshape(experts, capacity, 2, half_cols).transpose(0, 2, 1, 3)
    buffer = buffer.reshape(2 * experts, capacity, half_cols)
    arrived = lax.all_to_all(buffer, "expert", split_axis=0, concat_axis=0, tiled=True)
    partner = partner_2(arrived, "expert", 0)
    lower = jnp.where(parity == 0, arrived, partner)
    upper = jnp.where(parity == 0, partner, arrived)
    whole_rows = jnp.concatenate([lower, upper], axis=2)
    both_cores = collect(whole_rows[:, None], "sub", 1)
    leading = both_cores.shape[:-1]
    flat_rows = both_cores.reshape(-1, width)
    gate_vals = jnp.dot(flat_rows, gate_local, preferred_element_type=jnp.float32)
    up_vals = jnp.dot(flat_rows, up_local, preferred_element_type=jnp.float32)
    hidden = (jax.nn.silu(gate_vals) * up_vals).astype(jnp.bfloat16)
    terms = jnp.dot(hidden, down_local, preferred_element_type=jnp.float32).astype(jnp.bfloat16)
    send_terms = terms.reshape(leading + (width,))
    groups, _, items, _ = send_terms.shape
    kept = lax.optimization_barrier(send_terms.reshape(2 * groups, items, width))
    halves = summed_on_arrival(kept.astype(jnp.float32).astype(jnp.bfloat16), "sub", 2)
    fourth = width // 4
    mine = lax.dynamic_slice_in_dim(halves, parity * fourth, fourth, 2)
    other = lax.dynamic_slice_in_dim(halves, (1 - parity) * fourth, fourth, 2)
    total = mine + partner_2(other.astype(jnp.bfloat16), "expert", 0).astype(other.dtype)
    back = lax.all_to_all(
        total.astype(jnp.bfloat16), ("expert", "sub"), split_axis=0, concat_axis=0, tiled=True
    )
    arranged = back.reshape(groups // 2, 2, 2, items, fourth).transpose(0, 3, 2, 1, 4)
    returned = arranged.reshape(groups // 2, items, width)
    results = jnp.sum(returned.reshape(experts, -1, capacity, width), axis=1, dtype=jnp.float32)
    rounded = lax.optimization_barrier(
        results.reshape(experts * capacity, width).astype(jnp.bfloat16)
    )
    mixed = jnp.dot(
        weighting,
        rounded.astype(jnp.float32),
        precision=lax.Precision.HIGHEST,
        preferred_element_type=jnp.float32,
    )
    return mixed.astype(jnp.bfloat16)


def solution(mesh):
    return jax.shard_map(
        local,
        mesh=mesh,
        in_specs=(
            P(("replica", "expert", "sub"), None),
            P(("replica", "expert", "sub"), None),
            P(("replica", "expert", "sub"), None),
            P("expert", None, "sub"),
            P("expert", None, "sub"),
            P("expert", "sub", None),
        ),
        out_specs=P(("replica", "expert", "sub"), None),
        check_vma=False,
    )
```

profile of v0, /device:TPU:514, one launch (start us, length us, event | category | flops | bytes accessed | tf_op | source)
XLA Modules:
  0.0 289.2 jit_solution(7033853999286134103)
XLA Ops:
  0.0 0.0 copy-start
  0.0 0.8 reshape.71
  0.8 0.1 fusion.12
  0.9 0.1 reduce_window_sum.11
  1.0 0.2 select_reduce_fusion
  1.2 0.2 convolution_convert_fusion.3
  1.4 0.0 copy-done
  1.4 0.6 convolution_convert_fusion.1
  1.9 1.0 reshape_reshape.12
  3.0 0.7 copy.37
  3.7 66.0 %all_to_all.20 = bf16[64,3,3584]{2,1,0:T(4,128)(2,1)S(1)} all-to-all(bf16[64,3,3584]{2,1,0:T(4,128)(2,1)S(1)} %bitcast.37), channel_id=1, replica_groups=mesh['replica'=2,'expert'=64,'sub'=2] {'expert'}, dimensions={0} | all-to-all | bytes 2752512 | tf_op jit(solution)/shard_map/all_to_all | solution.py:76
  69.7 1.4 copy.26
  71.1 0.7 collective-permute-start
  71.8 26.0 %collective-permute-done = bf16[64,3,3584]{2,0,1:T(8,128)(2,1)S(1)} collective-permute-done((bf16[64,3,3584]{2,0,1:T(8,128)(2,1)}, bf16[64,3,3584]{2,0,1:T(8,128)(2,1)S(1)}, u32[]{:S(2)}, u32[]{:S(2)}) %collective-permute-start) | collective-permute-done | bytes 1376288 | tf_op jit(solution)/shard_map/ppermute | solution.py:25
  97.8 2.9 %broadcast_select_fusion.1 = (bf16[64,3,3584]{2,1,0:T(4,128)(2,1)S(1)}, bf16[64,3,3584]{2,1,0:T(4,128)(2,1)S(1)}) fusion(bf16[64,3,3584]{2,1,0:T(4,128)(2,1)S(1)} %all_to_all.20, pred[]{:T(512)S(6)} %eq.60, bf16[64,3,3584]{2,0,1:T(8,128)(2,1)S(1)} %collective-permute-done), kind=kLoop, calls=%fused_computation.13 | loop fusion | flops 1376256 | bytes 5505025 | tf_op jit(solution)/shard_map/jit(_where)/select_n | solution.py:78
  100.7 1.6 pad_maximum_fusion
  102.3 1.1 copy.29
  103.4 0.6 broadcast_in_dim.2
  104.0 9.4 %all_to_all.21 = bf16[2,64,1,3,7168]{4,1,3,2,0:T(8,128)(2,1)} all-to-all(bf16[2,64,1,3,7168]{4,1,3,2,0:T(8,128)(2,1)S(1)} %broadcast_in_dim.2), channel_id=1, replica_groups=mesh['replica'=2,'expert'=64,'sub'=2] {'sub'}, dimensions={0} | all-to-all | bytes 11010048 | tf_op jit(solution)/shard_map/all_to_all | solution.py:36
  113.4 10.2 %copy.30 = bf16[64,2,1,3,7168]{4,3,1,0,2:T(4,128)(2,1)} copy(bf16[64,2,1,3,7168]{4,0,3,2,1:T(8,128)(2,1)} %bitcast.34) | data formatting | bytes 11010048 | tf_op jit(solution)/shard_map/transpose | solution.py:29
  123.6 13.0 %reshape_reshape.13 = bf16[384,7168]{1,0:T(8,128)(2,1)} reshape(bf16[64,2,1,3,7168]{4,3,1,0,2:T(4,128)(2,1)} %copy.30) | data formatting | bytes 11010048 | tf_op jit(solution)/shard_map/reshape;reshape | solution.py:83
  136.6 5.4 %fusion.3 = f32[384,256]{1,0:T(8,128)S(1)} fusion(bf16[384,7168]{1,0:T(8,128)(2,1)} %reshape_reshape.13, bf16[1,7168,256]{2,1,0:T(8,128)(2,1)} %param.9), kind=kOutput, calls=%fused_computation.8 | convolution fusion | flops 1409286144 | bytes 9568256 | tf_op jit(solution)/shard_map/dot_general | solution.py:84
  142.0 0.9 copy-done.6
  143.0 1.6 fusion.8
  144.5 0.4 copy-done.4
  145.0 4.0 %convolution_convert_fusion = bf16[384,7168]{1,0:T(8,128)(2,1)} fusion(bf16[384,256]{1,0:T(8,128)(2,1)S(1)} %fusion.8, bf16[1,256,7168]{2,1,0:T(8,128)(2,1)S(1)} %copy-done.4), kind=kOutput, calls=%fused_computation.1 | convolution fusion | flops 1412038656 | bytes 9371648 | tf_op jit(solution)/shard_map/dot_general | solution.py:87
  149.0 12.3 %reshape_reshape.14 = bf16[128,3,7168]{2,1,0:T(4,128)(2,1)} reshape(bf16[384,7168]{1,0:T(8,128)(2,1)} %convolution_convert_fusion) | data formatting | bytes 11010048 | tf_op jit(solution)/shard_map/reshape;reshape | solution.py:90
  161.3 12.1 %copy.31 = bf16[128,3,7168]{0,2,1:T(8,128)(2,1)} copy(bf16[128,3,7168]{2,1,0:T(4,128)(2,1)} %reshape_reshape.14) | data formatting | bytes 11010048 | tf_op jit(solution)/shard_map/optimization_barrier | solution.py:90
  173.4 2.9 %copy.32 = bf16[2,128,3,3584]{1,3,2,0:T(8,128)(2,1)S(1)} copy(bf16[2,128,3,3584]{1,3,0,2:T(8,128)(2,1)} %bitcast.35) | data formatting | bytes 11010048 | tf_op jit(solution)/shard_map/transpose | solution.py:9
  176.3 8.2 %all_to_all.22 = bf16[2,128,3,3584]{1,3,2,0:T(8,128)(2,1)S(1)} all-to-all(bf16[2,128,3,3584]{1,3,2,0:T(8,128)(2,1)S(1)} %copy.32), channel_id=1, replica_groups=mesh['replica'=2,'expert'=64,'sub'=2] {'sub'}, dimensions={0} | all-to-all | bytes 11010048 | tf_op jit(solution)/shard_map/all_to_all | solution.py:14
  184.5 1.0 convert_reduce_fusion
  185.4 2.4 copy-done.2
  187.8 0.2 dynamic-slice_convert_fusion
  188.0 0.6 collective-permute-start.1
  188.6 31.9 %collective-permute-done.1 = bf16[128,3,1792]{0,2,1:T(8,128)(2,1)S(1)} collective-permute-done((bf16[128,3,1792]{0,2,1:T(8,128)(2,1)S(1)}, bf16[128,3,1792]{0,2,1:T(8,128)(2,1)S(1)}, u32[]{:S(2)}, u32[]{:S(2)}) %collective-permute-start.1) | collective-permute-done | bytes 1376288 | tf_op jit(solution)/shard_map/ppermute | solution.py:25
  220.6 2.0 add_convert_fusion
  222.6 0.0 copy-start.5
  222.6 3.3 %copy.34 = bf16[128,3,1792]{2,1,0:T(4,128)(2,1)} copy(bf16[128,3,1792]{0,2,1:T(8,128)(2,1)S(1)} %add_convert_fusion) | data formatting | bytes 2752512 | tf_op jit(solution)/shard_map/convert_element_type | solution.py:97
  225.9 12.5 %all-to-all-start.3 = ((bf16[128,3,1792]{2,1,0:T(4,128)(2,1)}), bf16[128,3,1792]{2,1,0:T(4,128)(2,1)S(1)}, u32[]{:S(2)}, u32[]{:S(2)}) async-start(bf16[128,3,1792]{2,1,0:T(4,128)(2,1)} %copy.34), calls=%async_computation.3 | async-start | bytes 3670016 | tf_op jit(solution)/shard_map/all_to_all | solution.py:96
  238.4 0.1 convert_reduce_fusion.1
  238.5 0.1 convert_divide_fusion
  238.6 0.1 mul.34
  238.7 0.2 fusion.11
  238.9 46.8 %all-to-all-done.3 = bf16[128,3,1792]{2,1,0:T(4,128)(2,1)S(1)} async-done(((bf16[128,3,1792]{2,1,0:T(4,128)(2,1)}), bf16[128,3,1792]{2,1,0:T(4,128)(2,1)S(1)}, u32[]{:S(2)}, u32[]{:S(2)}) %all-to-all-start.3) | async-done | bytes 1376288 | tf_op jit(solution)/shard_map/all_to_all | solution.py:96
  285.6 1.2 copy.47
  286.8 1.1 reshape_reshape.15
  287.9 1.3 convolution_convert_fusion.2
  289.2 0.0 copy-done.1
  (8 shorter events, 0.0 us)
Async XLA Ops:
  0.0 1.4 copy-start
  71.1 26.7 %collective-permute-start = (bf16[64,3,3584]{2,0,1:T(8,128)(2,1)}, bf16[64,3,3584]{2,0,1:T(8,128)(2,1)S(1)}, u32[]{:S(2)}, u32[]{:S(2)}) collective-permute-start(bf16[64,3,3584]{2,0,1:T(8,128)(2,1)} %copy.26), channel_id=1, source_target_pairs={{0,2},{2,0},{4,6},{6,4},{8,10},{10,8},{12,14},{14,12},{16,18},{18,... | collective-permute-start | bytes 4128776 | tf_op jit(solution)/shard_map/ppermute | solution.py:25
  136.6 5.4 %copy-start.3 = (bf16[384,7168]{1,0:T(8,128)(2,1)S(1)}, bf16[384,7168]{1,0:T(8,128)(2,1)}, u32[]{:S(2)}) copy-start(bf16[384,7168]{1,0:T(8,128)(2,1)} %reshape_reshape.13) | copy-start | bytes 16515076
  136.6 6.3 %copy-start.6 = (bf16[1,7168,256]{2,1,0:T(8,128)(2,1)S(1)}, bf16[1,7168,256]{2,1,0:T(8,128)(2,1)}, u32[]{:S(2)}) copy-start(bf16[1,7168,256]{2,1,0:T(8,128)(2,1)} %param.10) | copy-start | bytes 11010052
  143.0 2.0 copy-start.4
  185.4 2.4 copy-start.2
  188.0 32.6 %collective-permute-start.1 = (bf16[128,3,1792]{0,2,1:T(8,128)(2,1)S(1)}, bf16[128,3,1792]{0,2,1:T(8,128)(2,1)S(1)}, u32[]{:S(2)}, u32[]{:S(2)}) collective-permute-start(bf16[128,3,1792]{0,2,1:T(8,128)(2,1)S(1)} %dynamic-slice_convert_fusion), channel_id=1, source_target_pairs={{0,2},{2,0},{4,6},{6,4},{8,10},{10,8},{12,14},{14,12},{16,18},{18,... | collective-permute-start | bytes 4128776 | tf_op jit(solution)/shard_map/ppermute | solution.py:25
  222.6 15.8 %copy-start.5 = (s32[8,8]{1,0:T(8,128)S(1)}, s32[8,8]{1,0:T(8,128)}, u32[]{:S(2)}) copy-start(s32[8,8]{1,0:T(8,128)} %param.8) | copy-start | bytes 772
  225.9 59.7 %all-to-all-start.3 = ((bf16[128,3,1792]{2,1,0:T(4,128)(2,1)}), bf16[128,3,1792]{2,1,0:T(4,128)(2,1)S(1)}, u32[]{:S(2)}, u32[]{:S(2)}) async-start(bf16[128,3,1792]{2,1,0:T(4,128)(2,1)} %copy.34), calls=%async_computation.3 | async-start | bytes 3670016 | tf_op jit(solution)/shard_map/all_to_all | solution.py:96
  285.6 3.6 %copy-start.1 = (bf16[8,7168]{1,0:T(8,128)(2,1)S(1)}, bf16[8,7168]{1,0:T(8,128)(2,1)}, u32[]{:S(2)}) copy-start(bf16[8,7168]{1,0:T(8,128)(2,1)} %param.6) | copy-start | bytes 344068
where the time goes:
time: 295 us; the launch traced here: 289 us
  waiting for transfers between devices  105 us (36%)
  blocking collectives  83.5 us (28%)
  local copies, waits for them, and re-layouts  65.8 us (22%)
  starting transfers between devices  13.8 us (5%)
  matrix products  13.2 us (4%)
  other arithmetic  8.02 us (3%)
    all_to_all x1, blocking collectives, local(): lax.all_to_all(buffer, 'expert', split_axis=0, concat_axis=0, tiled=True)  66 us
    ppermute x2, waiting for transfers between devices, partner_2(): return lax.ppermute(block, axis, route)  57.9 us
    all_to_all x1, waiting for transfers between devices, local(): lax.all_to_all(total.astype(jnp.bfloat16), ('expert', 'sub'), split_axis=...  46.8 us
    another operation x1, local copies, waits for them, and re-layouts, local(): flat_rows = both_cores.reshape(-1, width)  13 us
    all_to_all x1, starting transfers between devices, local(): lax.all_to_all(total.astype(jnp.bfloat16), ('expert', 'sub'), split_axis=...  12.5 us
    another operation x1, local copies, waits for them, and re-layouts, local(): send_terms.reshape(2 * groups, items, width)  12.3 us
    optimization_barrier x1, local copies, waits for them, and re-layouts, local(): lax.optimization_barrier(send_terms.reshape(2 * groups, items, width))  12.1 us
    transpose x1, local copies, waits for them, and re-layouts, laid_out(): tiles = jnp.moveaxis(tiles, 0, dim)  10.2 us
  transfers between devices with their start and end apart: 3, of which 3 were waited for; matrix products, arithmetic and copies ran while one was open for 0% of the time, Pallas kernels for 0%

commit v1 on v0

v1 whole, which is shorter than its diff:
```python
import math

import jax
import jax.numpy as jnp
from jax import lax
from jax.experimental import pallas as pl
from jax.experimental.pallas import tpu as pltpu
from jax.sharding import PartitionSpec as P

GROUP = ("expert", "sub")
INFO = 128
CAP = 3


def crossing_groups(side):
    def at(y, x, c):
        return (y * side + x) * 2 + c

    r = range(side)
    along_y = [[[at(y, x, c) for y in r] for x in r] for c in (0, 1)]
    along_x = [[[at(y, x, c) for x in r] for y in r] for c in (0, 1)]
    return along_y[0] + along_x[1], along_x[0] + along_y[1]


def route_kernel(experts_ref, rows_ref, send_ref, mix_ref, *, side, picks, width):
    toks = rows_ref.shape[0]
    info = rows_ref[:, width:].astype(jnp.float32)
    info = jnp.concatenate([info, jnp.zeros((INFO - toks, INFO), jnp.float32)], axis=0)
    info = info.T
    ids = info[:picks]
    levels = info[picks : 2 * picks]
    total = jnp.sum(levels, axis=0, keepdims=True)
    total = jnp.where(total == 0.0, 1.0, total)
    named, share = [], []
    for i in range(side):
        hit = ids == experts_ref[i].astype(jnp.float32)
        named.append(jnp.sum(jnp.where(hit, 1.0, 0.0), axis=0, keepdims=True))
        share.append(jnp.sum(jnp.where(hit, levels, 0.0), axis=0, keepdims=True) / total)
    named_all = jnp.concatenate(named, axis=0)
    per = toks // side
    a = lax.broadcasted_iota(jnp.int32, (INFO, INFO), 0)
    b = lax.broadcasted_iota(jnp.int32, (INFO, INFO), 1)
    earlier = jnp.where((a // per == b // per) & (a < b), 1.0, 0.0).astype(jnp.bfloat16)
    slot = jnp.dot(named_all.astype(jnp.bfloat16), earlier, preferred_element_type=jnp.float32)
    own = (
        lax.broadcasted_iota(jnp.int32, (side, INFO), 1) // per
        == lax.broadcasted_iota(jnp.int32, (side, INFO), 0)
    )
    pieces, mixes = [], []
    for i in range(side):
        for s in range(CAP):
            here = jnp.where(slot[i : i + 1] == float(s), named[i], 0.0)
            pieces.append(jnp.where(own, here, 0.0))
            mixes.append(jnp.where(own, here * share[i], 0.0))
    select = jnp.concatenate(pieces, axis=0)[:, :toks].astype(jnp.bfloat16)
    count = select.shape[0]
    mix = jnp.concatenate(mixes, axis=0)
    pad = -count % INFO
    mix = jnp.concatenate([mix, jnp.zeros((pad, INFO), jnp.float32)], axis=0).T
    mix = mix[:toks, :count]
    high = mix.astype(jnp.bfloat16)
    rest = mix - high.astype(jnp.float32)
    mid = rest.astype(jnp.bfloat16)
    low = (rest - mid.astype(jnp.float32)).astype(jnp.bfloat16)
    mix_ref[0:toks] = high
    mix_ref[toks : 2 * toks] = mid
    mix_ref[2 * toks : 3 * toks] = low
    step = 1024
    for n in range(width // step):
        cols = slice(n * step, (n + 1) * step)
        send_ref[:, cols] = jnp.dot(
            select, rows_ref[:, cols], preferred_element_type=jnp.float32
        ).astype(jnp.bfloat16)


def hidden_kernel(x_ref, ga_ref, gb_ref, ua_ref, ub_ref, out_ref, acc_ref):
    k = pl.program_id(0)
    part = ga_ref.shape[1]

    @pl.when(k == 0)
    def _():
        acc_ref[...] = jnp.zeros_like(acc_ref)

    x = x_ref[...]
    for n, w in enumerate((ga_ref, gb_ref, ua_ref, ub_ref)):
        acc_ref[:, n * part : (n + 1) * part] += jnp.dot(
            x, w[...], preferred_element_type=jnp.float32
        )

    @pl.when(k == pl.num_programs(0) - 1)
    def _():
        gate = acc_ref[:, : 2 * part]
        up = acc_ref[:, 2 * part :]
        out_ref[...] = (gate / (1.0 + jnp.exp(-gate)) * up).astype(jnp.bfloat16)


def down_kernel(h_ref, da_ref, db_ref, out_ref):
    part = da_ref.shape[0]
    out_ref[...] = (
        jnp.dot(h_ref[:, :part], da_ref[...], preferred_element_type=jnp.float32)
        + jnp.dot(h_ref[:, part:], db_ref[...], preferred_element_type=jnp.float32)
    ).astype(jnp.bfloat16)


def mix_kernel(mix_ref, rows_ref, out_ref):
    toks = out_ref.shape[0]
    y = jnp.dot(mix_ref[...], rows_ref[...], preferred_element_type=jnp.float32)
    out_ref[...] = (y[:toks] + y[toks : 2 * toks] + y[2 * toks :]).astype(jnp.bfloat16)


def local(tokens, expert_ids, route_levels, gate_proj, up_proj, down_proj):
    mine, width = tokens.shape
    picks = expert_ids.shape[1]
    chips = lax.axis_size("expert")
    side = math.isqrt(chips)
    first, second = crossing_groups(side)
    core = lax.axis_index("sub")
    chip = lax.axis_index("expert")
    y, x = chip // side, chip % side
    i = jnp.arange(side, dtype=jnp.int32)
    experts = jnp.where(core == 0, (y * side + i) // 2, (i * side + x) // 2)

    swap = [(0, 1), (1, 0)]
    gate_peer, up_peer, down_peer = (
        lax.ppermute(w, "sub", swap) for w in (gate_proj, up_proj, down_proj)
    )

    info = jnp.concatenate(
        [expert_ids, route_levels, jnp.zeros((mine, INFO - 2 * picks), jnp.int32)], axis=1
    )
    rows = jnp.concatenate([tokens, info.astype(jnp.bfloat16)], axis=1)
    rows = lax.all_gather(rows, GROUP, axis=0, tiled=True, axis_index_groups=first)

    toks = side * mine
    slots = toks * CAP
    send, mix = pl.pallas_call(
        lambda *refs: route_kernel(*refs, side=side, picks=picks, width=width),
        out_shape=(
            jax.ShapeDtypeStruct((slots, width), jnp.bfloat16),
            jax.ShapeDtypeStruct((3 * toks, slots), jnp.bfloat16),
        ),
        in_specs=[
            pl.BlockSpec(memory_space=pltpu.SMEM),
            pl.BlockSpec(memory_space=pltpu.VMEM),
        ],
        out_specs=(
            pl.BlockSpec(memory_space=pltpu.VMEM),
            pl.BlockSpec(memory_space=pltpu.VMEM),
        ),
        name="route",
    )(experts, rows)

    def crossed(block):
        block = block.reshape(side, -1, width)
        block = lax.all_to_all(block, GROUP, 0, 0, tiled=True, axis_index_groups=second)
        return block.reshape(-1, width)

    arrived = crossed(send)

    part = gate_proj.shape[2]
    kb = 1024
    weight = pl.BlockSpec((None, kb, part), lambda k: (0, k, 0))
    hidden = pl.pallas_call(
        hidden_kernel,
        grid=(width // kb,),
        in_specs=[pl.BlockSpec((slots, kb), lambda k: (0, k)), weight, weight, weight, weight],
        out_specs=pl.BlockSpec((slots, 2 * part), lambda k: (0, 0)),
        out_shape=jax.ShapeDtypeStruct((slots, 2 * part), jnp.bfloat16),
        scratch_shapes=[pltpu.VMEM((slots, 4 * part), jnp.float32)],
        name="hidden",
    )(arrived, gate_proj, gate_peer, up_proj, up_peer)

    nb = 1024
    down = pl.BlockSpec((None, part, nb), lambda n: (0, 0, n))
    terms = pl.pallas_call(
        down_kernel,
        grid=(width // nb,),
        in_specs=[pl.BlockSpec((slots, 2 * part), lambda n: (0, 0)), down, down],
        out_specs=pl.BlockSpec((slots, nb), lambda n: (0, n)),
        out_shape=jax.ShapeDtypeStruct((slots, width), jnp.bfloat16),
        name="down",
    )(hidden, down_proj, down_peer)

    returned = crossed(terms)

    mixed = pl.pallas_call(
        mix_kernel,
        grid=(width // nb,),
        in_specs=[
            pl.BlockSpec((3 * toks, slots), lambda n: (0, 0)),
            pl.BlockSpec((slots, nb), lambda n: (0, n)),
        ],
        out_specs=pl.BlockSpec((toks, nb), lambda n: (0, n)),
        out_shape=jax.ShapeDtypeStruct((toks, width), jnp.bfloat16),
        name="mix",
    )(mix, returned)

    sums = lax.all_to_all(
        mixed.reshape(side, mine, width), GROUP, 0, 0, tiled=True, axis_index_groups=first
    )
    return jnp.sum(sums.astype(jnp.float32), axis=0).astype(jnp.bfloat16)


def solution(mesh):
    return jax.shard_map(
        local,
        mesh=mesh,
        in_specs=(
            P(("replica", "expert", "sub"), None),
            P(("replica", "expert", "sub"), None),
            P(("replica", "expert", "sub"), None),
            P("expert", None, "sub"),
            P("expert", None, "sub"),
            P("expert", "sub", None),
        ),
        out_specs=P(("replica", "expert", "sub"), None),
        check_vma=False,
    )
```

time: 295 us -> 194 us (0.66); the launches traced: 289 us -> 193 us
  waiting for transfers between devices: 105 us -> 32.9 us
  local copies, waits for them, and re-layouts: 65.8 us -> 4.55 us
  Pallas kernels: 0 us -> 27.6 us
  blocking collectives: 83.5 us -> 104 us
  matrix products: 13.2 us -> 0 us
  starting transfers between devices: 13.8 us -> 21.5 us
  other arithmetic: 8.02 us -> 2.76 us
    ppermute x2 -> x3, waiting for transfers between devices: 57.9 us -> 9.58 us  [local(): lax.ppermute(w, 'sub', swap)]
    all_gather x0 -> x1, blocking collectives: none -> 36.7 us  [local(): lax.all_gather(rows, GROUP, axis=0, tiled=True, axis_index_groups=first)]
    pallas_call x0 -> x4, Pallas kernels: none -> 27.6 us  [the longest x1 9.93 us: local(): pl.pallas_call(hidden_kernel, grid=(width // kb,), in_specs=[pl.BlockSpec...]
    another operation x4 -> x0, local copies, waits for them, and re-layouts: 27.4 us -> none  [the longest x1 13 us: local(): flat_rows = both_cores.reshape(-1, width)]
    all_to_all x1, waiting for transfers between devices: 46.8 us -> 23.4 us  [crossed(): lax.all_to_all(block, GROUP, 0, 0, tiled=True, axis_index_groups=second)]
    all_to_all x3 -> x2, blocking collectives: 83.5 us -> 67.3 us  [the longest x1 46.3 us: crossed(): lax.all_to_all(block, GROUP, 0, 0, tiled=True, axis_index_groups=second)]
    transpose x3 -> x0, local copies, waits for them, and re-layouts: 14.3 us -> none  [the longest x1 10.2 us: laid_out(): tiles = jnp.moveaxis(tiles, 0, dim)]
    dot_general x7 -> x0, matrix products: 13.2 us -> none  [the longest x1 5.39 us: local(): jnp.dot(flat_rows, gate_local, preferred_element_type=jnp.float32)]
  transfers between devices with their start and end apart: 3 -> 4, of which waited for: 3 -> 3; matrix products, arithmetic and copies ran while one was open for 0% -> 0% of each run, Pallas kernels for 0% -> 5%
where the time goes in v1:
time: 194 us; the launch traced here: 193 us
  blocking collectives  104 us (54%)
  waiting for transfers between devices  32.9 us (17%)
  Pallas kernels  27.6 us (14%)
  starting transfers between devices  21.5 us (11%)
  local copies, waits for them, and re-layouts  4.55 us (2%)
  other arithmetic  2.76 us (1%)
    all_to_all x1, blocking collectives, crossed(): lax.all_to_all(block, GROUP, 0, 0, tiled=True, axis_index_groups=second)  46.3 us
    all_gather x1, blocking collectives, local(): lax.all_gather(rows, GROUP, axis=0, tiled=True, axis_index_groups=first)  36.7 us
    all_to_all x1, waiting for transfers between devices, crossed(): lax.all_to_all(block, GROUP, 0, 0, tiled=True, axis_index_groups=second)  23.4 us
    all_to_all x1, blocking collectives, local(): lax.all_to_all(mixed.reshape(side, mine, width), GROUP, 0, 0, tiled=True,...  21 us
    all_to_all x1, starting transfers between devices, crossed(): lax.all_to_all(block, GROUP, 0, 0, tiled=True, axis_index_groups=second)  21 us
    pallas_call x1, Pallas kernels, local(): pl.pallas_call(hidden_kernel, grid=(width // kb,), in_specs=[pl.BlockSpec...  9.93 us
    ppermute x3, waiting for transfers between devices, local(): lax.ppermute(w, 'sub', swap)  9.58 us
    pallas_call x1, Pallas kernels, local(): pl.pallas_call(down_kernel, grid=(width // nb,), in_specs=[pl.BlockSpec((...  7.87 us
  transfers between devices with their start and end apart: 4, of which 3 were waited for; matrix products, arithmetic and copies ran while one was open for 0% of the time, Pallas kernels for 5%

profile of v1, /device:TPU:514, one launch (start us, length us, event | category | flops | bytes accessed | tf_op | source)
XLA Modules:
  0.0 193.4 jit_solution(12488898575999975653)
XLA Ops:
  0.0 0.7 convert.9
  0.7 0.7 convert.10
  1.4 1.0 concatenate.6
  2.4 36.7 %all_gather.3.refs_1_ = bf16[64,7296]{1,0:T(8,128)(2,1)} all-gather(bf16[8,7296]{1,0:T(8,128)(2,1)S(1)} %concatenate.6), channel_id=1, replica_groups={{0,16,32,48,64,80,96,112},{2,18,34,50,66,82,98,114},{4,20,36,52,68,84,1..., dimensions={0}, use_global_device_ids=true | all-gather | bytes 1050624 | tf_op jit(solution)/shard_map/all_gather | solution.py:132
  39.1 0.6 broadcast_select_fusion.refs_0_
  39.7 3.9 %route.1 = (bf16[192,7168]{1,0:T(8,128)(2,1)}, bf16[192,192]{1,0:T(8,128)(2,1)}) custom-call(s32[8]{0:T(128)} %broadcast_select_fusion.refs_0_, bf16[64,7296]{1,0:T(8,128)(2,1)} %all_gather.3.refs_1_), custom_call_target="tpu_custom_call" | custom-call | tf_op jit(solution)/shard_map/route/pallas_call | solution.py:136
  43.6 21.0 %all-to-all-start = ((bf16[8,24,7168]{2,1,0:T(8,128)(2,1)}), bf16[8,24,7168]{2,1,0:T(8,128)(2,1)S(1)}, u32[]{:S(2)}, u32[]{:S(2)}) async-start(bf16[8,24,7168]{2,1,0:T(8,128)(2,1)} %bitcast.9), calls=%async_computation | async-start | bytes 5505024 | tf_op jit(solution)/shard_map/all_to_all | solution.py:155
  64.6 0.0 collective-permute-start
  64.6 0.5 collective-permute-start.1
  65.1 0.0 collective-permute-start.2
  65.1 6.1 %collective-permute-done.gb_ref = bf16[1,7168,256]{2,1,0:T(8,128)(2,1)S(1)} collective-permute-done((bf16[1,7168,256]{2,1,0:T(8,128)(2,1)}, bf16[1,7168,256]{2,1,0:T(8,128)(2,1)S(1)}, u32[]{:S(2)}, u32[]{:S(2)}) %collective-permute-start) | collective-permute-done | bytes 3670048 | tf_op jit(solution)/shard_map/ppermute | solution.py:125
  71.2 0.0 copy-start.1
  71.2 1.9 copy-done.1
  73.1 3.5 %collective-permute-done.1.ub_ref = bf16[1,7168,256]{2,1,0:T(8,128)(2,1)} collective-permute-done((bf16[1,7168,256]{2,1,0:T(8,128)(2,1)}, bf16[1,7168,256]{2,1,0:T(8,128)(2,1)}, u32[]{:S(2)}, u32[]{:S(2)}) %collective-permute-start.1) | collective-permute-done | bytes 3670048 | tf_op jit(solution)/shard_map/ppermute | solution.py:125
  76.6 23.4 %all-to-all-done = bf16[8,24,7168]{2,1,0:T(8,128)(2,1)S(1)} async-done(((bf16[8,24,7168]{2,1,0:T(8,128)(2,1)}), bf16[8,24,7168]{2,1,0:T(8,128)(2,1)S(1)}, u32[]{:S(2)}, u32[]{:S(2)}) %all-to-all-start) | async-done | bytes 2752544 | tf_op jit(solution)/shard_map/all_to_all | solution.py:155
  99.9 0.0 copy-start
  99.9 1.6 copy-done
  101.6 9.9 %hidden.1.h_ref = bf16[192,512]{1,0:T(8,128)(2,1)} custom-call(bf16[192,7168]{1,0:T(8,128)(2,1)} %bitcast.7, bf16[1,7168,256]{2,1,0:T(8,128)(2,1)} %ga_ref.1, bf16[1,7168,256]{2,1,0:T(8,128)(2,1)} %copy-done.1, bf16[1,7168,256]{2,1,0:T(8,128)(2,1)} %ua_ref.1, bf16[1,7168,256]{2,1,0:T(8,128)(2,1)} %collective-permute-done.1.ub_ref), custom_call_target="tpu_custom_call" | custom-call | tf_op jit(solution)/shard_map/hidden/pallas_call | solution.py:163
  111.5 0.0 collective-permute-done.2.db_ref
  111.5 7.9 %down.1 = bf16[192,7168]{1,0:T(8,128)(2,1)} custom-call(bf16[192,512]{1,0:T(8,128)(2,1)} %hidden.1.h_ref, bf16[1,256,7168]{2,1,0:T(8,128)(2,1)} %da_ref.1, bf16[1,256,7168]{2,1,0:T(8,128)(2,1)} %collective-permute-done.2.db_ref), custom_call_target="tpu_custom_call" | custom-call | tf_op jit(solution)/shard_map/down/pallas_call | solution.py:175
  119.4 46.3 %all_to_all.15 = bf16[8,24,7168]{2,1,0:T(8,128)(2,1)} all-to-all(bf16[8,24,7168]{2,1,0:T(8,128)(2,1)} %bitcast.6), channel_id=1, replica_groups={{0,2,4,6,8,10,12,14},{16,18,20,22,24,26,28,30},{32,34,36,38,40,42,44,46..., dimensions={0} | all-to-all | bytes 5505024 | tf_op jit(solution)/shard_map/all_to_all | solution.py:155
  165.7 5.9 %mix.1 = bf16[64,7168]{1,0:T(8,128)(2,1)} custom-call(bf16[192,192]{1,0:T(8,128)(2,1)} %get-tuple-element.7.mix_ref, bf16[192,7168]{1,0:T(8,128)(2,1)} %bitcast.5), custom_call_target="tpu_custom_call" | custom-call | tf_op jit(solution)/shard_map/mix/pallas_call | solution.py:186
  171.6 21.0 %all_to_all.16 = bf16[8,8,7168]{2,1,0:T(8,128)(2,1)S(1)} all-to-all(bf16[8,8,7168]{2,1,0:T(8,128)(2,1)} %bitcast.8), channel_id=1, replica_groups={{0,16,32,48,64,80,96,112},{2,18,34,50,66,82,98,114},{4,20,36,52,68,84,1..., dimensions={0} | all-to-all | bytes 1835008 | tf_op jit(solution)/shard_map/all_to_all | solution.py:198
  192.6 0.8 reduce_sum.12
  (1 shorter events, 0.0 us)
Async XLA Ops:
  43.6 56.3 %all-to-all-start = ((bf16[8,24,7168]{2,1,0:T(8,128)(2,1)}), bf16[8,24,7168]{2,1,0:T(8,128)(2,1)S(1)}, u32[]{:S(2)}, u32[]{:S(2)}) async-start(bf16[8,24,7168]{2,1,0:T(8,128)(2,1)} %bitcast.9), calls=%async_computation | async-start | bytes 5505024 | tf_op jit(solution)/shard_map/all_to_all | solution.py:155
  64.6 6.6 %collective-permute-start = (bf16[1,7168,256]{2,1,0:T(8,128)(2,1)}, bf16[1,7168,256]{2,1,0:T(8,128)(2,1)S(1)}, u32[]{:S(2)}, u32[]{:S(2)}) collective-permute-start(bf16[1,7168,256]{2,1,0:T(8,128)(2,1)} %ga_ref.1), channel_id=1, source_target_pairs={{0,1},{1,0},{2,3},{3,2},{4,5},{5,4},{6,7},{7,6},{8,9},{9,8},{10,11... | collective-permute-start | bytes 11010056 | tf_op jit(solution)/shard_map/ppermute | solution.py:125
  64.6 12.0 %collective-permute-start.1 = (bf16[1,7168,256]{2,1,0:T(8,128)(2,1)}, bf16[1,7168,256]{2,1,0:T(8,128)(2,1)}, u32[]{:S(2)}, u32[]{:S(2)}) collective-permute-start(bf16[1,7168,256]{2,1,0:T(8,128)(2,1)} %ua_ref.1), channel_id=1, source_target_pairs={{0,1},{1,0},{2,3},{3,2},{4,5},{5,4},{6,7},{7,6},{8,9},{9,8},{10,11... | collective-permute-start | bytes 11010056 | tf_op jit(solution)/shard_map/ppermute | solution.py:125
  65.1 46.4 %collective-permute-start.2 = (bf16[1,256,7168]{2,1,0:T(8,128)(2,1)}, bf16[1,256,7168]{2,1,0:T(8,128)(2,1)}, u32[]{:S(2)}, u32[]{:S(2)}) collective-permute-start(bf16[1,256,7168]{2,1,0:T(8,128)(2,1)} %da_ref.1), channel_id=1, source_target_pairs={{0,1},{1,0},{2,3},{3,2},{4,5},{5,4},{6,7},{7,6},{8,9},{9,8},{10,11... | collective-permute-start | bytes 11010056 | tf_op jit(solution)/shard_map/ppermute | solution.py:125
  71.2 1.9 copy-start.1
  99.9 1.6 copy-start

commit v2 on v1

v2 whole, which is shorter than its diff:
```python
import functools
import math

import jax
import jax.numpy as jnp
from jax import lax
from jax.experimental import pallas as pl
from jax.experimental.pallas import tpu as pltpu
from jax.sharding import PartitionSpec as P


GROUP = ("expert", "sub")
LANES = 128
INFO = 2 * LANES
CAP = 3
STEPS = 4
MIB = 1 << 20


def crossing_groups(side):
    def at(y, x, c):
        return (y * side + x) * 2 + c

    r = range(side)
    along_y = [[[at(y, x, c) for y in r] for x in r] for c in (0, 1)]
    along_x = [[[at(y, x, c) for x in r] for y in r] for c in (0, 1)]
    return along_y[0] + along_x[1], along_x[0] + along_y[1]


def held_in(x, space):
    return pltpu.with_memory_space_constraint(x, space)


V = pltpu.VMEM
S = pltpu.SMEM
A = pltpu.HBM
PLAIN = None


def call(kernel, ins, outs, scratch=(), limit=16):
    got = pl.pallas_call(
        kernel,
        in_specs=[pl.BlockSpec(memory_space=V if space is PLAIN else space) for _, space in ins],
        out_shape=[
            V(shape, dtype) if space is V else jax.ShapeDtypeStruct(shape, dtype)
            for shape, dtype, space in outs
        ],
        out_specs=[pl.BlockSpec(memory_space=V) for _ in outs],
        scratch_shapes=list(scratch),
        compiler_params=pltpu.CompilerParams(vmem_limit_bytes=limit * MIB),
    )(*[x if space is S else held_in(x, A if space is PLAIN else space) for x, space in ins])
    return got[0] if len(outs) == 1 else got


def pack_kernel(tokens_ref, ids_ref, levels_ref, out):
    mine, width = tokens_ref.shape
    picks = ids_ref.shape[1]
    rest = jnp.zeros((mine, LANES - picks), jnp.float32)
    info = [
        jnp.concatenate([r[...].astype(jnp.float32), rest], axis=1).astype(jnp.bfloat16)
        for r in (ids_ref, levels_ref)
    ]
    for i in range(out.shape[0] // mine):
        here = slice(i * mine, (i + 1) * mine)
        out[here, :width] = tokens_ref[...]
        out[here, width : width + LANES] = info[0]
        out[here, width + LANES :] = info[1]


def selection(experts_ref, info, side, picks, toks):
    info = jnp.concatenate([info, jnp.zeros((LANES - toks, INFO), jnp.float32)], axis=0)
    ids = info[:, :LANES].T[:picks]
    levels = info[:, LANES:].T[:picks]
    total = jnp.sum(levels, axis=0, keepdims=True)
    total = jnp.where(total == 0.0, 1.0, total)
    named, share = [], []
    for i in range(side):
        hit = ids == experts_ref[i].astype(jnp.float32)
        named.append(jnp.sum(jnp.where(hit, 1.0, 0.0), axis=0, keepdims=True))
        share.append(jnp.sum(jnp.where(hit, levels, 0.0), axis=0, keepdims=True) / total)
    per = toks // side
    a = lax.broadcasted_iota(jnp.int32, (LANES, LANES), 0)
    b = lax.broadcasted_iota(jnp.int32, (LANES, LANES), 1)
    earlier = jnp.where((a // per == b // per) & (a < b), 1.0, 0.0).astype(jnp.bfloat16)
    slot = jnp.dot(
        jnp.concatenate(named, axis=0).astype(jnp.bfloat16),
        earlier,
        preferred_element_type=jnp.float32,
    )
    own = (
        lax.broadcasted_iota(jnp.int32, (side, LANES), 1) // per
        == lax.broadcasted_iota(jnp.int32, (side, LANES), 0)
    )
    pieces, mixes = [], []
    for i in range(side):
        for s in range(CAP):
            here = jnp.where(slot[i : i + 1] == float(s), named[i], 0.0)
            pieces.append(jnp.where(own, here, 0.0))
            mixes.append(jnp.where(own, here * share[i], 0.0))
    select = jnp.concatenate(pieces, axis=0)[:, :toks].astype(jnp.bfloat16)
    count = select.shape[0]
    mix = jnp.concatenate(mixes + [jnp.zeros((-count % LANES, LANES), jnp.float32)], axis=0).T
    mix = mix[:toks, :count]
    high = mix.astype(jnp.bfloat16)
    rest = mix - high.astype(jnp.float32)
    mid = rest.astype(jnp.bfloat16)
    low = (rest - mid.astype(jnp.float32)).astype(jnp.bfloat16)
    return select, (high, mid, low)


def blocks(size, step):
    return [slice(n, n + step) for n in range(0, size, step)]


def spread(select, rows_ref, out_ref):
    for cols in blocks(out_ref.shape[1], 4 * LANES):
        out_ref[:, cols] = jnp.dot(
            select, rows_ref[:, cols], preferred_element_type=jnp.float32
        ).astype(jnp.bfloat16)


def route_kernel(experts_ref, rows_ref, *refs, side, picks):
    out_ref, mix_ref = refs[-2:]
    size = out_ref.shape[1]
    toks = rows_ref.shape[0]
    info = rows_ref[:, size:].astype(jnp.float32)
    select, mix = selection(experts_ref, info, side, picks, toks)
    for n, m in enumerate(mix):
        mix_ref[n * toks : (n + 1) * toks] = m
    spread(select, rows_ref, out_ref)


def expert_kernel(x_ref, *refs):
    weights, out_ref = refs[:6], refs[6]
    held, acc_ref, h_ref, sems = refs[7:13], refs[13], refs[14], refs[15]
    part = held[0].shape[1]
    width = x_ref.shape[1]
    pieces = blocks(width, width // STEPS)
    copies = []
    for k, rows in enumerate(pieces):
        copies.append([
            pltpu.make_async_copy(weights[n].at[0, rows], held[n].at[rows], sems.at[n, k])
            for n in range(4)
        ])
    for k, cols in enumerate(pieces):
        copies.append([
            pltpu.make_async_copy(weights[n].at[0, :, cols], held[n].at[:, cols], sems.at[n, k])
            for n in (4, 5)
        ])
    for group in copies:
        for copy in group:
            copy.start()
    for k, rows in enumerate(pieces):
        for copy in copies[k]:
            copy.wait()
        for n in range(4):
            cols = slice(n * part, (n + 1) * part)
            got = jnp.dot(x_ref[:, rows], held[n][rows], preferred_element_type=jnp.float32)
            acc_ref[:, cols] = acc_ref[:, cols] + got if k else got
    gate = acc_ref[:, : 2 * part]
    up = acc_ref[:, 2 * part :]
    h_ref[...] = (gate / (1.0 + jnp.exp(-gate)) * up).astype(jnp.bfloat16)
    for k, cols in enumerate(pieces):
        for copy in copies[STEPS + k]:
            copy.wait()
        out_ref[:, cols] = (
            jnp.dot(h_ref[:, :part], held[4][:, cols], preferred_element_type=jnp.float32)
            + jnp.dot(h_ref[:, part:], held[5][:, cols], preferred_element_type=jnp.float32)
        ).astype(jnp.bfloat16)


def mix_kernel(mix_ref, rows_ref, out_ref):
    toks = out_ref.shape[0]
    for cols in blocks(out_ref.shape[1], 4 * LANES):
        y = jnp.dot(mix_ref[...], rows_ref[:, cols], preferred_element_type=jnp.float32)
        out_ref[:, cols] = (y[:toks] + y[toks : 2 * toks] + y[2 * toks :]).astype(jnp.bfloat16)


def sum_kernel(rows_ref, out_ref):
    mine = out_ref.shape[0]
    total = rows_ref[:mine].astype(jnp.float32)
    for i in range(1, rows_ref.shape[0] // mine):
        total = total + rows_ref[i * mine : (i + 1) * mine].astype(jnp.float32)
    out_ref[...] = total.astype(jnp.bfloat16)


def local(tokens, expert_ids, route_levels, gate_proj, up_proj, down_proj):
    mine, width = tokens.shape
    picks = expert_ids.shape[1]
    side = math.isqrt(lax.axis_size("expert"))
    first, second = crossing_groups(side)
    core = lax.axis_index("sub")
    chip = lax.axis_index("expert")
    y, x = chip // side, chip % side
    i = jnp.arange(side, dtype=jnp.int32)
    experts = jnp.where(core == 0, (y * side + i) // 2, (i * side + x) // 2)
    toks = side * mine
    slots = toks * CAP
    part = gate_proj.shape[2]
    bf16, f32 = jnp.bfloat16, jnp.float32

    def crossed(block, groups):
        rows, cols = block.shape
        block = block.reshape(side, rows // side, cols)
        block = lax.all_to_all(block, GROUP, 0, 0, tiled=True, axis_index_groups=groups)
        return block.reshape(rows, cols)

    gate_peer, up_peer, down_peer = (
        lax.ppermute(w, "sub", [(0, 1), (1, 0)]) for w in (gate_proj, up_proj, down_proj)
    )

    rows = call(
        pack_kernel,
        [(tokens, PLAIN), (expert_ids, PLAIN), (route_levels, PLAIN)],
        [((toks, width + INFO), bf16, PLAIN)],
    )
    rows = crossed(rows, first)
    rows, mix = call(
        functools.partial(route_kernel, side=side, picks=picks),
        [(experts, S), (rows, V)] + [(w, A) for w in (gate_peer, up_peer, down_peer)],
        [((slots, width), bf16, V), ((3 * toks, slots), bf16, PLAIN)],
    )
    rows = crossed(rows, second)
    rows = call(
        expert_kernel,
        [(rows, V)]
        + [(w, A) for w in (gate_proj, gate_peer, up_proj, up_peer, down_proj, down_peer)],
        [((slots, width), bf16, V)],
        [V((width, part), bf16)] * 4
        + [V((part, width), bf16)] * 2
        + [V((slots, 4 * part), f32), V((slots, 2 * part), bf16)]
        + [pltpu.SemaphoreType.DMA((6, STEPS))],
        limit=36,
    )
    rows = crossed(rows, second)
    rows = call(mix_kernel, [(mix, PLAIN), (rows, V)], [((toks, width), bf16, V)])
    rows = crossed(rows, first)
    return call(sum_kernel, [(rows, V)], [((mine, width), bf16, PLAIN)])


def solution(mesh):
    return jax.shard_map(
        local,
        mesh=mesh,
        in_specs=(
            P(("replica", "expert", "sub"), None),
            P(("replica", "expert", "sub"), None),
            P(("replica", "expert", "sub"), None),
            P("expert", None, "sub"),
            P("expert", None, "sub"),
            P("expert", "sub", None),
        ),
        out_specs=P(("replica", "expert", "sub"), None),
        check_vma=False,
    )
```

time: 194 us -> 154 us (0.79)
  waiting for transfers between devices: 32.9 us -> 17.9 us
  Pallas kernels: 27.6 us -> 14.7 us
  starting transfers between devices: 21.5 us -> 13.7 us
  local copies, waits for them, and re-layouts: 4.55 us -> 0.01 us
  blocking collectives: 104 us -> 108 us
  other arithmetic: 2.76 us -> 0.01 us
    all_to_all x2 -> x3, blocking collectives: 67.3 us -> 108 us  [crossed(): lax.all_to_all(block, GROUP, 0, 0, tiled=True, axis_index_groups=groups)]
    all_gather x1 -> x0, blocking collectives: 36.7 us -> none  [local(): lax.all_gather(rows, GROUP, axis=0, tiled=True, axis_index_groups=first)]
    pallas_call x4 -> x5, Pallas kernels: 27.6 us -> 14.7 us  [call(): pl.pallas_call(kernel, in_specs=[pl.BlockSpec(memory_space=V if space is...]
    ppermute x3, waiting for transfers between devices: 9.58 us -> 0.01 us  [local(): lax.ppermute(w, 'sub', [(0, 1), (1, 0)])]
    all_to_all x1, starting transfers between devices: 21 us -> 13.2 us  [crossed(): lax.all_to_all(block, GROUP, 0, 0, tiled=True, axis_index_groups=groups)]
    all_to_all x1, waiting for transfers between devices: 23.4 us -> 17.9 us  [crossed(): lax.all_to_all(block, GROUP, 0, 0, tiled=True, axis_index_groups=groups)]
    unnamed x4 -> x2, local copies, waits for them, and re-layouts: 3.56 us -> 0.01 us
  transfers between devices with their start and end apart: 4 -> 4, of which waited for: 3 -> 1; matrix products, arithmetic and copies ran while one was open for 0% -> 0% of each run, Pallas kernels for 5% -> 1%
where the time goes in v2:
time: 154 us
  blocking collectives  108 us (70%)
  waiting for transfers between devices  17.9 us (12%)
  Pallas kernels  14.7 us (10%)
  starting transfers between devices  13.7 us (9%)
    all_to_all x3, blocking collectives, crossed(): lax.all_to_all(block, GROUP, 0, 0, tiled=True, axis_index_groups=groups)  108 us
    all_to_all x1, waiting for transfers between devices, crossed(): lax.all_to_all(block, GROUP, 0, 0, tiled=True, axis_index_groups=groups)  17.9 us
    pallas_call x5, Pallas kernels, call(): pl.pallas_call(kernel, in_specs=[pl.BlockSpec(memory_space=V if space is...  14.7 us
    all_to_all x1, starting transfers between devices, crossed(): lax.all_to_all(block, GROUP, 0, 0, tiled=True, axis_index_groups=groups)  13.2 us
  transfers between devices with their start and end apart: 4, of which 1 were waited for; matrix products, arithmetic and copies ran while one was open for 0% of the time, Pallas kernels for 1%

profile of v2, /device:TPU:514, one launch (start us, length us, event | category | flops | bytes accessed | tf_op | source)
XLA Modules:
  0.0 153.8 jit_solution(15302285968663401235)
XLA Ops:
  0.0 0.0 collective-permute-start
  0.0 0.5 collective-permute-start.1
  0.5 0.0 collective-permute-start.2
  0.5 1.9 %shard_map.64 = bf16[64,7424]{1,0:T(8,128)(2,1)} custom-call(bf16[8,7168]{1,0:T(8,128)(2,1)} %tokens_ref.1, s32[8,8]{1,0:T(8,128)} %ids_ref.1, s32[8,8]{1,0:T(8,128)} %levels_ref.1), custom_call_target="tpu_custom_call" | custom-call | tf_op jit(solution)/shard_map/pallas_call | solution.py:41
  2.4 13.2 %all-to-all-start = ((bf16[8,8,7424]{2,1,0:T(8,128)(2,1)}), bf16[8,8,7424]{2,1,0:T(8,128)(2,1)S(1)}, u32[]{:S(2)}, u32[]{:S(2)}) async-start(bf16[8,8,7424]{2,1,0:T(8,128)(2,1)} %bitcast), calls=%async_computation | async-start | bytes 1900544 | tf_op jit(solution)/shard_map/all_to_all | solution.py:205
  15.6 17.9 %all-to-all-done = bf16[8,8,7424]{2,1,0:T(8,128)(2,1)S(1)} async-done(((bf16[8,8,7424]{2,1,0:T(8,128)(2,1)}), bf16[8,8,7424]{2,1,0:T(8,128)(2,1)S(1)}, u32[]{:S(2)}, u32[]{:S(2)}) %all-to-all-start) | async-done | bytes 950304 | tf_op jit(solution)/shard_map/all_to_all | solution.py:205
  33.5 0.0 collective-permute-done.refs_0_.refs_1_
  33.5 0.0 collective-permute-done.1.refs_1_.refs_3_
  33.5 0.0 collective-permute-done.2.refs_2_.refs_5_
  33.5 1.6 %shard_map.65 = (bf16[192,7168]{1,0:T(8,128)(2,1)S(1)}, bf16[192,192]{1,0:T(8,128)(2,1)S(1)}) custom-call(s32[8]{0:T(128)S(1)} %broadcast_select_fusion.experts_ref, bf16[64,7424]{1,0:T(8,128)(2,1)S(1)} %bitcast.11, bf16[1,7168,256]{2,1,0:T(8,128)(2,1)} %collective-permute-done.refs_0_.refs_1_, bf16[1,7168,256]{2,1,0:T(8,128)(2,1)} %collective-permute-done.1.refs_1_.refs_3_, ...), custom_call_target="tpu_custom_call" | custom-call | tf_op jit(solution)/shard_map/pallas_call | solution.py:41
  35.1 0.0 copy-start
  35.1 48.0 %all_to_all.20 = bf16[8,24,7168]{2,1,0:T(8,128)(2,1)S(1)} all-to-all(bf16[8,24,7168]{2,1,0:T(8,128)(2,1)S(1)} %bitcast.14), channel_id=1, replica_groups={{0,2,4,6,8,10,12,14},{16,18,20,22,24,26,28,30},{32,34,36,38,40,42,44,46..., dimensions={0} | all-to-all | bytes 5505024 | tf_op jit(solution)/shard_map/all_to_all | solution.py:205
  83.1 0.0 copy-done
  83.1 8.6 %shard_map.66 = bf16[192,7168]{1,0:T(8,128)(2,1)S(1)} custom-call(bf16[192,7168]{1,0:T(8,128)(2,1)S(1)} %bitcast.9, bf16[1,7168,256]{2,1,0:T(8,128)(2,1)} %refs_0_.1, bf16[1,7168,256]{2,1,0:T(8,128)(2,1)} %collective-permute-done.refs_0_.refs_1_, bf16[1,7168,256]{2,1,0:T(8,128)(2,1)} %refs_2_.1, ...), custom_call_target="tpu_custom_call" | custom-call | tf_op jit(solution)/shard_map/pallas_call | solution.py:41
  91.7 39.6 %all_to_all.21 = bf16[8,24,7168]{2,1,0:T(8,128)(2,1)S(1)} all-to-all(bf16[8,24,7168]{2,1,0:T(8,128)(2,1)S(1)} %bitcast.10), channel_id=1, replica_groups={{0,2,4,6,8,10,12,14},{16,18,20,22,24,26,28,30},{32,34,36,38,40,42,44,46..., dimensions={0} | all-to-all | bytes 5505024 | tf_op jit(solution)/shard_map/all_to_all | solution.py:205
  131.4 1.8 %shard_map.67 = bf16[64,7168]{1,0:T(8,128)(2,1)S(1)} custom-call(bf16[192,192]{1,0:T(8,128)(2,1)} %copy-done, bf16[192,7168]{1,0:T(8,128)(2,1)S(1)} %bitcast.8), custom_call_target="tpu_custom_call" | custom-call | tf_op jit(solution)/shard_map/pallas_call | solution.py:41
  133.1 19.9 %all_to_all.22 = bf16[8,8,7168]{2,1,0:T(8,128)(2,1)S(1)} all-to-all(bf16[8,8,7168]{2,1,0:T(8,128)(2,1)S(1)} %bitcast.12), channel_id=1, replica_groups={{0,16,32,48,64,80,96,112},{2,18,34,50,66,82,98,114},{4,20,36,52,68,84,1..., dimensions={0} | all-to-all | bytes 1835008 | tf_op jit(solution)/shard_map/all_to_all | solution.py:205
  153.1 0.8 shard_map.68
  (1 shorter events, 0.0 us)
Async XLA Ops:
  0.0 33.5 %collective-permute-start = (bf16[1,7168,256]{2,1,0:T(8,128)(2,1)}, bf16[1,7168,256]{2,1,0:T(8,128)(2,1)}, u32[]{:S(2)}, u32[]{:S(2)}) collective-permute-start(bf16[1,7168,256]{2,1,0:T(8,128)(2,1)} %refs_0_.1), channel_id=1, source_target_pairs={{0,1},{1,0},{2,3},{3,2},{4,5},{5,4},{6,7},{7,6},{8,9},{9,8},{10,11... | collective-permute-start | bytes 11010056 | tf_op jit(solution)/shard_map/ppermute | solution.py:209
  0.0 33.5 %collective-permute-start.1 = (bf16[1,7168,256]{2,1,0:T(8,128)(2,1)}, bf16[1,7168,256]{2,1,0:T(8,128)(2,1)}, u32[]{:S(2)}, u32[]{:S(2)}) collective-permute-start(bf16[1,7168,256]{2,1,0:T(8,128)(2,1)} %refs_2_.1), channel_id=1, source_target_pairs={{0,1},{1,0},{2,3},{3,2},{4,5},{5,4},{6,7},{7,6},{8,9},{9,8},{10,11... | collective-permute-start | bytes 11010056 | tf_op jit(solution)/shard_map/ppermute | solution.py:209
  0.5 33.0 %collective-permute-start.2 = (bf16[1,256,7168]{2,1,0:T(8,128)(2,1)}, bf16[1,256,7168]{2,1,0:T(8,128)(2,1)}, u32[]{:S(2)}, u32[]{:S(2)}) collective-permute-start(bf16[1,256,7168]{2,1,0:T(8,128)(2,1)} %refs_4_.1), channel_id=1, source_target_pairs={{0,1},{1,0},{2,3},{3,2},{4,5},{5,4},{6,7},{7,6},{8,9},{9,8},{10,11... | collective-permute-start | bytes 11010056 | tf_op jit(solution)/shard_map/ppermute | solution.py:209
  2.4 31.1 %all-to-all-start = ((bf16[8,8,7424]{2,1,0:T(8,128)(2,1)}), bf16[8,8,7424]{2,1,0:T(8,128)(2,1)S(1)}, u32[]{:S(2)}, u32[]{:S(2)}) async-start(bf16[8,8,7424]{2,1,0:T(8,128)(2,1)} %bitcast), calls=%async_computation | async-start | bytes 1900544 | tf_op jit(solution)/shard_map/all_to_all | solution.py:205
  35.1 48.0 %copy-start = (bf16[192,192]{1,0:T(8,128)(2,1)}, bf16[192,192]{1,0:T(8,128)(2,1)S(1)}, u32[]{:S(2)}) copy-start(bf16[192,192]{1,0:T(8,128)(2,1)S(1)} %get-tuple-element.7.mix_ref) | copy-start | bytes 221188

commit v3 on v2

--- a/solution.py
+++ b/solution.py
@@ -17,14 +17,32 @@
 MIB = 1 << 20
 
 
-def crossing_groups(side):
-    def at(y, x, c):
-        return (y * side + x) * 2 + c
-
+def device(side, y, x, c):
+    return (y * side + x) * 2 + c
+
+
+def first_groups(side):
     r = range(side)
-    along_y = [[[at(y, x, c) for y in r] for x in r] for c in (0, 1)]
-    along_x = [[[at(y, x, c) for x in r] for y in r] for c in (0, 1)]
-    return along_y[0] + along_x[1], along_x[0] + along_y[1]
+    down = [[device(side, y, x, 0) for y in r] for x in r]
+    over = [[device(side, y, x, 1) for x in r] for y in r]
+    return down + over
+
+
+def second_route(side, k):
+    pairs = []
+    for y in range(side):
+        for x in range(side):
+            over, down = (x + k) % side, (y + k) % side
+            pairs.append((device(side, y, x, 0), device(side, y, over, 0)))
+            pairs.append((device(side, y, x, 1), device(side, down, x, 1)))
+    return pairs
+
+
+def near_first(side):
+    order = [0]
+    for k in range(1, side // 2):
+        order += [k, side - k]
+    return order + [side // 2]
 
 
 def held_in(x, space):
@@ -112,27 +130,34 @@
     return [slice(n, n + step) for n in range(0, size, step)]
 
 
-def spread(select, rows_ref, out_ref):
-    for cols in blocks(out_ref.shape[1], 4 * LANES):
-        out_ref[:, cols] = jnp.dot(
-            select, rows_ref[:, cols], preferred_element_type=jnp.float32
-        ).astype(jnp.bfloat16)
+def put(outs, cols, got):
+    each = outs[0].shape[0]
+    for k, out in enumerate(outs):
+        out[:, cols] = got[k * each : (k + 1) * each].astype(jnp.bfloat16)
+
+
+def gathered(ref, rows):
+    each = rows[0].shape[0]
+    for k, r in enumerate(rows):
+        ref[k * each : (k + 1) * each] = r[...]
 
 
 def route_kernel(experts_ref, rows_ref, *refs, side, picks):
-    out_ref, mix_ref = refs[-2:]
-    size = out_ref.shape[1]
+    outs, mix_ref = refs[-side - 1 : -1], refs[-1]
+    width = outs[0].shape[1]
     toks = rows_ref.shape[0]
-    info = rows_ref[:, size:].astype(jnp.float32)
+    info = rows_ref[:, width:].astype(jnp.float32)
     select, mix = selection(experts_ref, info, side, picks, toks)
     for n, m in enumerate(mix):
         mix_ref[n * toks : (n + 1) * toks] = m
-    spread(select, rows_ref, out_ref)
-
-
-def expert_kernel(x_ref, *refs):
-    weights, out_ref = refs[:6], refs[6]
-    held, acc_ref, h_ref, sems = refs[7:13], refs[13], refs[14], refs[15]
+    for cols in blocks(width, 4 * LANES):
+        put(outs, cols, jnp.dot(select, rows_ref[:, cols], preferred_element_type=jnp.float32))
+
+
+def expert_kernel(*refs, side):
+    arrived, weights, outs = refs[:side], refs[side : side + 6], refs[side + 6 : 2 * side + 6]
+    refs = refs[2 * side + 6 :]
+    held, acc_ref, h_ref, x_ref, sems = refs[:6], refs[6], refs[7], refs[8], refs[9]
     part = held[0].shape[1]
     width = x_ref.shape[1]
     pieces = blocks(width, width // STEPS)
@@ -150,6 +175,7 @@
     for group in copies:
         for copy in group:
             copy.start()
+    gathered(x_ref, arrived)
     for k, rows in enumerate(pieces):
         for copy in copies[k]:
             copy.wait()
@@ -163,14 +189,18 @@
     for k, cols in enumerate(pieces):
         for copy in copies[STEPS + k]:
             copy.wait()
-        out_ref[:, cols] = (
+        put(
+            outs,
+            cols,
             jnp.dot(h_ref[:, :part], held[4][:, cols], preferred_element_type=jnp.float32)
-            + jnp.dot(h_ref[:, part:], held[5][:, cols], preferred_element_type=jnp.float32)
-        ).astype(jnp.bfloat16)
-
-
-def mix_kernel(mix_ref, rows_ref, out_ref):
+            + jnp.dot(h_ref[:, part:], held[5][:, cols], preferred_element_type=jnp.float32),
+        )
+
+
+def mix_kernel(mix_ref, *refs):
+    rows, out_ref, rows_ref = refs[:-2], refs[-2], refs[-1]
     toks = out_ref.shape[0]
+    gathered(rows_ref, rows)
     for cols in blocks(out_ref.shape[1], 4 * LANES):
         y = jnp.dot(mix_ref[...], rows_ref[:, cols], preferred_element_type=jnp.float32)
         out_ref[:, cols] = (y[:toks] + y[toks : 2 * toks] + y[2 * toks :]).astype(jnp.bfloat16)
@@ -188,22 +218,32 @@
     mine, width = tokens.shape
     picks = expert_ids.shape[1]
     side = math.isqrt(lax.axis_size("expert"))
-    first, second = crossing_groups(side)
+    order = near_first(side)
     core = lax.axis_index("sub")
     chip = lax.axis_index("expert")
     y, x = chip // side, chip % side
-    i = jnp.arange(side, dtype=jnp.int32)
-    experts = jnp.where(core == 0, (y * side + i) // 2, (i * side + x) // 2)
+    k = jnp.array(order, dtype=jnp.int32)
+    experts = jnp.where(
+        core == 0, (y * side + (x + k) % side) // 2, ((y + k) % side * side + x) // 2
+    )
     toks = side * mine
     slots = toks * CAP
     part = gate_proj.shape[2]
     bf16, f32 = jnp.bfloat16, jnp.float32
 
-    def crossed(block, groups):
+    each = slots // side
+
+    def first_crossed(block):
         rows, cols = block.shape
         block = block.reshape(side, rows // side, cols)
-        block = lax.all_to_all(block, GROUP, 0, 0, tiled=True, axis_index_groups=groups)
+        block = lax.all_to_all(block, GROUP, 0, 0, tiled=True, axis_index_groups=first_groups(side))
         return block.reshape(rows, cols)
+
+    def second_crossed(rows, sign):
+        moved = [rows[0]]
+        for n in range(1, side):
+            moved.append(lax.ppermute(rows[n], GROUP, second_route(side, sign * order[n])))
+        return moved
 
     gate_peer, up_peer, down_peer = (
         lax.ppermute(w, "sub", [(0, 1), (1, 0)]) for w in (gate_proj, up_proj, down_proj)
@@ -214,27 +254,32 @@
         [(tokens, PLAIN), (expert_ids, PLAIN), (route_levels, PLAIN)],
         [((toks, width + INFO), bf16, PLAIN)],
     )
-    rows = crossed(rows, first)
-    rows, mix = call(
+    rows = first_crossed(rows)
+    *rows, mix = call(
         functools.partial(route_kernel, side=side, picks=picks),
         [(experts, S), (rows, V)] + [(w, A) for w in (gate_peer, up_peer, down_peer)],
-        [((slots, width), bf16, V), ((3 * toks, slots), bf16, PLAIN)],
-    )
-    rows = crossed(rows, second)
+        [((each, width), bf16, V)] * side + [((3 * toks, slots), bf16, V)],
+    )
+    rows = second_crossed(rows, 1)
     rows = call(
-        expert_kernel,
-        [(rows, V)]
+        functools.partial(expert_kernel, side=side),
+        [(r, V) for r in rows]
         + [(w, A) for w in (gate_proj, gate_peer, up_proj, up_peer, down_proj, down_peer)],
-        [((slots, width), bf16, V)],
+        [((each, width), bf16, V)] * side,
         [V((width, part), bf16)] * 4
         + [V((part, width), bf16)] * 2
-        + [V((slots, 4 * part), f32), V((slots, 2 * part), bf16)]
+        + [V((slots, 4 * part), f32), V((slots, 2 * part), bf16), V((slots, width), bf16)]
         + [pltpu.SemaphoreType.DMA((6, STEPS))],
         limit=36,
     )
-    rows = crossed(rows, second)
-    rows = call(mix_kernel, [(mix, PLAIN), (rows, V)], [((toks, width), bf16, V)])
-    rows = crossed(rows, first)
+    rows = second_crossed(rows, -1)
+    rows = call(
+        mix_kernel,
+        [(mix, V)] + [(r, V) for r in rows],
+        [((toks, width), bf16, V)],
+        [V((slots, width), bf16)],
+    )
+    rows = first_crossed(rows)
     return call(sum_kernel, [(rows, V)], [((mine, width), bf16, PLAIN)])
 
 

time: 154 us -> 147 us (0.955)
  the two profiles are of different devices: /device:TPU:514 before, /device:TPU:516 now
where the time goes in v3:
time: 147 us
  waiting for transfers between devices  61.5 us (42%)
  starting transfers between devices  48.9 us (33%)
  blocking collectives  21.8 us (15%)
  Pallas kernels  13.8 us (9%)
    ppermute x14, waiting for transfers between devices, second_crossed(): lax.ppermute(rows[n], GROUP, second_route(side, sign * order[n]))  44.2 us
    ppermute x14, starting transfers between devices, second_crossed(): lax.ppermute(rows[n], GROUP, second_route(side, sign * order[n]))  35.3 us
    all_to_all x1, blocking collectives, first_crossed(): lax.all_to_all(block, GROUP, 0, 0, tiled=True, axis_index_groups=first_gr...  21.8 us
    all_to_all x1, waiting for transfers between devices, first_crossed(): lax.all_to_all(block, GROUP, 0, 0, tiled=True, axis_index_groups=first_gr...  17.2 us
    pallas_call x5, Pallas kernels, call(): pl.pallas_call(kernel, in_specs=[pl.BlockSpec(memory_space=V if space is...  13.8 us
    all_to_all x1, starting transfers between devices, first_crossed(): lax.all_to_all(block, GROUP, 0, 0, tiled=True, axis_index_groups=first_gr...  13.2 us
  transfers between devices with their start and end apart: 18, of which 7 were waited for; matrix products, arithmetic and copies ran while one was open for 0% of the time, Pallas kernels for 1%

profile of v3, /device:TPU:516, one launch (start us, length us, event | category | flops | bytes accessed | tf_op | source)
XLA Modules:
  0.0 146.7 jit_solution(16695847619823311928)
XLA Ops:
  0.0 0.0 collective-permute-start
  0.0 0.5 collective-permute-start.1
  0.5 0.0 collective-permute-start.2
  0.5 1.9 %shard_map.73 = bf16[64,7424]{1,0:T(8,128)(2,1)} custom-call(bf16[8,7168]{1,0:T(8,128)(2,1)} %tokens_ref.1, s32[8,8]{1,0:T(8,128)} %ids_ref.1, s32[8,8]{1,0:T(8,128)} %levels_ref.1), custom_call_target="tpu_custom_call" | custom-call | tf_op jit(solution)/shard_map/pallas_call | solution.py:59
  2.4 13.2 %all-to-all-start = ((bf16[8,8,7424]{2,1,0:T(8,128)(2,1)}), bf16[8,8,7424]{2,1,0:T(8,128)(2,1)S(1)}, u32[]{:S(2)}, u32[]{:S(2)}) async-start(bf16[8,8,7424]{2,1,0:T(8,128)(2,1)} %bitcast), calls=%async_computation | async-start | bytes 1900544 | tf_op jit(solution)/shard_map/all_to_all | solution.py:239
  15.6 0.7 broadcast_select_fusion.experts_ref
  16.3 17.2 %all-to-all-done = bf16[8,8,7424]{2,1,0:T(8,128)(2,1)S(1)} async-done(((bf16[8,8,7424]{2,1,0:T(8,128)(2,1)}), bf16[8,8,7424]{2,1,0:T(8,128)(2,1)S(1)}, u32[]{:S(2)}, u32[]{:S(2)}) %all-to-all-start) | async-done | bytes 950304 | tf_op jit(solution)/shard_map/all_to_all | solution.py:239
  33.5 0.0 collective-permute-done.refs_0_.refs_9_
  33.5 0.0 collective-permute-done.1.refs_1_.refs_11_
  33.5 0.0 collective-permute-done.2.refs_2_.refs_13_
  33.5 1.6 %shard_map.74 = (bf16[24,7168]{1,0:T(8,128)(2,1)S(1)}, bf16[24,7168]{1,0:T(8,128)(2,1)S(1)}, bf16[24,7168]{1,0:T(8,128)(2,1)S(1)}, bf16[24,7168]{1,0:T(8,128)(2,...) custom-call(s32[8]{0:T(128)S(1)} %broadcast_select_fusion.experts_re, ...), custom_call_target="tpu_custom_call" | custom-call | tf_op jit(solution)/shard_map/pallas_call | solution.py:59
  35.1 1.7 %collective-permute-start.3 = (bf16[24,7168]{1,0:T(8,128)(2,1)S(1)}, bf16[24,7168]{1,0:T(8,128)(2,1)S(1)}, u32[]{:S(2)}, u32[]{:S(2)}) collective-permute-start(bf16[24,7168]{1,0:T(8,128)(2,1)S(1)} %get-tuple-element.24), channel_id=1, source_target_pairs={{0,2},{1,17},{2,4},{3,19},{4,6},{5,21},{6,8},{7,23},{8,10},{9,25},... | collective-permute-start | bytes 1032200 | tf_op jit(solution)/shard_map/ppermute | solution.py:245
  36.8 0.4 collective-permute-start.4
  37.2 5.1 %collective-permute-start.5 = (bf16[24,7168]{1,0:T(8,128)(2,1)S(1)}, bf16[24,7168]{1,0:T(8,128)(2,1)S(1)}, u32[]{:S(2)}, u32[]{:S(2)}) collective-permute-start(bf16[24,7168]{1,0:T(8,128)(2,1)S(1)} %get-tuple-element.26), channel_id=1, source_target_pairs={{0,4},{1,33},{2,6},{3,35},{4,8},{5,37},{6,10},{7,39},{8,12},{9,41}... | collective-permute-start | bytes 1032200 | tf_op jit(solution)/shard_map/ppermute | solution.py:245
  42.3 4.4 %collective-permute-start.6 = (bf16[24,7168]{1,0:T(8,128)(2,1)S(1)}, bf16[24,7168]{1,0:T(8,128)(2,1)S(1)}, u32[]{:S(2)}, u32[]{:S(2)}) collective-permute-start(bf16[24,7168]{1,0:T(8,128)(2,1)S(1)} %get-tuple-element.27), channel_id=1, source_target_pairs={{0,12},{1,97},{2,14},{3,99},{4,0},{5,101},{6,2},{7,103},{8,4},{9,1... | collective-permute-start | bytes 1032200 | tf_op jit(solution)/shard_map/ppermute | solution.py:245
  46.8 0.9 collective-permute-start.7
  47.7 0.0 collective-permute-done.3.refs_1_
  47.7 4.1 %collective-permute-start.8 = (bf16[24,7168]{1,0:T(8,128)(2,1)S(1)}, bf16[24,7168]{1,0:T(8,128)(2,1)S(1)}, u32[]{:S(2)}, u32[]{:S(2)}) collective-permute-start(bf16[24,7168]{1,0:T(8,128)(2,1)S(1)} %get-tuple-element.29), channel_id=1, source_target_pairs={{0,10},{1,81},{2,12},{3,83},{4,14},{5,85},{6,0},{7,87},{8,2},{9,89... | collective-permute-start | bytes 1032200 | tf_op jit(solution)/shard_map/ppermute | solution.py:245
  51.8 0.0 collective-permute-done.4.refs_2_
  51.8 3.6 %collective-permute-start.9 = (bf16[24,7168]{1,0:T(8,128)(2,1)S(1)}, bf16[24,7168]{1,0:T(8,128)(2,1)S(1)}, u32[]{:S(2)}, u32[]{:S(2)}) collective-permute-start(bf16[24,7168]{1,0:T(8,128)(2,1)S(1)} %get-tuple-element.30), channel_id=1, source_target_pairs={{0,8},{1,65},{2,10},{3,67},{4,12},{5,69},{6,14},{7,71},{8,0},{9,73... | collective-permute-start | bytes 1032200 | tf_op jit(solution)/shard_map/ppermute | solution.py:245
  55.4 4.1 %collective-permute-done.5.refs_3_ = bf16[24,7168]{1,0:T(8,128)(2,1)S(1)} collective-permute-done((bf16[24,7168]{1,0:T(8,128)(2,1)S(1)}, bf16[24,7168]{1,0:T(8,128)(2,1)S(1)}, u32[]{:S(2)}, u32[]{:S(2)}) %collective-permute-start.5) | collective-permute-done | bytes 344096 | tf_op jit(solution)/shard_map/ppermute | solution.py:245
  59.5 0.0 collective-permute-done.6.refs_4_
  59.5 17.7 %collective-permute-done.7.refs_5_ = bf16[24,7168]{1,0:T(8,128)(2,1)S(1)} collective-permute-done((bf16[24,7168]{1,0:T(8,128)(2,1)S(1)}, bf16[24,7168]{1,0:T(8,128)(2,1)S(1)}, u32[]{:S(2)}, u32[]{:S(2)}) %collective-permute-start.7) | collective-permute-done | bytes 344096 | tf_op jit(solution)/shard_map/ppermute | solution.py:245
  77.3 0.0 collective-permute-done.8.refs_6_
  77.3 0.0 collective-permute-done.9.refs_7_
  77.3 8.6 %shard_map.75 = (bf16[24,7168]{1,0:T(8,128)(2,1)S(1)}, bf16[24,7168]{1,0:T(8,128)(2,1)S(1)}, bf16[24,7168]{1,0:T(8,128)(2,1)S(1)}, bf16[24,7168]{1,0:T(8,128)(2,...) custom-call(bf16[24,7168]{1,0:T(8,128)(2,1)S(1)} %get-tuple-element., ...), custom_call_target="tpu_custom_call" | custom-call | tf_op jit(solution)/shard_map/pallas_call | solution.py:59
  85.9 1.9 %collective-permute-start.10 = (bf16[24,7168]{1,0:T(8,128)(2,1)S(1)}, bf16[24,7168]{1,0:T(8,128)(2,1)S(1)}, u32[]{:S(2)}, u32[]{:S(2)}) collective-permute-start(bf16[24,7168]{1,0:T(8,128)(2,1)S(1)} %get-tuple-element.32), channel_id=1, source_target_pairs={{0,14},{1,113},{2,0},{3,115},{4,2},{5,117},{6,4},{7,119},{8,6},{9,... | collective-permute-start | bytes 1032200 | tf_op jit(solution)/shard_map/ppermute | solution.py:245
  87.8 0.2 collective-permute-start.11
  88.0 1.4 collective-permute-start.12
  89.4 2.7 %collective-permute-start.13 = (bf16[24,7168]{1,0:T(8,128)(2,1)S(1)}, bf16[24,7168]{1,0:T(8,128)(2,1)S(1)}, u32[]{:S(2)}, u32[]{:S(2)}) collective-permute-start(bf16[24,7168]{1,0:T(8,128)(2,1)S(1)} %get-tuple-element.35), channel_id=1, source_target_pairs={{0,4},{1,33},{2,6},{3,35},{4,8},{5,37},{6,10},{7,39},{8,12},{9,41}... | collective-permute-start | bytes 1032200 | tf_op jit(solution)/shard_map/ppermute | solution.py:245
  92.2 1.5 %collective-permute-start.14 = (bf16[24,7168]{1,0:T(8,128)(2,1)S(1)}, bf16[24,7168]{1,0:T(8,128)(2,1)S(1)}, u32[]{:S(2)}, u32[]{:S(2)}) collective-permute-start(bf16[24,7168]{1,0:T(8,128)(2,1)S(1)} %get-tuple-element.36), channel_id=1, source_target_pairs={{0,10},{1,81},{2,12},{3,83},{4,14},{5,85},{6,0},{7,87},{8,2},{9,89... | collective-permute-start | bytes 1032200 | tf_op jit(solution)/shard_map/ppermute | solution.py:245
  93.7 0.0 collective-permute-done.10.refs_1_
  93.7 6.6 %collective-permute-start.15 = (bf16[24,7168]{1,0:T(8,128)(2,1)S(1)}, bf16[24,7168]{1,0:T(8,128)(2,1)S(1)}, u32[]{:S(2)}, u32[]{:S(2)}) collective-permute-start(bf16[24,7168]{1,0:T(8,128)(2,1)S(1)} %get-tuple-element.37), channel_id=1, source_target_pairs={{0,6},{1,49},{2,8},{3,51},{4,10},{5,53},{6,12},{7,55},{8,14},{9,57... | collective-permute-start | bytes 1032200 | tf_op jit(solution)/shard_map/ppermute | solution.py:245
  100.3 0.0 collective-permute-done.11.refs_2_
  100.3 0.6 collective-permute-start.16
  100.9 1.9 %collective-permute-done.12.refs_3_ = bf16[24,7168]{1,0:T(8,128)(2,1)S(1)} collective-permute-done((bf16[24,7168]{1,0:T(8,128)(2,1)S(1)}, bf16[24,7168]{1,0:T(8,128)(2,1)S(1)}, u32[]{:S(2)}, u32[]{:S(2)}) %collective-permute-start.12) | collective-permute-done | bytes 344096 | tf_op jit(solution)/shard_map/ppermute | solution.py:245
  102.7 0.5 collective-permute-done.13.refs_4_
  103.3 15.4 %collective-permute-done.14.refs_5_ = bf16[24,7168]{1,0:T(8,128)(2,1)S(1)} collective-permute-done((bf16[24,7168]{1,0:T(8,128)(2,1)S(1)}, bf16[24,7168]{1,0:T(8,128)(2,1)S(1)}, u32[]{:S(2)}, u32[]{:S(2)}) %collective-permute-start.14) | collective-permute-done | bytes 344096 | tf_op jit(solution)/shard_map/ppermute | solution.py:245
  118.6 0.0 collective-permute-done.15.refs_6_
  118.7 4.6 %collective-permute-done.16.refs_7_ = bf16[24,7168]{1,0:T(8,128)(2,1)S(1)} collective-permute-done((bf16[24,7168]{1,0:T(8,128)(2,1)S(1)}, bf16[24,7168]{1,0:T(8,128)(2,1)S(1)}, u32[]{:S(2)}, u32[]{:S(2)}) %collective-permute-start.16) | collective-permute-done | bytes 344096 | tf_op jit(solution)/shard_map/ppermute | solution.py:245
  123.3 0.9 shard_map.76
  124.1 21.8 %all_to_all.10 = bf16[8,8,7168]{2,1,0:T(8,128)(2,1)S(1)} all-to-all(bf16[8,8,7168]{2,1,0:T(8,128)(2,1)S(1)} %bitcast.5), channel_id=1, replica_groups={{0,16,32,48,64,80,96,112},{2,18,34,50,66,82,98,114},{4,20,36,52,68,84,1..., dimensions={0} | all-to-all | bytes 1835008 | tf_op jit(solution)/shard_map/all_to_all | solution.py:239
  145.9 0.8 shard_map.77
Async XLA Ops:
  0.0 33.5 %collective-permute-start = (bf16[1,7168,256]{2,1,0:T(8,128)(2,1)}, bf16[1,7168,256]{2,1,0:T(8,128)(2,1)}, u32[]{:S(2)}, u32[]{:S(2)}) collective-permute-start(bf16[1,7168,256]{2,1,0:T(8,128)(2,1)} %refs_8_.1), channel_id=1, source_target_pairs={{0,1},{1,0},{2,3},{3,2},{4,5},{5,4},{6,7},{7,6},{8,9},{9,8},{10,11... | collective-permute-start | bytes 11010056 | tf_op jit(solution)/shard_map/ppermute | solution.py:249
  0.0 33.5 %collective-permute-start.1 = (bf16[1,7168,256]{2,1,0:T(8,128)(2,1)}, bf16[1,7168,256]{2,1,0:T(8,128)(2,1)}, u32[]{:S(2)}, u32[]{:S(2)}) collective-permute-start(bf16[1,7168,256]{2,1,0:T(8,128)(2,1)} %refs_10_.1), channel_id=1, source_target_pairs={{0,1},{1,0},{2,3},{3,2},{4,5},{5,4},{6,7},{7,6},{8,9},{9,8},{10,11... | collective-permute-start | bytes 11010056 | tf_op jit(solution)/shard_map/ppermute | solution.py:249
  0.5 33.0 %collective-permute-start.2 = (bf16[1,256,7168]{2,1,0:T(8,128)(2,1)}, bf16[1,256,7168]{2,1,0:T(8,128)(2,1)}, u32[]{:S(2)}, u32[]{:S(2)}) collective-permute-start(bf16[1,256,7168]{2,1,0:T(8,128)(2,1)} %refs_12_.1), channel_id=1, source_target_pairs={{0,1},{1,0},{2,3},{3,2},{4,5},{5,4},{6,7},{7,6},{8,9},{9,8},{10,11... | collective-permute-start | bytes 11010056 | tf_op jit(solution)/shard_map/ppermute | solution.py:249
  2.4 31.1 %all-to-all-start = ((bf16[8,8,7424]{2,1,0:T(8,128)(2,1)}), bf16[8,8,7424]{2,1,0:T(8,128)(2,1)S(1)}, u32[]{:S(2)}, u32[]{:S(2)}) async-start(bf16[8,8,7424]{2,1,0:T(8,128)(2,1)} %bitcast), calls=%async_computation | async-start | bytes 1900544 | tf_op jit(solution)/shard_map/all_to_all | solution.py:239
  35.1 12.6 %collective-permute-start.3 = (bf16[24,7168]{1,0:T(8,128)(2,1)S(1)}, bf16[24,7168]{1,0:T(8,128)(2,1)S(1)}, u32[]{:S(2)}, u32[]{:S(2)}) collective-permute-start(bf16[24,7168]{1,0:T(8,128)(2,1)S(1)} %get-tuple-element.24), channel_id=1, source_target_pairs={{0,2},{1,17},{2,4},{3,19},{4,6},{5,21},{6,8},{7,23},{8,10},{9,25},... | collective-permute-start | bytes 1032200 | tf_op jit(solution)/shard_map/ppermute | solution.py:245
  36.8 15.0 %collective-permute-start.4 = (bf16[24,7168]{1,0:T(8,128)(2,1)S(1)}, bf16[24,7168]{1,0:T(8,128)(2,1)S(1)}, u32[]{:S(2)}, u32[]{:S(2)}) collective-permute-start(bf16[24,7168]{1,0:T(8,128)(2,1)S(1)} %get-tuple-element.25), channel_id=1, source_target_pairs={{0,14},{1,113},{2,0},{3,115},{4,2},{5,117},{6,4},{7,119},{8,6},{9,... | collective-permute-start | bytes 1032200 | tf_op jit(solution)/shard_map/ppermute | solution.py:245
  37.2 22.3 %collective-permute-start.5 = (bf16[24,7168]{1,0:T(8,128)(2,1)S(1)}, bf16[24,7168]{1,0:T(8,128)(2,1)S(1)}, u32[]{:S(2)}, u32[]{:S(2)}) collective-permute-start(bf16[24,7168]{1,0:T(8,128)(2,1)S(1)} %get-tuple-element.26), channel_id=1, source_target_pairs={{0,4},{1,33},{2,6},{3,35},{4,8},{5,37},{6,10},{7,39},{8,12},{9,41}... | collective-permute-start | bytes 1032200 | tf_op jit(solution)/shard_map/ppermute | solution.py:245
  42.3 17.2 %collective-permute-start.6 = (bf16[24,7168]{1,0:T(8,128)(2,1)S(1)}, bf16[24,7168]{1,0:T(8,128)(2,1)S(1)}, u32[]{:S(2)}, u32[]{:S(2)}) collective-permute-start(bf16[24,7168]{1,0:T(8,128)(2,1)S(1)} %get-tuple-element.27), channel_id=1, source_target_pairs={{0,12},{1,97},{2,14},{3,99},{4,0},{5,101},{6,2},{7,103},{8,4},{9,1... | collective-permute-start | bytes 1032200 | tf_op jit(solution)/shard_map/ppermute | solution.py:245
  46.8 30.5 %collective-permute-start.7 = (bf16[24,7168]{1,0:T(8,128)(2,1)S(1)}, bf16[24,7168]{1,0:T(8,128)(2,1)S(1)}, u32[]{:S(2)}, u32[]{:S(2)}) collective-permute-start(bf16[24,7168]{1,0:T(8,128)(2,1)S(1)} %get-tuple-element.28), channel_id=1, source_target_pairs={{0,6},{1,49},{2,8},{3,51},{4,10},{5,53},{6,12},{7,55},{8,14},{9,57... | collective-permute-start | bytes 1032200 | tf_op jit(solution)/shard_map/ppermute | solution.py:245
  47.7 29.6 %collective-permute-start.8 = (bf16[24,7168]{1,0:T(8,128)(2,1)S(1)}, bf16[24,7168]{1,0:T(8,128)(2,1)S(1)}, u32[]{:S(2)}, u32[]{:S(2)}) collective-permute-start(bf16[24,7168]{1,0:T(8,128)(2,1)S(1)} %get-tuple-element.29), channel_id=1, source_target_pairs={{0,10},{1,81},{2,12},{3,83},{4,14},{5,85},{6,0},{7,87},{8,2},{9,89... | collective-permute-start | bytes 1032200 | tf_op jit(solution)/shard_map/ppermute | solution.py:245
  51.8 25.4 %collective-permute-start.9 = (bf16[24,7168]{1,0:T(8,128)(2,1)S(1)}, bf16[24,7168]{1,0:T(8,128)(2,1)S(1)}, u32[]{:S(2)}, u32[]{:S(2)}) collective-permute-start(bf16[24,7168]{1,0:T(8,128)(2,1)S(1)} %get-tuple-element.30), channel_id=1, source_target_pairs={{0,8},{1,65},{2,10},{3,67},{4,12},{5,69},{6,14},{7,71},{8,0},{9,73... | collective-permute-start | bytes 1032200 | tf_op jit(solution)/shard_map/ppermute | solution.py:245
  85.9 7.8 %collective-permute-start.10 = (bf16[24,7168]{1,0:T(8,128)(2,1)S(1)}, bf16[24,7168]{1,0:T(8,128)(2,1)S(1)}, u32[]{:S(2)}, u32[]{:S(2)}) collective-permute-start(bf16[24,7168]{1,0:T(8,128)(2,1)S(1)} %get-tuple-element.32), channel_id=1, source_target_pairs={{0,14},{1,113},{2,0},{3,115},{4,2},{5,117},{6,4},{7,119},{8,6},{9,... | collective-permute-start | bytes 1032200 | tf_op jit(solution)/shard_map/ppermute | solution.py:245
  87.8 12.4 %collective-permute-start.11 = (bf16[24,7168]{1,0:T(8,128)(2,1)S(1)}, bf16[24,7168]{1,0:T(8,128)(2,1)S(1)}, u32[]{:S(2)}, u32[]{:S(2)}) collective-permute-start(bf16[24,7168]{1,0:T(8,128)(2,1)S(1)} %get-tuple-element.33), channel_id=1, source_target_pairs={{0,2},{1,17},{2,4},{3,19},{4,6},{5,21},{6,8},{7,23},{8,10},{9,25},... | collective-permute-start | bytes 1032200 | tf_op jit(solution)/shard_map/ppermute | solution.py:245
  88.0 14.7 %collective-permute-start.12 = (bf16[24,7168]{1,0:T(8,128)(2,1)S(1)}, bf16[24,7168]{1,0:T(8,128)(2,1)S(1)}, u32[]{:S(2)}, u32[]{:S(2)}) collective-permute-start(bf16[24,7168]{1,0:T(8,128)(2,1)S(1)} %get-tuple-element.34), channel_id=1, source_target_pairs={{0,12},{1,97},{2,14},{3,99},{4,0},{5,101},{6,2},{7,103},{8,4},{9,1... | collective-permute-start | bytes 1032200 | tf_op jit(solution)/shard_map/ppermute | solution.py:245
  89.4 13.8 %collective-permute-start.13 = (bf16[24,7168]{1,0:T(8,128)(2,1)S(1)}, bf16[24,7168]{1,0:T(8,128)(2,1)S(1)}, u32[]{:S(2)}, u32[]{:S(2)}) collective-permute-start(bf16[24,7168]{1,0:T(8,128)(2,1)S(1)} %get-tuple-element.35), channel_id=1, source_target_pairs={{0,4},{1,33},{2,6},{3,35},{4,8},{5,37},{6,10},{7,39},{8,12},{9,41}... | collective-permute-start | bytes 1032200 | tf_op jit(solution)/shard_map/ppermute | solution.py:245
  92.2 26.5 %collective-permute-start.14 = (bf16[24,7168]{1,0:T(8,128)(2,1)S(1)}, bf16[24,7168]{1,0:T(8,128)(2,1)S(1)}, u32[]{:S(2)}, u32[]{:S(2)}) collective-permute-start(bf16[24,7168]{1,0:T(8,128)(2,1)S(1)} %get-tuple-element.36), channel_id=1, source_target_pairs={{0,10},{1,81},{2,12},{3,83},{4,14},{5,85},{6,0},{7,87},{8,2},{9,89... | collective-permute-start | bytes 1032200 | tf_op jit(solution)/shard_map/ppermute | solution.py:245
  93.7 24.9 %collective-permute-start.15 = (bf16[24,7168]{1,0:T(8,128)(2,1)S(1)}, bf16[24,7168]{1,0:T(8,128)(2,1)S(1)}, u32[]{:S(2)}, u32[]{:S(2)}) collective-permute-start(bf16[24,7168]{1,0:T(8,128)(2,1)S(1)} %get-tuple-element.37), channel_id=1, source_target_pairs={{0,6},{1,49},{2,8},{3,51},{4,10},{5,53},{6,12},{7,55},{8,14},{9,57... | collective-permute-start | bytes 1032200 | tf_op jit(solution)/shard_map/ppermute | solution.py:245
  100.3 23.0 %collective-permute-start.16 = (bf16[24,7168]{1,0:T(8,128)(2,1)S(1)}, bf16[24,7168]{1,0:T(8,128)(2,1)S(1)}, u32[]{:S(2)}, u32[]{:S(2)}) collective-permute-start(bf16[24,7168]{1,0:T(8,128)(2,1)S(1)} %get-tuple-element.38), channel_id=1, source_target_pairs={{0,8},{1,65},{2,10},{3,67},{4,12},{5,69},{6,14},{7,71},{8,0},{9,73... | collective-permute-start | bytes 1032200 | tf_op jit(solution)/shard_map/ppermute | solution.py:245

commit v4 on v3

--- a/solution.py
+++ b/solution.py
@@ -13,7 +13,6 @@
 LANES = 128
 INFO = 2 * LANES
 CAP = 3
-STEPS = 4
 MIB = 1 << 20
 
 
@@ -21,20 +20,14 @@
     return (y * side + x) * 2 + c
 
 
-def first_groups(side):
-    r = range(side)
-    down = [[device(side, y, x, 0) for y in r] for x in r]
-    over = [[device(side, y, x, 1) for x in r] for y in r]
-    return down + over
-
-
-def second_route(side, k):
+def route_pairs(side, k, stage):
     pairs = []
     for y in range(side):
         for x in range(side):
             over, down = (x + k) % side, (y + k) % side
-            pairs.append((device(side, y, x, 0), device(side, y, over, 0)))
-            pairs.append((device(side, y, x, 1), device(side, down, x, 1)))
+            for c in (0, 1):
+                far = (y, over) if c != stage else (down, x)
+                pairs.append((device(side, y, x, c), device(side, *far, c)))
     return pairs
 
 
@@ -78,11 +71,9 @@
         jnp.concatenate([r[...].astype(jnp.float32), rest], axis=1).astype(jnp.bfloat16)
         for r in (ids_ref, levels_ref)
     ]
-    for i in range(out.shape[0] // mine):
-        here = slice(i * mine, (i + 1) * mine)
-        out[here, :width] = tokens_ref[...]
-        out[here, width : width + LANES] = info[0]
-        out[here, width + LANES :] = info[1]
+    out[:, :width] = tokens_ref[...]
+    out[:, width : width + LANES] = info[0]
+    out[:, width + LANES :] = info[1]
 
 
 def selection(experts_ref, info, side, picks, toks):
@@ -142,10 +133,11 @@
         ref[k * each : (k + 1) * each] = r[...]
 
 
-def route_kernel(experts_ref, rows_ref, *refs, side, picks):
-    outs, mix_ref = refs[-side - 1 : -1], refs[-1]
+def route_kernel(experts_ref, *refs, side, picks):
+    rows, outs, mix_ref, rows_ref = refs[:side], refs[side:-2], refs[-2], refs[-1]
     width = outs[0].shape[1]
     toks = rows_ref.shape[0]
+    gathered(rows_ref, rows)
     info = rows_ref[:, width:].astype(jnp.float32)
     select, mix = selection(experts_ref, info, side, picks, toks)
     for n, m in enumerate(mix):
@@ -154,64 +146,50 @@
         put(outs, cols, jnp.dot(select, rows_ref[:, cols], preferred_element_type=jnp.float32))
 
 
+def load_kernel(*refs):
+    count = len(refs) // 2
+    sems = refs[-1]
+    copies = [pltpu.make_async_copy(refs[n], refs[count + n], sems.at[n]) for n in range(count)]
+    for copy in copies:
+        copy.start()
+    for copy in copies:
+        copy.wait()
+
+
 def expert_kernel(*refs, side):
-    arrived, weights, outs = refs[:side], refs[side : side + 6], refs[side + 6 : 2 * side + 6]
-    refs = refs[2 * side + 6 :]
-    held, acc_ref, h_ref, x_ref, sems = refs[:6], refs[6], refs[7], refs[8], refs[9]
-    part = held[0].shape[1]
-    width = x_ref.shape[1]
-    pieces = blocks(width, width // STEPS)
-    copies = []
-    for k, rows in enumerate(pieces):
-        copies.append([
-            pltpu.make_async_copy(weights[n].at[0, rows], held[n].at[rows], sems.at[n, k])
-            for n in range(4)
-        ])
-    for k, cols in enumerate(pieces):
-        copies.append([
-            pltpu.make_async_copy(weights[n].at[0, :, cols], held[n].at[:, cols], sems.at[n, k])
-            for n in (4, 5)
-        ])
-    for group in copies:
-        for copy in group:
-            copy.start()
+    arrived, held, outs = refs[:side], refs[side : side + 6], refs[side + 6 : 2 * side + 6]
+    acc_ref, h_ref, x_ref = refs[2 * side + 6 :]
+    part = held[0].shape[2]
     gathered(x_ref, arrived)
-    for k, rows in enumerate(pieces):
-        for copy in copies[k]:
-            copy.wait()
-        for n in range(4):
-            cols = slice(n * part, (n + 1) * part)
-            got = jnp.dot(x_ref[:, rows], held[n][rows], preferred_element_type=jnp.float32)
-            acc_ref[:, cols] = acc_ref[:, cols] + got if k else got
+    for n in range(4):
+        cols = slice(n * part, (n + 1) * part)
+        acc_ref[:, cols] = jnp.dot(x_ref[...], held[n][0], preferred_element_type=jnp.float32)
     gate = acc_ref[:, : 2 * part]
     up = acc_ref[:, 2 * part :]
     h_ref[...] = (gate / (1.0 + jnp.exp(-gate)) * up).astype(jnp.bfloat16)
-    for k, cols in enumerate(pieces):
-        for copy in copies[STEPS + k]:
-            copy.wait()
+    for cols in blocks(x_ref.shape[1], 4 * LANES):
         put(
             outs,
             cols,
-            jnp.dot(h_ref[:, :part], held[4][:, cols], preferred_element_type=jnp.float32)
-            + jnp.dot(h_ref[:, part:], held[5][:, cols], preferred_element_type=jnp.float32),
+            jnp.dot(h_ref[:, :part], held[4][0, :, cols], preferred_element_type=jnp.float32)
+            + jnp.dot(h_ref[:, part:], held[5][0, :, cols], preferred_element_type=jnp.float32),
         )
 
 
-def mix_kernel(mix_ref, *refs):
-    rows, out_ref, rows_ref = refs[:-2], refs[-2], refs[-1]
-    toks = out_ref.shape[0]
+def mix_kernel(mix_ref, *refs, side):
+    rows, outs, rows_ref = refs[:side], refs[side:-1], refs[-1]
+    toks = side * outs[0].shape[0]
     gathered(rows_ref, rows)
-    for cols in blocks(out_ref.shape[1], 4 * LANES):
+    for cols in blocks(rows_ref.shape[1], 4 * LANES):
         y = jnp.dot(mix_ref[...], rows_ref[:, cols], preferred_element_type=jnp.float32)
-        out_ref[:, cols] = (y[:toks] + y[toks : 2 * toks] + y[2 * toks :]).astype(jnp.bfloat16)
-
-
-def sum_kernel(rows_ref, out_ref):
-    mine = out_ref.shape[0]
-    total = rows_ref[:mine].astype(jnp.float32)
-    for i in range(1, rows_ref.shape[0] // mine):
-        total = total + rows_ref[i * mine : (i + 1) * mine].astype(jnp.float32)
-    out_ref[...] = total.astype(jnp.bfloat16)
+        put(outs, cols, y[:toks] + y[toks : 2 * toks] + y[2 * toks :])
+
+
+def sum_kernel(*refs):
+    total = refs[0][...].astype(jnp.float32)
+    for r in refs[1:-1]:
+        total = total + r[...].astype(jnp.float32)
+    refs[-1][...] = total.astype(jnp.bfloat16)
 
 
 def local(tokens, expert_ids, route_levels, gate_proj, up_proj, down_proj):
@@ -233,54 +211,54 @@
 
     each = slots // side
 
-    def first_crossed(block):
-        rows, cols = block.shape
-        block = block.reshape(side, rows // side, cols)
-        block = lax.all_to_all(block, GROUP, 0, 0, tiled=True, axis_index_groups=first_groups(side))
-        return block.reshape(rows, cols)
-
-    def second_crossed(rows, sign):
+
+    def crossed(rows, stage, sign):
         moved = [rows[0]]
         for n in range(1, side):
-            moved.append(lax.ppermute(rows[n], GROUP, second_route(side, sign * order[n])))
+            pairs = route_pairs(side, sign * order[n], stage)
+            moved.append(lax.ppermute(rows[n], GROUP, pairs))
         return moved
-
-    gate_peer, up_peer, down_peer = (
-        lax.ppermute(w, "sub", [(0, 1), (1, 0)]) for w in (gate_proj, up_proj, down_proj)
-    )
 
     rows = call(
         pack_kernel,
         [(tokens, PLAIN), (expert_ids, PLAIN), (route_levels, PLAIN)],
-        [((toks, width + INFO), bf16, PLAIN)],
-    )
-    rows = first_crossed(rows)
+        [((mine, width + INFO), bf16, V)],
+    )
+    rows = crossed([rows] * side, 0, 1)
+
+    gate_peer, up_peer, down_peer = (
+        lax.ppermute(w, "sub", [(0, 1), (1, 0)]) for w in (gate_proj, up_proj, down_proj)
+    )
+
     *rows, mix = call(
         functools.partial(route_kernel, side=side, picks=picks),
-        [(experts, S), (rows, V)] + [(w, A) for w in (gate_peer, up_peer, down_peer)],
+        [(experts, S)] + [(r, V) for r in rows],
         [((each, width), bf16, V)] * side + [((3 * toks, slots), bf16, V)],
-    )
-    rows = second_crossed(rows, 1)
+        [V((toks, width + INFO), bf16)],
+    )
+    rows = crossed(rows, 1, 1)
+    weights = [gate_proj, gate_peer, up_proj, up_peer, down_proj, down_peer]
+    weights = call(
+        load_kernel,
+        [(w, A) for w in weights],
+        [(w.shape, bf16, V) for w in weights],
+        [pltpu.SemaphoreType.DMA((len(weights),))],
+    )
     rows = call(
         functools.partial(expert_kernel, side=side),
-        [(r, V) for r in rows]
-        + [(w, A) for w in (gate_proj, gate_peer, up_proj, up_peer, down_proj, down_peer)],
+        [(r, V) for r in rows] + [(w, V) for w in weights],
         [((each, width), bf16, V)] * side,
-        [V((width, part), bf16)] * 4
-        + [V((part, width), bf16)] * 2
-        + [V((slots, 4 * part), f32), V((slots, 2 * part), bf16), V((slots, width), bf16)]
-        + [pltpu.SemaphoreType.DMA((6, STEPS))],
-        limit=36,
-    )
-    rows = second_crossed(rows, -1)
+        [V((slots, 4 * part), f32), V((slots, 2 * part), bf16), V((slots, width), bf16)],
+    )
+    rows = crossed(rows, 1, -1)
     rows = call(
-        mix_kernel,
+        functools.partial(mix_kernel, side=side),
         [(mix, V)] + [(r, V) for r in rows],
-        [((toks, width), bf16, V)],
+        [((mine, width), bf16, V)] * side,
         [V((slots, width), bf16)],
     )
-    rows = first_crossed(rows)
-    return call(sum_kernel, [(rows, V)], [((mine, width), bf16, PLAIN)])
+    rows = crossed(rows, 0, -1)
+    return call(sum_kernel, [(r, V) for r in rows], [((mine, width), bf16, PLAIN)])
 
 
 def solution(mesh):

time: 147 us -> 162 us (1.10)
  starting transfers between devices: 48.9 us -> 77.4 us
  blocking collectives: 21.8 us -> 0 us
  waiting for transfers between devices: 61.5 us -> 67.6 us
  Pallas kernels: 13.8 us -> 16.1 us
    ppermute x14 -> x28, starting transfers between devices: 35.3 us -> 76.9 us  [crossed(): moved.append(lax.ppermute(rows[n], GROUP, pairs))]
    ppermute x14 -> x28, waiting for transfers between devices: 44.2 us -> 67.6 us  [crossed(): moved.append(lax.ppermute(rows[n], GROUP, pairs))]
    all_to_all x1 -> x0, blocking collectives: 21.8 us -> none  [first_crossed(): lax.all_to_all(block, GROUP, 0, 0, tiled=True, axis_index_groups=first_gr...]
    all_to_all x1 -> x0, waiting for transfers between devices: 17.2 us -> none  [first_crossed(): lax.all_to_all(block, GROUP, 0, 0, tiled=True, axis_index_groups=first_gr...]
    all_to_all x1 -> x0, starting transfers between devices: 13.2 us -> none  [first_crossed(): lax.all_to_all(block, GROUP, 0, 0, tiled=True, axis_index_groups=first_gr...]
    pallas_call x5 -> x6, Pallas kernels: 13.8 us -> 16.1 us  [call(): pl.pallas_call(kernel, in_specs=[pl.BlockSpec(memory_space=V if space is...]
  transfers between devices with their start and end apart: 18 -> 31, of which waited for: 7 -> 15; matrix products, arithmetic and copies ran while one was open for 0% -> 0% of each run, Pallas kernels for 1% -> 6%
where the time goes in v4:
time: 162 us
  starting transfers between devices  77.4 us (48%)
  waiting for transfers between devices  67.6 us (42%)
  Pallas kernels  16.1 us (10%)
    ppermute x28, starting transfers between devices, crossed(): moved.append(lax.ppermute(rows[n], GROUP, pairs))  76.9 us
    ppermute x28, waiting for transfers between devices, crossed(): moved.append(lax.ppermute(rows[n], GROUP, pairs))  67.6 us
    pallas_call x6, Pallas kernels, call(): pl.pallas_call(kernel, in_specs=[pl.BlockSpec(memory_space=V if space is...  16.1 us
  transfers between devices with their start and end apart: 31, of which 15 were waited for; matrix products, arithmetic and copies ran while one was open for 0% of the time, Pallas kernels for 6%

profile of v4, /device:TPU:516, one launch (start us, length us, event | category | flops | bytes accessed | tf_op | source)
XLA Modules:
  0.0 161.8 jit_solution(10621523459466700735)
XLA Ops:
  0.0 0.5 collective-permute-start.15
  0.5 0.9 shard_map.73.refs_0_
  1.4 10.7 %collective-permute-start.6 = (bf16[8,7424]{1,0:T(8,128)(2,1)S(1)}, bf16[8,7424]{1,0:T(8,128)(2,1)S(1)}, u32[]{:S(2)}, u32[]{:S(2)}) collective-permute-start(bf16[8,7424]{1,0:T(8,128)(2,1)S(1)} %shard_map.73.refs_0_), channel_id=1, source_target_pairs={{0,64},{1,9},{2,66},{3,11},{4,68},{5,13},{6,70},{7,15},{8,72},{9,1... | collective-permute-start | bytes 356360 | tf_op jit(solution)/shard_map/ppermute | solution.py:219
  12.2 0.6 collective-permute-start.5
  12.7 3.1 %collective-permute-done.6.refs_7_ = bf16[8,7424]{1,0:T(8,128)(2,1)S(1)} collective-permute-done((bf16[8,7424]{1,0:T(8,128)(2,1)S(1)}, bf16[8,7424]{1,0:T(8,128)(2,1)S(1)}, u32[]{:S(2)}, u32[]{:S(2)}) %collective-permute-start.6) | collective-permute-done | bytes 118816 | tf_op jit(solution)/shard_map/ppermute | solution.py:219
  15.9 3.7 %collective-permute-start.4 = (bf16[8,7424]{1,0:T(8,128)(2,1)S(1)}, bf16[8,7424]{1,0:T(8,128)(2,1)S(1)}, u32[]{:S(2)}, u32[]{:S(2)}) collective-permute-start(bf16[8,7424]{1,0:T(8,128)(2,1)S(1)} %shard_map.73.refs_0_), channel_id=1, source_target_pairs={{0,48},{1,7},{2,50},{3,9},{4,52},{5,11},{6,54},{7,13},{8,56},{9,15... | collective-permute-start | bytes 356360 | tf_op jit(solution)/shard_map/ppermute | solution.py:219
  19.5 3.9 %collective-permute-done.5.refs_6_ = bf16[8,7424]{1,0:T(8,128)(2,1)S(1)} collective-permute-done((bf16[8,7424]{1,0:T(8,128)(2,1)S(1)}, bf16[8,7424]{1,0:T(8,128)(2,1)S(1)}, u32[]{:S(2)}, u32[]{:S(2)}) %collective-permute-start.5) | collective-permute-done | bytes 118816 | tf_op jit(solution)/shard_map/ppermute | solution.py:219
  23.4 1.0 collective-permute-start.3
  24.5 4.8 %collective-permute-start.2 = (bf16[8,7424]{1,0:T(8,128)(2,1)S(1)}, bf16[8,7424]{1,0:T(8,128)(2,1)S(1)}, u32[]{:S(2)}, u32[]{:S(2)}) collective-permute-start(bf16[8,7424]{1,0:T(8,128)(2,1)S(1)} %shard_map.73.refs_0_), channel_id=1, source_target_pairs={{0,32},{1,5},{2,34},{3,7},{4,36},{5,9},{6,38},{7,11},{8,40},{9,13}... | collective-permute-start | bytes 356360 | tf_op jit(solution)/shard_map/ppermute | solution.py:219
  29.3 0.1 collective-permute-done.3.refs_4_
  29.4 3.4 %collective-permute-start.1 = (bf16[8,7424]{1,0:T(8,128)(2,1)S(1)}, bf16[8,7424]{1,0:T(8,128)(2,1)S(1)}, u32[]{:S(2)}, u32[]{:S(2)}) collective-permute-start(bf16[8,7424]{1,0:T(8,128)(2,1)S(1)} %shard_map.73.refs_0_), channel_id=1, source_target_pairs={{0,112},{1,15},{2,114},{3,1},{4,116},{5,3},{6,118},{7,5},{8,120},{... | collective-permute-start | bytes 356360 | tf_op jit(solution)/shard_map/ppermute | solution.py:219
  32.8 3.4 %collective-permute-done.2.refs_3_ = bf16[8,7424]{1,0:T(8,128)(2,1)S(1)} collective-permute-done((bf16[8,7424]{1,0:T(8,128)(2,1)S(1)}, bf16[8,7424]{1,0:T(8,128)(2,1)S(1)}, u32[]{:S(2)}, u32[]{:S(2)}) %collective-permute-start.2) | collective-permute-done | bytes 118816 | tf_op jit(solution)/shard_map/ppermute | solution.py:219
  36.2 0.7 broadcast_select_fusion.experts_ref
  36.9 5.4 %collective-permute-done.refs_1_ = bf16[8,7424]{1,0:T(8,128)(2,1)S(1)} collective-permute-done((bf16[8,7424]{1,0:T(8,128)(2,1)S(1)}, bf16[8,7424]{1,0:T(8,128)(2,1)S(1)}, u32[]{:S(2)}, u32[]{:S(2)}) %collective-permute-start) | collective-permute-done | bytes 118816 | tf_op jit(solution)/shard_map/ppermute | solution.py:219
  42.2 1.6 shard_map.74
  43.8 1.8 %collective-permute-start.7 = (bf16[24,7168]{1,0:T(8,128)(2,1)S(1)}, bf16[24,7168]{1,0:T(8,128)(2,1)S(1)}, u32[]{:S(2)}, u32[]{:S(2)}) collective-permute-start(bf16[24,7168]{1,0:T(8,128)(2,1)S(1)} %get-tuple-element.38), channel_id=1, source_target_pairs={{0,2},{1,17},{2,4},{3,19},{4,6},{5,21},{6,8},{7,23},{8,10},{9,25},... | collective-permute-start | bytes 1032200 | tf_op jit(solution)/shard_map/ppermute | solution.py:219
  45.6 0.4 collective-permute-start.8
  46.0 5.2 %collective-permute-done.7.refs_1_ = bf16[24,7168]{1,0:T(8,128)(2,1)S(1)} collective-permute-done((bf16[24,7168]{1,0:T(8,128)(2,1)S(1)}, bf16[24,7168]{1,0:T(8,128)(2,1)S(1)}, u32[]{:S(2)}, u32[]{:S(2)}) %collective-permute-start.7) | collective-permute-done | bytes 344096 | tf_op jit(solution)/shard_map/ppermute | solution.py:219
  51.2 5.1 %collective-permute-start.9 = (bf16[24,7168]{1,0:T(8,128)(2,1)S(1)}, bf16[24,7168]{1,0:T(8,128)(2,1)S(1)}, u32[]{:S(2)}, u32[]{:S(2)}) collective-permute-start(bf16[24,7168]{1,0:T(8,128)(2,1)S(1)} %get-tuple-element.40), channel_id=1, source_target_pairs={{0,4},{1,33},{2,6},{3,35},{4,8},{5,37},{6,10},{7,39},{8,12},{9,41}... | collective-permute-start | bytes 1032200 | tf_op jit(solution)/shard_map/ppermute | solution.py:219
  56.3 7.6 %collective-permute-start.10 = (bf16[24,7168]{1,0:T(8,128)(2,1)S(1)}, bf16[24,7168]{1,0:T(8,128)(2,1)S(1)}, u32[]{:S(2)}, u32[]{:S(2)}) collective-permute-start(bf16[24,7168]{1,0:T(8,128)(2,1)S(1)} %get-tuple-element.41), channel_id=1, source_target_pairs={{0,12},{1,97},{2,14},{3,99},{4,0},{5,101},{6,2},{7,103},{8,4},{9,1... | collective-permute-start | bytes 1032200 | tf_op jit(solution)/shard_map/ppermute | solution.py:219
  63.9 0.7 collective-permute-start.11
  64.6 4.3 %collective-permute-start.12 = (bf16[24,7168]{1,0:T(8,128)(2,1)S(1)}, bf16[24,7168]{1,0:T(8,128)(2,1)S(1)}, u32[]{:S(2)}, u32[]{:S(2)}) collective-permute-start(bf16[24,7168]{1,0:T(8,128)(2,1)S(1)} %get-tuple-element.43), channel_id=1, source_target_pairs={{0,10},{1,81},{2,12},{3,83},{4,14},{5,85},{6,0},{7,87},{8,2},{9,89... | collective-permute-start | bytes 1032200 | tf_op jit(solution)/shard_map/ppermute | solution.py:219
  68.9 3.9 %collective-permute-start.13 = (bf16[24,7168]{1,0:T(8,128)(2,1)S(1)}, bf16[24,7168]{1,0:T(8,128)(2,1)S(1)}, u32[]{:S(2)}, u32[]{:S(2)}) collective-permute-start(bf16[24,7168]{1,0:T(8,128)(2,1)S(1)} %get-tuple-element.44), channel_id=1, source_target_pairs={{0,8},{1,65},{2,10},{3,67},{4,12},{5,69},{6,14},{7,71},{8,0},{9,73... | collective-permute-start | bytes 1032200 | tf_op jit(solution)/shard_map/ppermute | solution.py:219
  72.8 7.4 %shard_map.75 = (bf16[1,7168,256]{2,1,0:T(8,128)(2,1)S(1)}, bf16[1,7168,256]{2,1,0:T(8,128)(2,1)S(1)}, bf16[1,7168,256]{2,1,0:T(8,128)(2,1)S(1)}, bf16[1,7168,25...) custom-call(bf16[1,7168,256]{2,1,0:T(8,128)(2,1)} %refs_0_.1, ...), custom_call_target="tpu_custom_call" | custom-call | tf_op jit(solution)/shard_map/pallas_call | solution.py:52
  80.2 2.8 %collective-permute-done.10.refs_4_ = bf16[24,7168]{1,0:T(8,128)(2,1)S(1)} collective-permute-done((bf16[24,7168]{1,0:T(8,128)(2,1)S(1)}, bf16[24,7168]{1,0:T(8,128)(2,1)S(1)}, u32[]{:S(2)}, u32[]{:S(2)}) %collective-permute-start.10) | collective-permute-done | bytes 344096 | tf_op jit(solution)/shard_map/ppermute | solution.py:219
  83.0 6.0 %collective-permute-done.12.refs_6_ = bf16[24,7168]{1,0:T(8,128)(2,1)S(1)} collective-permute-done((bf16[24,7168]{1,0:T(8,128)(2,1)S(1)}, bf16[24,7168]{1,0:T(8,128)(2,1)S(1)}, u32[]{:S(2)}, u32[]{:S(2)}) %collective-permute-start.12) | collective-permute-done | bytes 344096 | tf_op jit(solution)/shard_map/ppermute | solution.py:219
  89.0 3.6 %collective-permute-done.13.refs_7_ = bf16[24,7168]{1,0:T(8,128)(2,1)S(1)} collective-permute-done((bf16[24,7168]{1,0:T(8,128)(2,1)S(1)}, bf16[24,7168]{1,0:T(8,128)(2,1)S(1)}, u32[]{:S(2)}, u32[]{:S(2)}) %collective-permute-start.13) | collective-permute-done | bytes 344096 | tf_op jit(solution)/shard_map/ppermute | solution.py:219
  92.5 4.5 %shard_map.76 = (bf16[24,7168]{1,0:T(8,128)(2,1)S(1)}, bf16[24,7168]{1,0:T(8,128)(2,1)S(1)}, bf16[24,7168]{1,0:T(8,128)(2,1)S(1)}, bf16[24,7168]{1,0:T(8,128)(2,...) custom-call(bf16[24,7168]{1,0:T(8,128)(2,1)S(1)} %get-tuple-element., ...), custom_call_target="tpu_custom_call" | custom-call | tf_op jit(solution)/shard_map/pallas_call | solution.py:52
  97.1 3.8 %collective-permute-start.17 = (bf16[24,7168]{1,0:T(8,128)(2,1)S(1)}, bf16[24,7168]{1,0:T(8,128)(2,1)S(1)}, u32[]{:S(2)}, u32[]{:S(2)}) collective-permute-start(bf16[24,7168]{1,0:T(8,128)(2,1)S(1)} %get-tuple-element.52), channel_id=1, source_target_pairs={{0,14},{1,113},{2,0},{3,115},{4,2},{5,117},{6,4},{7,119},{8,6},{9,... | collective-permute-start | bytes 1032200 | tf_op jit(solution)/shard_map/ppermute | solution.py:219
  100.9 1.6 collective-permute-start.19
  102.5 2.5 %collective-permute-start.20 = (bf16[24,7168]{1,0:T(8,128)(2,1)S(1)}, bf16[24,7168]{1,0:T(8,128)(2,1)S(1)}, u32[]{:S(2)}, u32[]{:S(2)}) collective-permute-start(bf16[24,7168]{1,0:T(8,128)(2,1)S(1)} %get-tuple-element.55), channel_id=1, source_target_pairs={{0,4},{1,33},{2,6},{3,35},{4,8},{5,37},{6,10},{7,39},{8,12},{9,41}... | collective-permute-start | bytes 1032200 | tf_op jit(solution)/shard_map/ppermute | solution.py:219
  105.0 2.1 %collective-permute-start.21 = (bf16[24,7168]{1,0:T(8,128)(2,1)S(1)}, bf16[24,7168]{1,0:T(8,128)(2,1)S(1)}, u32[]{:S(2)}, u32[]{:S(2)}) collective-permute-start(bf16[24,7168]{1,0:T(8,128)(2,1)S(1)} %get-tuple-element.56), channel_id=1, source_target_pairs={{0,10},{1,81},{2,12},{3,83},{4,14},{5,85},{6,0},{7,87},{8,2},{9,89... | collective-permute-start | bytes 1032200 | tf_op jit(solution)/shard_map/ppermute | solution.py:219
  107.2 6.6 %collective-permute-start.22 = (bf16[24,7168]{1,0:T(8,128)(2,1)S(1)}, bf16[24,7168]{1,0:T(8,128)(2,1)S(1)}, u32[]{:S(2)}, u32[]{:S(2)}) collective-permute-start(bf16[24,7168]{1,0:T(8,128)(2,1)S(1)} %get-tuple-element.57), channel_id=1, source_target_pairs={{0,6},{1,49},{2,8},{3,51},{4,10},{5,53},{6,12},{7,55},{8,14},{9,57... | collective-permute-start | bytes 1032200 | tf_op jit(solution)/shard_map/ppermute | solution.py:219
  113.7 1.2 collective-permute-start.23
  114.9 0.7 collective-permute-done.19.refs_3_
  115.6 14.1 %collective-permute-done.21.refs_5_ = bf16[24,7168]{1,0:T(8,128)(2,1)S(1)} collective-permute-done((bf16[24,7168]{1,0:T(8,128)(2,1)S(1)}, bf16[24,7168]{1,0:T(8,128)(2,1)S(1)}, u32[]{:S(2)}, u32[]{:S(2)}) %collective-permute-start.21) | collective-permute-done | bytes 344096 | tf_op jit(solution)/shard_map/ppermute | solution.py:219
  129.8 12.2 %collective-permute-done.23.refs_7_ = bf16[24,7168]{1,0:T(8,128)(2,1)S(1)} collective-permute-done((bf16[24,7168]{1,0:T(8,128)(2,1)S(1)}, bf16[24,7168]{1,0:T(8,128)(2,1)S(1)}, u32[]{:S(2)}, u32[]{:S(2)}) %collective-permute-start.23) | collective-permute-done | bytes 344096 | tf_op jit(solution)/shard_map/ppermute | solution.py:219
  142.0 0.9 shard_map.77
  142.9 0.1 collective-permute-start.24
  143.0 2.0 %collective-permute-start.25 = (bf16[8,7168]{1,0:T(8,128)(2,1)S(1)}, bf16[8,7168]{1,0:T(8,128)(2,1)S(1)}, u32[]{:S(2)}, u32[]{:S(2)}) collective-permute-start(bf16[8,7168]{1,0:T(8,128)(2,1)S(1)} %get-tuple-element.61), channel_id=1, source_target_pairs={{0,16},{1,3},{2,18},{3,5},{4,20},{5,7},{6,22},{7,9},{8,24},{9,11},... | collective-permute-start | bytes 344072 | tf_op jit(solution)/shard_map/ppermute | solution.py:219
  145.0 2.9 %collective-permute-start.27 = (bf16[8,7168]{1,0:T(8,128)(2,1)S(1)}, bf16[8,7168]{1,0:T(8,128)(2,1)S(1)}, u32[]{:S(2)}, u32[]{:S(2)}) collective-permute-start(bf16[8,7168]{1,0:T(8,128)(2,1)S(1)} %get-tuple-element.63), channel_id=1, source_target_pairs={{0,32},{1,5},{2,34},{3,7},{4,36},{5,9},{6,38},{7,11},{8,40},{9,13}... | collective-permute-start | bytes 344072 | tf_op jit(solution)/shard_map/ppermute | solution.py:219
  147.9 1.0 collective-permute-start.28
  148.9 2.8 %collective-permute-start.29 = (bf16[8,7168]{1,0:T(8,128)(2,1)S(1)}, bf16[8,7168]{1,0:T(8,128)(2,1)S(1)}, u32[]{:S(2)}, u32[]{:S(2)}) collective-permute-start(bf16[8,7168]{1,0:T(8,128)(2,1)S(1)} %get-tuple-element.65), channel_id=1, source_target_pairs={{0,48},{1,7},{2,50},{3,9},{4,52},{5,11},{6,54},{7,13},{8,56},{9,15... | collective-permute-start | bytes 344072 | tf_op jit(solution)/shard_map/ppermute | solution.py:219
  151.8 2.2 %collective-permute-start.30 = (bf16[8,7168]{1,0:T(8,128)(2,1)S(1)}, bf16[8,7168]{1,0:T(8,128)(2,1)S(1)}, u32[]{:S(2)}, u32[]{:S(2)}) collective-permute-start(bf16[8,7168]{1,0:T(8,128)(2,1)S(1)} %get-tuple-element.66), channel_id=1, source_target_pairs={{0,64},{1,9},{2,66},{3,11},{4,68},{5,13},{6,70},{7,15},{8,72},{9,1... | collective-permute-start | bytes 344072 | tf_op jit(solution)/shard_map/ppermute | solution.py:219
  154.0 1.2 collective-permute-done.28.refs_5_
  155.1 3.6 %collective-permute-done.29.refs_6_ = bf16[8,7168]{1,0:T(8,128)(2,1)S(1)} collective-permute-done((bf16[8,7168]{1,0:T(8,128)(2,1)S(1)}, bf16[8,7168]{1,0:T(8,128)(2,1)S(1)}, u32[]{:S(2)}, u32[]{:S(2)}) %collective-permute-start.29) | collective-permute-done | bytes 114720 | tf_op jit(solution)/shard_map/ppermute | solution.py:219
  158.8 2.2 %collective-permute-done.30.refs_7_ = bf16[8,7168]{1,0:T(8,128)(2,1)S(1)} collective-permute-done((bf16[8,7168]{1,0:T(8,128)(2,1)S(1)}, bf16[8,7168]{1,0:T(8,128)(2,1)S(1)}, u32[]{:S(2)}, u32[]{:S(2)}) %collective-permute-start.30) | collective-permute-done | bytes 114720 | tf_op jit(solution)/shard_map/ppermute | solution.py:219
  161.0 0.8 shard_map.78
  (21 shorter events, 0.1 us)
Async XLA Ops:
  0.0 63.9 %collective-permute-start.14 = (bf16[1,7168,256]{2,1,0:T(8,128)(2,1)}, bf16[1,7168,256]{2,1,0:T(8,128)(2,1)}, u32[]{:S(2)}, u32[]{:S(2)}) collective-permute-start(bf16[1,7168,256]{2,1,0:T(8,128)(2,1)} %refs_0_.1), channel_id=1, source_target_pairs={{0,1},{1,0},{2,3},{3,2},{4,5},{5,4},{6,7},{7,6},{8,9},{9,8},{10,11... | collective-permute-start | bytes 11010056 | tf_op jit(solution)/shard_map/ppermute | solution.py:230
  0.0 64.6 %collective-permute-start.15 = (bf16[1,7168,256]{2,1,0:T(8,128)(2,1)}, bf16[1,7168,256]{2,1,0:T(8,128)(2,1)}, u32[]{:S(2)}, u32[]{:S(2)}) collective-permute-start(bf16[1,7168,256]{2,1,0:T(8,128)(2,1)} %refs_2_.1), channel_id=1, source_target_pairs={{0,1},{1,0},{2,3},{3,2},{4,5},{5,4},{6,7},{7,6},{8,9},{9,8},{10,11... | collective-permute-start | bytes 11010056 | tf_op jit(solution)/shard_map/ppermute | solution.py:230
  0.5 68.4 %collective-permute-start.16 = (bf16[1,256,7168]{2,1,0:T(8,128)(2,1)}, bf16[1,256,7168]{2,1,0:T(8,128)(2,1)}, u32[]{:S(2)}, u32[]{:S(2)}) collective-permute-start(bf16[1,256,7168]{2,1,0:T(8,128)(2,1)} %refs_4_.1), channel_id=1, source_target_pairs={{0,1},{1,0},{2,3},{3,2},{4,5},{5,4},{6,7},{7,6},{8,9},{9,8},{10,11... | collective-permute-start | bytes 11010056 | tf_op jit(solution)/shard_map/ppermute | solution.py:230
  1.4 14.4 %collective-permute-start.6 = (bf16[8,7424]{1,0:T(8,128)(2,1)S(1)}, bf16[8,7424]{1,0:T(8,128)(2,1)S(1)}, u32[]{:S(2)}, u32[]{:S(2)}) collective-permute-start(bf16[8,7424]{1,0:T(8,128)(2,1)S(1)} %shard_map.73.refs_0_), channel_id=1, source_target_pairs={{0,64},{1,9},{2,66},{3,11},{4,68},{5,13},{6,70},{7,15},{8,72},{9,1... | collective-permute-start | bytes 356360 | tf_op jit(solution)/shard_map/ppermute | solution.py:219
  12.2 11.2 %collective-permute-start.5 = (bf16[8,7424]{1,0:T(8,128)(2,1)S(1)}, bf16[8,7424]{1,0:T(8,128)(2,1)S(1)}, u32[]{:S(2)}, u32[]{:S(2)}) collective-permute-start(bf16[8,7424]{1,0:T(8,128)(2,1)S(1)} %shard_map.73.refs_0_), channel_id=1, source_target_pairs={{0,80},{1,11},{2,82},{3,13},{4,84},{5,15},{6,86},{7,1},{8,88},{9,3... | collective-permute-start | bytes 356360 | tf_op jit(solution)/shard_map/ppermute | solution.py:219
  15.9 8.7 %collective-permute-start.4 = (bf16[8,7424]{1,0:T(8,128)(2,1)S(1)}, bf16[8,7424]{1,0:T(8,128)(2,1)S(1)}, u32[]{:S(2)}, u32[]{:S(2)}) collective-permute-start(bf16[8,7424]{1,0:T(8,128)(2,1)S(1)} %shard_map.73.refs_0_), channel_id=1, source_target_pairs={{0,48},{1,7},{2,50},{3,9},{4,52},{5,11},{6,54},{7,13},{8,56},{9,15... | collective-permute-start | bytes 356360 | tf_op jit(solution)/shard_map/ppermute | solution.py:219
  23.4 5.9 %collective-permute-start.3 = (bf16[8,7424]{1,0:T(8,128)(2,1)S(1)}, bf16[8,7424]{1,0:T(8,128)(2,1)S(1)}, u32[]{:S(2)}, u32[]{:S(2)}) collective-permute-start(bf16[8,7424]{1,0:T(8,128)(2,1)S(1)} %shard_map.73.refs_0_), channel_id=1, source_target_pairs={{0,96},{1,13},{2,98},{3,15},{4,100},{5,1},{6,102},{7,3},{8,104},{9... | collective-permute-start | bytes 356360 | tf_op jit(solution)/shard_map/ppermute | solution.py:219
  24.5 11.7 %collective-permute-start.2 = (bf16[8,7424]{1,0:T(8,128)(2,1)S(1)}, bf16[8,7424]{1,0:T(8,128)(2,1)S(1)}, u32[]{:S(2)}, u32[]{:S(2)}) collective-permute-start(bf16[8,7424]{1,0:T(8,128)(2,1)S(1)} %shard_map.73.refs_0_), channel_id=1, source_target_pairs={{0,32},{1,5},{2,34},{3,7},{4,36},{5,9},{6,38},{7,11},{8,40},{9,13}... | collective-permute-start | bytes 356360 | tf_op jit(solution)/shard_map/ppermute | solution.py:219
  29.4 7.5 %collective-permute-start.1 = (bf16[8,7424]{1,0:T(8,128)(2,1)S(1)}, bf16[8,7424]{1,0:T(8,128)(2,1)S(1)}, u32[]{:S(2)}, u32[]{:S(2)}) collective-permute-start(bf16[8,7424]{1,0:T(8,128)(2,1)S(1)} %shard_map.73.refs_0_), channel_id=1, source_target_pairs={{0,112},{1,15},{2,114},{3,1},{4,116},{5,3},{6,118},{7,5},{8,120},{... | collective-permute-start | bytes 356360 | tf_op jit(solution)/shard_map/ppermute | solution.py:219
  36.2 6.0 %collective-permute-start = (bf16[8,7424]{1,0:T(8,128)(2,1)S(1)}, bf16[8,7424]{1,0:T(8,128)(2,1)S(1)}, u32[]{:S(2)}, u32[]{:S(2)}) collective-permute-start(bf16[8,7424]{1,0:T(8,128)(2,1)S(1)} %shard_map.73.refs_0_), channel_id=1, source_target_pairs={{0,16},{1,3},{2,18},{3,5},{4,20},{5,7},{6,22},{7,9},{8,24},{9,11},... | collective-permute-start | bytes 356360 | tf_op jit(solution)/shard_map/ppermute | solution.py:219
  43.8 7.4 %collective-permute-start.7 = (bf16[24,7168]{1,0:T(8,128)(2,1)S(1)}, bf16[24,7168]{1,0:T(8,128)(2,1)S(1)}, u32[]{:S(2)}, u32[]{:S(2)}) collective-permute-start(bf16[24,7168]{1,0:T(8,128)(2,1)S(1)} %get-tuple-element.38), channel_id=1, source_target_pairs={{0,2},{1,17},{2,4},{3,19},{4,6},{5,21},{6,8},{7,23},{8,10},{9,25},... | collective-permute-start | bytes 1032200 | tf_op jit(solution)/shard_map/ppermute | solution.py:219
  45.6 10.7 %collective-permute-start.8 = (bf16[24,7168]{1,0:T(8,128)(2,1)S(1)}, bf16[24,7168]{1,0:T(8,128)(2,1)S(1)}, u32[]{:S(2)}, u32[]{:S(2)}) collective-permute-start(bf16[24,7168]{1,0:T(8,128)(2,1)S(1)} %get-tuple-element.39), channel_id=1, source_target_pairs={{0,14},{1,113},{2,0},{3,115},{4,2},{5,117},{6,4},{7,119},{8,6},{9,... | collective-permute-start | bytes 1032200 | tf_op jit(solution)/shard_map/ppermute | solution.py:219
  51.2 29.0 %collective-permute-start.9 = (bf16[24,7168]{1,0:T(8,128)(2,1)S(1)}, bf16[24,7168]{1,0:T(8,128)(2,1)S(1)}, u32[]{:S(2)}, u32[]{:S(2)}) collective-permute-start(bf16[24,7168]{1,0:T(8,128)(2,1)S(1)} %get-tuple-element.40), channel_id=1, source_target_pairs={{0,4},{1,33},{2,6},{3,35},{4,8},{5,37},{6,10},{7,39},{8,12},{9,41}... | collective-permute-start | bytes 1032200 | tf_op jit(solution)/shard_map/ppermute | solution.py:219
  56.3 26.7 %collective-permute-start.10 = (bf16[24,7168]{1,0:T(8,128)(2,1)S(1)}, bf16[24,7168]{1,0:T(8,128)(2,1)S(1)}, u32[]{:S(2)}, u32[]{:S(2)}) collective-permute-start(bf16[24,7168]{1,0:T(8,128)(2,1)S(1)} %get-tuple-element.41), channel_id=1, source_target_pairs={{0,12},{1,97},{2,14},{3,99},{4,0},{5,101},{6,2},{7,103},{8,4},{9,1... | collective-permute-start | bytes 1032200 | tf_op jit(solution)/shard_map/ppermute | solution.py:219
  63.9 19.1 %collective-permute-start.11 = (bf16[24,7168]{1,0:T(8,128)(2,1)S(1)}, bf16[24,7168]{1,0:T(8,128)(2,1)S(1)}, u32[]{:S(2)}, u32[]{:S(2)}) collective-permute-start(bf16[24,7168]{1,0:T(8,128)(2,1)S(1)} %get-tuple-element.42), channel_id=1, source_target_pairs={{0,6},{1,49},{2,8},{3,51},{4,10},{5,53},{6,12},{7,55},{8,14},{9,57... | collective-permute-start | bytes 1032200 | tf_op jit(solution)/shard_map/ppermute | solution.py:219
  64.6 24.4 %collective-permute-start.12 = (bf16[24,7168]{1,0:T(8,128)(2,1)S(1)}, bf16[24,7168]{1,0:T(8,128)(2,1)S(1)}, u32[]{:S(2)}, u32[]{:S(2)}) collective-permute-start(bf16[24,7168]{1,0:T(8,128)(2,1)S(1)} %get-tuple-element.43), channel_id=1, source_target_pairs={{0,10},{1,81},{2,12},{3,83},{4,14},{5,85},{6,0},{7,87},{8,2},{9,89... | collective-permute-start | bytes 1032200 | tf_op jit(solution)/shard_map/ppermute | solution.py:219
  68.9 23.6 %collective-permute-start.13 = (bf16[24,7168]{1,0:T(8,128)(2,1)S(1)}, bf16[24,7168]{1,0:T(8,128)(2,1)S(1)}, u32[]{:S(2)}, u32[]{:S(2)}) collective-permute-start(bf16[24,7168]{1,0:T(8,128)(2,1)S(1)} %get-tuple-element.44), channel_id=1, source_target_pairs={{0,8},{1,65},{2,10},{3,67},{4,12},{5,69},{6,14},{7,71},{8,0},{9,73... | collective-permute-start | bytes 1032200 | tf_op jit(solution)/shard_map/ppermute | solution.py:219
  97.1 10.1 %collective-permute-start.17 = (bf16[24,7168]{1,0:T(8,128)(2,1)S(1)}, bf16[24,7168]{1,0:T(8,128)(2,1)S(1)}, u32[]{:S(2)}, u32[]{:S(2)}) collective-permute-start(bf16[24,7168]{1,0:T(8,128)(2,1)S(1)} %get-tuple-element.52), channel_id=1, source_target_pairs={{0,14},{1,113},{2,0},{3,115},{4,2},{5,117},{6,4},{7,119},{8,6},{9,... | collective-permute-start | bytes 1032200 | tf_op jit(solution)/shard_map/ppermute | solution.py:219
  100.9 12.8 %collective-permute-start.18 = (bf16[24,7168]{1,0:T(8,128)(2,1)S(1)}, bf16[24,7168]{1,0:T(8,128)(2,1)S(1)}, u32[]{:S(2)}, u32[]{:S(2)}) collective-permute-start(bf16[24,7168]{1,0:T(8,128)(2,1)S(1)} %get-tuple-element.53), channel_id=1, source_target_pairs={{0,2},{1,17},{2,4},{3,19},{4,6},{5,21},{6,8},{7,23},{8,10},{9,25},... | collective-permute-start | bytes 1032200 | tf_op jit(solution)/shard_map/ppermute | solution.py:219
  100.9 14.7 %collective-permute-start.19 = (bf16[24,7168]{1,0:T(8,128)(2,1)S(1)}, bf16[24,7168]{1,0:T(8,128)(2,1)S(1)}, u32[]{:S(2)}, u32[]{:S(2)}) collective-permute-start(bf16[24,7168]{1,0:T(8,128)(2,1)S(1)} %get-tuple-element.54), channel_id=1, source_target_pairs={{0,12},{1,97},{2,14},{3,99},{4,0},{5,101},{6,2},{7,103},{8,4},{9,1... | collective-permute-start | bytes 1032200 | tf_op jit(solution)/shard_map/ppermute | solution.py:219
  102.5 13.1 %collective-permute-start.20 = (bf16[24,7168]{1,0:T(8,128)(2,1)S(1)}, bf16[24,7168]{1,0:T(8,128)(2,1)S(1)}, u32[]{:S(2)}, u32[]{:S(2)}) collective-permute-start(bf16[24,7168]{1,0:T(8,128)(2,1)S(1)} %get-tuple-element.55), channel_id=1, source_target_pairs={{0,4},{1,33},{2,6},{3,35},{4,8},{5,37},{6,10},{7,39},{8,12},{9,41}... | collective-permute-start | bytes 1032200 | tf_op jit(solution)/shard_map/ppermute | solution.py:219
  105.0 24.7 %collective-permute-start.21 = (bf16[24,7168]{1,0:T(8,128)(2,1)S(1)}, bf16[24,7168]{1,0:T(8,128)(2,1)S(1)}, u32[]{:S(2)}, u32[]{:S(2)}) collective-permute-start(bf16[24,7168]{1,0:T(8,128)(2,1)S(1)} %get-tuple-element.56), channel_id=1, source_target_pairs={{0,10},{1,81},{2,12},{3,83},{4,14},{5,85},{6,0},{7,87},{8,2},{9,89... | collective-permute-start | bytes 1032200 | tf_op jit(solution)/shard_map/ppermute | solution.py:219
  107.2 22.6 %collective-permute-start.22 = (bf16[24,7168]{1,0:T(8,128)(2,1)S(1)}, bf16[24,7168]{1,0:T(8,128)(2,1)S(1)}, u32[]{:S(2)}, u32[]{:S(2)}) collective-permute-start(bf16[24,7168]{1,0:T(8,128)(2,1)S(1)} %get-tuple-element.57), channel_id=1, source_target_pairs={{0,6},{1,49},{2,8},{3,51},{4,10},{5,53},{6,12},{7,55},{8,14},{9,57... | collective-permute-start | bytes 1032200 | tf_op jit(solution)/shard_map/ppermute | solution.py:219
  113.7 28.3 %collective-permute-start.23 = (bf16[24,7168]{1,0:T(8,128)(2,1)S(1)}, bf16[24,7168]{1,0:T(8,128)(2,1)S(1)}, u32[]{:S(2)}, u32[]{:S(2)}) collective-permute-start(bf16[24,7168]{1,0:T(8,128)(2,1)S(1)} %get-tuple-element.58), channel_id=1, source_target_pairs={{0,8},{1,65},{2,10},{3,67},{4,12},{5,69},{6,14},{7,71},{8,0},{9,73... | collective-permute-start | bytes 1032200 | tf_op jit(solution)/shard_map/ppermute | solution.py:219
  142.9 6.1 %collective-permute-start.24 = (bf16[8,7168]{1,0:T(8,128)(2,1)S(1)}, bf16[8,7168]{1,0:T(8,128)(2,1)S(1)}, u32[]{:S(2)}, u32[]{:S(2)}) collective-permute-start(bf16[8,7168]{1,0:T(8,128)(2,1)S(1)} %get-tuple-element.60), channel_id=1, source_target_pairs={{0,112},{1,15},{2,114},{3,1},{4,116},{5,3},{6,118},{7,5},{8,120},{... | collective-permute-start | bytes 344072 | tf_op jit(solution)/shard_map/ppermute | solution.py:219
  143.0 8.8 %collective-permute-start.25 = (bf16[8,7168]{1,0:T(8,128)(2,1)S(1)}, bf16[8,7168]{1,0:T(8,128)(2,1)S(1)}, u32[]{:S(2)}, u32[]{:S(2)}) collective-permute-start(bf16[8,7168]{1,0:T(8,128)(2,1)S(1)} %get-tuple-element.61), channel_id=1, source_target_pairs={{0,16},{1,3},{2,18},{3,5},{4,20},{5,7},{6,22},{7,9},{8,24},{9,11},... | collective-permute-start | bytes 344072 | tf_op jit(solution)/shard_map/ppermute | solution.py:219
  145.0 9.0 %collective-permute-start.26 = (bf16[8,7168]{1,0:T(8,128)(2,1)S(1)}, bf16[8,7168]{1,0:T(8,128)(2,1)S(1)}, u32[]{:S(2)}, u32[]{:S(2)}) collective-permute-start(bf16[8,7168]{1,0:T(8,128)(2,1)S(1)} %get-tuple-element.62), channel_id=1, source_target_pairs={{0,96},{1,13},{2,98},{3,15},{4,100},{5,1},{6,102},{7,3},{8,104},{9... | collective-permute-start | bytes 344072 | tf_op jit(solution)/shard_map/ppermute | solution.py:219
  145.0 9.0 %collective-permute-start.27 = (bf16[8,7168]{1,0:T(8,128)(2,1)S(1)}, bf16[8,7168]{1,0:T(8,128)(2,1)S(1)}, u32[]{:S(2)}, u32[]{:S(2)}) collective-permute-start(bf16[8,7168]{1,0:T(8,128)(2,1)S(1)} %get-tuple-element.63), channel_id=1, source_target_pairs={{0,32},{1,5},{2,34},{3,7},{4,36},{5,9},{6,38},{7,11},{8,40},{9,13}... | collective-permute-start | bytes 344072 | tf_op jit(solution)/shard_map/ppermute | solution.py:219
  147.9 7.2 %collective-permute-start.28 = (bf16[8,7168]{1,0:T(8,128)(2,1)S(1)}, bf16[8,7168]{1,0:T(8,128)(2,1)S(1)}, u32[]{:S(2)}, u32[]{:S(2)}) collective-permute-start(bf16[8,7168]{1,0:T(8,128)(2,1)S(1)} %get-tuple-element.64), channel_id=1, source_target_pairs={{0,80},{1,11},{2,82},{3,13},{4,84},{5,15},{6,86},{7,1},{8,88},{9,3... | collective-permute-start | bytes 344072 | tf_op jit(solution)/shard_map/ppermute | solution.py:219
  148.9 9.9 %collective-permute-start.29 = (bf16[8,7168]{1,0:T(8,128)(2,1)S(1)}, bf16[8,7168]{1,0:T(8,128)(2,1)S(1)}, u32[]{:S(2)}, u32[]{:S(2)}) collective-permute-start(bf16[8,7168]{1,0:T(8,128)(2,1)S(1)} %get-tuple-element.65), channel_id=1, source_target_pairs={{0,48},{1,7},{2,50},{3,9},{4,52},{5,11},{6,54},{7,13},{8,56},{9,15... | collective-permute-start | bytes 344072 | tf_op jit(solution)/shard_map/ppermute | solution.py:219
  151.8 9.3 %collective-permute-start.30 = (bf16[8,7168]{1,0:T(8,128)(2,1)S(1)}, bf16[8,7168]{1,0:T(8,128)(2,1)S(1)}, u32[]{:S(2)}, u32[]{:S(2)}) collective-permute-start(bf16[8,7168]{1,0:T(8,128)(2,1)S(1)} %get-tuple-element.66), channel_id=1, source_target_pairs={{0,64},{1,9},{2,66},{3,11},{4,68},{5,13},{6,70},{7,15},{8,72},{9,1... | collective-permute-start | bytes 344072 | tf_op jit(solution)/shard_map/ppermute | solution.py:219

commit v5 on v4

--- a/solution.py
+++ b/solution.py
@@ -156,9 +156,9 @@
         copy.wait()
 
 
-def expert_kernel(*refs, side):
-    arrived, held, outs = refs[:side], refs[side : side + 6], refs[side + 6 : 2 * side + 6]
-    acc_ref, h_ref, x_ref = refs[2 * side + 6 :]
+def expert_kernel(*refs, count):
+    arrived, held, outs = refs[:count], refs[count : count + 6], refs[count + 6 : 2 * count + 6]
+    acc_ref, h_ref, x_ref = refs[2 * count + 6 :]
     part = held[0].shape[2]
     gathered(x_ref, arrived)
     for n in range(4):
@@ -212,19 +212,17 @@
     each = slots // side
 
 
-    def crossed(rows, stage, sign):
-        moved = [rows[0]]
-        for n in range(1, side):
-            pairs = route_pairs(side, sign * order[n], stage)
-            moved.append(lax.ppermute(rows[n], GROUP, pairs))
-        return moved
+    def crossed(rows, n, stage, sign):
+        if not n:
+            return rows
+        return lax.ppermute(rows, GROUP, route_pairs(side, sign * order[n], stage))
 
     rows = call(
         pack_kernel,
         [(tokens, PLAIN), (expert_ids, PLAIN), (route_levels, PLAIN)],
         [((mine, width + INFO), bf16, V)],
     )
-    rows = crossed([rows] * side, 0, 1)
+    rows = [crossed(rows, n, 0, 1) for n in range(side)]
 
     gate_peer, up_peer, down_peer = (
         lax.ppermute(w, "sub", [(0, 1), (1, 0)]) for w in (gate_proj, up_proj, down_proj)
@@ -236,28 +234,37 @@
         [((each, width), bf16, V)] * side + [((3 * toks, slots), bf16, V)],
         [V((toks, width + INFO), bf16)],
     )
-    rows = crossed(rows, 1, 1)
-    weights = [gate_proj, gate_peer, up_proj, up_peer, down_proj, down_peer]
-    weights = call(
+    rows = [crossed(r, n, 1, 1) for n, r in enumerate(rows)]
+    gate, up, down = call(
         load_kernel,
-        [(w, A) for w in weights],
-        [(w.shape, bf16, V) for w in weights],
-        [pltpu.SemaphoreType.DMA((len(weights),))],
-    )
-    rows = call(
-        functools.partial(expert_kernel, side=side),
-        [(r, V) for r in rows] + [(w, V) for w in weights],
-        [((each, width), bf16, V)] * side,
-        [V((slots, 4 * part), f32), V((slots, 2 * part), bf16), V((slots, width), bf16)],
-    )
-    rows = crossed(rows, 1, -1)
+        [(w, A) for w in (gate_proj, up_proj, down_proj)],
+        [(w.shape, bf16, V) for w in (gate_proj, up_proj, down_proj)],
+        [pltpu.SemaphoreType.DMA((3,))],
+    )
+
+    near = side // 2 + 1
+    for blocks_here in (range(near, side), range(near)):
+        count = len(blocks_here)
+        done = call(
+            functools.partial(expert_kernel, count=count),
+            [(rows[n], V) for n in blocks_here]
+            + [(w, V) for w in (gate, gate_peer, up, up_peer, down, down_peer)],
+            [((each, width), bf16, V)] * count,
+            [
+                V((count * each, 4 * part), f32),
+                V((count * each, 2 * part), bf16),
+                V((count * each, width), bf16),
+            ],
+        )
+        for n, block in zip(blocks_here, done):
+            rows[n] = crossed(block, n, 1, -1)
     rows = call(
         functools.partial(mix_kernel, side=side),
         [(mix, V)] + [(r, V) for r in rows],
         [((mine, width), bf16, V)] * side,
         [V((slots, width), bf16)],
     )
-    rows = crossed(rows, 0, -1)
+    rows = [crossed(r, n, 0, -1) for n, r in enumerate(rows)]
     return call(sum_kernel, [(r, V) for r in rows], [((mine, width), bf16, PLAIN)])
 
 

time: 162 us -> 165 us (1.019)
  the two profiles are of different devices: /device:TPU:516 before, /device:TPU:514 now
where the time goes in v5:
time: 165 us; the launch traced here: 163 us
  starting transfers between devices  78.9 us (48%)
  waiting for transfers between devices  59.1 us (36%)
  Pallas kernels  23.9 us (14%)
    ppermute x28, starting transfers between devices, crossed(): return lax.ppermute(rows, GROUP, route_pairs(side, sign * order[n], stage))  78.4 us
    ppermute x28, waiting for transfers between devices, crossed(): return lax.ppermute(rows, GROUP, route_pairs(side, sign * order[n], stage))  59.1 us
    pallas_call x7, Pallas kernels, call(): pl.pallas_call(kernel, in_specs=[pl.BlockSpec(memory_space=V if space is...  23.9 us
  transfers between devices with their start and end apart: 31, of which 14 were waited for; matrix products, arithmetic and copies ran while one was open for 0% of the time, Pallas kernels for 14%

profile of v5, /device:TPU:514, one launch (start us, length us, event | category | flops | bytes accessed | tf_op | source)
XLA Modules:
  0.0 162.7 jit_solution(5561239822311960542)
XLA Ops:
  0.0 0.0 collective-permute-start.11
  0.0 0.5 collective-permute-start.12
  0.5 0.9 shard_map.73.refs_0_
  1.4 10.7 %collective-permute-start.6 = (bf16[8,7424]{1,0:T(8,128)(2,1)S(1)}, bf16[8,7424]{1,0:T(8,128)(2,1)S(1)}, u32[]{:S(2)}, u32[]{:S(2)}) collective-permute-start(bf16[8,7424]{1,0:T(8,128)(2,1)S(1)} %shard_map.73.refs_0_), channel_id=1, source_target_pairs={{0,64},{1,9},{2,66},{3,11},{4,68},{5,13},{6,70},{7,15},{8,72},{9,1... | collective-permute-start | bytes 356360 | tf_op jit(solution)/shard_map/ppermute | solution.py:218
  12.2 0.6 collective-permute-start.5
  12.7 3.1 %collective-permute-done.6.refs_7_ = bf16[8,7424]{1,0:T(8,128)(2,1)S(1)} collective-permute-done((bf16[8,7424]{1,0:T(8,128)(2,1)S(1)}, bf16[8,7424]{1,0:T(8,128)(2,1)S(1)}, u32[]{:S(2)}, u32[]{:S(2)}) %collective-permute-start.6) | collective-permute-done | bytes 118816 | tf_op jit(solution)/shard_map/ppermute | solution.py:218
  15.9 3.7 %collective-permute-start.4 = (bf16[8,7424]{1,0:T(8,128)(2,1)S(1)}, bf16[8,7424]{1,0:T(8,128)(2,1)S(1)}, u32[]{:S(2)}, u32[]{:S(2)}) collective-permute-start(bf16[8,7424]{1,0:T(8,128)(2,1)S(1)} %shard_map.73.refs_0_), channel_id=1, source_target_pairs={{0,48},{1,7},{2,50},{3,9},{4,52},{5,11},{6,54},{7,13},{8,56},{9,15... | collective-permute-start | bytes 356360 | tf_op jit(solution)/shard_map/ppermute | solution.py:218
  19.5 3.9 %collective-permute-done.5.refs_6_ = bf16[8,7424]{1,0:T(8,128)(2,1)S(1)} collective-permute-done((bf16[8,7424]{1,0:T(8,128)(2,1)S(1)}, bf16[8,7424]{1,0:T(8,128)(2,1)S(1)}, u32[]{:S(2)}, u32[]{:S(2)}) %collective-permute-start.5) | collective-permute-done | bytes 118816 | tf_op jit(solution)/shard_map/ppermute | solution.py:218
  23.4 1.0 collective-permute-start.3
  24.5 0.0 collective-permute-done.4.refs_5_
  24.5 4.8 %collective-permute-start.2 = (bf16[8,7424]{1,0:T(8,128)(2,1)S(1)}, bf16[8,7424]{1,0:T(8,128)(2,1)S(1)}, u32[]{:S(2)}, u32[]{:S(2)}) collective-permute-start(bf16[8,7424]{1,0:T(8,128)(2,1)S(1)} %shard_map.73.refs_0_), channel_id=1, source_target_pairs={{0,32},{1,5},{2,34},{3,7},{4,36},{5,9},{6,38},{7,11},{8,40},{9,13}... | collective-permute-start | bytes 356360 | tf_op jit(solution)/shard_map/ppermute | solution.py:218
  29.3 0.1 collective-permute-done.3.refs_4_
  29.4 3.4 %collective-permute-start.1 = (bf16[8,7424]{1,0:T(8,128)(2,1)S(1)}, bf16[8,7424]{1,0:T(8,128)(2,1)S(1)}, u32[]{:S(2)}, u32[]{:S(2)}) collective-permute-start(bf16[8,7424]{1,0:T(8,128)(2,1)S(1)} %shard_map.73.refs_0_), channel_id=1, source_target_pairs={{0,112},{1,15},{2,114},{3,1},{4,116},{5,3},{6,118},{7,5},{8,120},{... | collective-permute-start | bytes 356360 | tf_op jit(solution)/shard_map/ppermute | solution.py:218
  32.8 3.4 %collective-permute-done.2.refs_3_ = bf16[8,7424]{1,0:T(8,128)(2,1)S(1)} collective-permute-done((bf16[8,7424]{1,0:T(8,128)(2,1)S(1)}, bf16[8,7424]{1,0:T(8,128)(2,1)S(1)}, u32[]{:S(2)}, u32[]{:S(2)}) %collective-permute-start.2) | collective-permute-done | bytes 118816 | tf_op jit(solution)/shard_map/ppermute | solution.py:218
  36.2 0.7 broadcast_select_fusion.experts_ref
  36.9 5.4 %collective-permute-done.refs_1_ = bf16[8,7424]{1,0:T(8,128)(2,1)S(1)} collective-permute-done((bf16[8,7424]{1,0:T(8,128)(2,1)S(1)}, bf16[8,7424]{1,0:T(8,128)(2,1)S(1)}, u32[]{:S(2)}, u32[]{:S(2)}) %collective-permute-start) | collective-permute-done | bytes 118816 | tf_op jit(solution)/shard_map/ppermute | solution.py:218
  42.2 1.6 shard_map.74
  43.8 1.7 %collective-permute-start.7 = (bf16[24,7168]{1,0:T(8,128)(2,1)S(1)}, bf16[24,7168]{1,0:T(8,128)(2,1)S(1)}, u32[]{:S(2)}, u32[]{:S(2)}) collective-permute-start(bf16[24,7168]{1,0:T(8,128)(2,1)S(1)} %get-tuple-element.35), channel_id=1, source_target_pairs={{0,2},{1,17},{2,4},{3,19},{4,6},{5,21},{6,8},{7,23},{8,10},{9,25},... | collective-permute-start | bytes 1032200 | tf_op jit(solution)/shard_map/ppermute | solution.py:218
  45.6 10.2 %collective-permute-start.8 = (bf16[24,7168]{1,0:T(8,128)(2,1)S(1)}, bf16[24,7168]{1,0:T(8,128)(2,1)S(1)}, u32[]{:S(2)}, u32[]{:S(2)}) collective-permute-start(bf16[24,7168]{1,0:T(8,128)(2,1)S(1)} %get-tuple-element.36), channel_id=1, source_target_pairs={{0,14},{1,113},{2,0},{3,115},{4,2},{5,117},{6,4},{7,119},{8,6},{9,... | collective-permute-start | bytes 1032200 | tf_op jit(solution)/shard_map/ppermute | solution.py:218
  55.7 5.1 %collective-permute-done.7.refs_1_ = bf16[24,7168]{1,0:T(8,128)(2,1)S(1)} collective-permute-done((bf16[24,7168]{1,0:T(8,128)(2,1)S(1)}, bf16[24,7168]{1,0:T(8,128)(2,1)S(1)}, u32[]{:S(2)}, u32[]{:S(2)}) %collective-permute-start.7) | collective-permute-done | bytes 344096 | tf_op jit(solution)/shard_map/ppermute | solution.py:218
  60.8 5.9 %collective-permute-start.10 = (bf16[24,7168]{1,0:T(8,128)(2,1)S(1)}, bf16[24,7168]{1,0:T(8,128)(2,1)S(1)}, u32[]{:S(2)}, u32[]{:S(2)}) collective-permute-start(bf16[24,7168]{1,0:T(8,128)(2,1)S(1)} %get-tuple-element.38), channel_id=1, source_target_pairs={{0,12},{1,97},{2,14},{3,99},{4,0},{5,101},{6,2},{7,103},{8,4},{9,1... | collective-permute-start | bytes 1032200 | tf_op jit(solution)/shard_map/ppermute | solution.py:218
  66.7 4.2 %shard_map.75 = (bf16[1,7168,256]{2,1,0:T(8,128)(2,1)S(1)}, bf16[1,7168,256]{2,1,0:T(8,128)(2,1)S(1)}, bf16[1,256,7168]{2,1,0:T(8,128)(2,1)S(1)}) custom-call(bf16[1,7168,256]{2,1,0:T(8,128)(2,1)} %refs_0_.1, bf16[1,7168,256]{2,1,0:T(8,128)(2,1)} %refs_1_.1, bf16[1,256,7168]{2,1,0:T(8,128)(2,1)} %refs_2_.1), custom_call_target="tpu_custom_call" | custom-call | tf_op jit(solution)/shard_map/pallas_call | solution.py:52
  71.0 0.3 collective-permute-start.18
  71.3 3.8 %collective-permute-done.10.refs_4_ = bf16[24,7168]{1,0:T(8,128)(2,1)S(1)} collective-permute-done((bf16[24,7168]{1,0:T(8,128)(2,1)S(1)}, bf16[24,7168]{1,0:T(8,128)(2,1)S(1)}, u32[]{:S(2)}, u32[]{:S(2)}) %collective-permute-start.10) | collective-permute-done | bytes 344096 | tf_op jit(solution)/shard_map/ppermute | solution.py:218
  75.1 3.7 %collective-permute-start.19 = (bf16[24,7168]{1,0:T(8,128)(2,1)S(1)}, bf16[24,7168]{1,0:T(8,128)(2,1)S(1)}, u32[]{:S(2)}, u32[]{:S(2)}) collective-permute-start(bf16[24,7168]{1,0:T(8,128)(2,1)S(1)} %get-tuple-element.48), channel_id=1, source_target_pairs={{0,10},{1,81},{2,12},{3,83},{4,14},{5,85},{6,0},{7,87},{8,2},{9,89... | collective-permute-start | bytes 1032200 | tf_op jit(solution)/shard_map/ppermute | solution.py:218
  78.8 0.7 collective-permute-start.20
  79.5 7.3 %shard_map.76 = (bf16[24,7168]{1,0:T(8,128)(2,1)S(1)}, bf16[24,7168]{1,0:T(8,128)(2,1)S(1)}, bf16[24,7168]{1,0:T(8,128)(2,1)S(1)}, bf16[24,7168]{1,0:T(8,128)(2,1)S(1)}, bf16[24,7168]{1,0:T(8,128)(2,1)S(1)}) custom-call(bf16[24,7168]{1,0:T(8,128)(2,1)S(1)} %get-tuple-element.34.refs_0_, bf16[24,7168]{1,0:T(8,128)(2,1)S(1)} %collective-permute-done.7.refs_1_, ...), custom_call_target="tpu_custom_call" | custom-call | tf_op jit(solution)/shard_map/pallas_call | solution.py:52
  86.8 2.3 %collective-permute-start.14 = (bf16[24,7168]{1,0:T(8,128)(2,1)S(1)}, bf16[24,7168]{1,0:T(8,128)(2,1)S(1)}, u32[]{:S(2)}, u32[]{:S(2)}) collective-permute-start(bf16[24,7168]{1,0:T(8,128)(2,1)S(1)} %get-tuple-element.43), channel_id=1, source_target_pairs={{0,14},{1,113},{2,0},{3,115},{4,2},{5,117},{6,4},{7,119},{8,6},{9,... | collective-permute-start | bytes 1032200 | tf_op jit(solution)/shard_map/ppermute | solution.py:218
  89.1 8.3 %collective-permute-start.16 = (bf16[24,7168]{1,0:T(8,128)(2,1)S(1)}, bf16[24,7168]{1,0:T(8,128)(2,1)S(1)}, u32[]{:S(2)}, u32[]{:S(2)}) collective-permute-start(bf16[24,7168]{1,0:T(8,128)(2,1)S(1)} %get-tuple-element.45), channel_id=1, source_target_pairs={{0,12},{1,97},{2,14},{3,99},{4,0},{5,101},{6,2},{7,103},{8,4},{9,1... | collective-permute-start | bytes 1032200 | tf_op jit(solution)/shard_map/ppermute | solution.py:218
  97.4 1.9 %collective-permute-done.20.refs_2_ = bf16[24,7168]{1,0:T(8,128)(2,1)S(1)} collective-permute-done((bf16[24,7168]{1,0:T(8,128)(2,1)S(1)}, bf16[24,7168]{1,0:T(8,128)(2,1)S(1)}, u32[]{:S(2)}, u32[]{:S(2)}) %collective-permute-start.20) | collective-permute-done | bytes 344096 | tf_op jit(solution)/shard_map/ppermute | solution.py:218
  99.4 8.2 %shard_map.77 = (bf16[24,7168]{1,0:T(8,128)(2,1)S(1)}, bf16[24,7168]{1,0:T(8,128)(2,1)S(1)}, bf16[24,7168]{1,0:T(8,128)(2,1)S(1)}) custom-call(bf16[24,7168]{1,0:T(8,128)(2,1)S(1)} %collective-permute-done.18.refs_0_, bf16[24,7168]{1,0:T(8,128)(2,1)S(1)} %collective-permute-done.19.refs_1_, bf16[24,7168]{1,0:T(8,128)(2,1)S(1)} %collective-permute-done.20.refs_2_, ...), custom_call_target="tpu_custom_call" | custom-call | tf_op jit(solution)/shard_map/pallas_call | solution.py:52
  107.5 3.9 %collective-permute-start.21 = (bf16[24,7168]{1,0:T(8,128)(2,1)S(1)}, bf16[24,7168]{1,0:T(8,128)(2,1)S(1)}, u32[]{:S(2)}, u32[]{:S(2)}) collective-permute-start(bf16[24,7168]{1,0:T(8,128)(2,1)S(1)} %get-tuple-element.50), channel_id=1, source_target_pairs={{0,10},{1,81},{2,12},{3,83},{4,14},{5,85},{6,0},{7,87},{8,2},{9,89... | collective-permute-start | bytes 1032200 | tf_op jit(solution)/shard_map/ppermute | solution.py:218
  111.4 1.3 collective-permute-start.22
  112.7 5.1 %collective-permute-start.23 = (bf16[24,7168]{1,0:T(8,128)(2,1)S(1)}, bf16[24,7168]{1,0:T(8,128)(2,1)S(1)}, u32[]{:S(2)}, u32[]{:S(2)}) collective-permute-start(bf16[24,7168]{1,0:T(8,128)(2,1)S(1)} %get-tuple-element.52), channel_id=1, source_target_pairs={{0,8},{1,65},{2,10},{3,67},{4,12},{5,69},{6,14},{7,71},{8,0},{9,73... | collective-permute-start | bytes 1032200 | tf_op jit(solution)/shard_map/ppermute | solution.py:218
  117.8 0.3 collective-permute-done.21.refs_5_
  118.1 13.4 %collective-permute-done.22.refs_6_ = bf16[24,7168]{1,0:T(8,128)(2,1)S(1)} collective-permute-done((bf16[24,7168]{1,0:T(8,128)(2,1)S(1)}, bf16[24,7168]{1,0:T(8,128)(2,1)S(1)}, u32[]{:S(2)}, u32[]{:S(2)}) %collective-permute-start.22) | collective-permute-done | bytes 344096 | tf_op jit(solution)/shard_map/ppermute | solution.py:218
  131.5 12.0 %collective-permute-done.23.refs_7_ = bf16[24,7168]{1,0:T(8,128)(2,1)S(1)} collective-permute-done((bf16[24,7168]{1,0:T(8,128)(2,1)S(1)}, bf16[24,7168]{1,0:T(8,128)(2,1)S(1)}, u32[]{:S(2)}, u32[]{:S(2)}) %collective-permute-start.23) | collective-permute-done | bytes 344096 | tf_op jit(solution)/shard_map/ppermute | solution.py:218
  143.5 0.9 shard_map.78
  144.4 0.1 collective-permute-start.24
  144.5 2.0 %collective-permute-start.25 = (bf16[8,7168]{1,0:T(8,128)(2,1)S(1)}, bf16[8,7168]{1,0:T(8,128)(2,1)S(1)}, u32[]{:S(2)}, u32[]{:S(2)}) collective-permute-start(bf16[8,7168]{1,0:T(8,128)(2,1)S(1)} %get-tuple-element.55), channel_id=1, source_target_pairs={{0,16},{1,3},{2,18},{3,5},{4,20},{5,7},{6,22},{7,9},{8,24},{9,11},... | collective-permute-start | bytes 344072 | tf_op jit(solution)/shard_map/ppermute | solution.py:218
  146.5 2.9 %collective-permute-start.27 = (bf16[8,7168]{1,0:T(8,128)(2,1)S(1)}, bf16[8,7168]{1,0:T(8,128)(2,1)S(1)}, u32[]{:S(2)}, u32[]{:S(2)}) collective-permute-start(bf16[8,7168]{1,0:T(8,128)(2,1)S(1)} %get-tuple-element.57), channel_id=1, source_target_pairs={{0,32},{1,5},{2,34},{3,7},{4,36},{5,9},{6,38},{7,11},{8,40},{9,13}... | collective-permute-start | bytes 344072 | tf_op jit(solution)/shard_map/ppermute | solution.py:218
  149.4 0.8 collective-permute-start.28
  150.2 3.0 %collective-permute-start.29 = (bf16[8,7168]{1,0:T(8,128)(2,1)S(1)}, bf16[8,7168]{1,0:T(8,128)(2,1)S(1)}, u32[]{:S(2)}, u32[]{:S(2)}) collective-permute-start(bf16[8,7168]{1,0:T(8,128)(2,1)S(1)} %get-tuple-element.59), channel_id=1, source_target_pairs={{0,48},{1,7},{2,50},{3,9},{4,52},{5,11},{6,54},{7,13},{8,56},{9,15... | collective-permute-start | bytes 344072 | tf_op jit(solution)/shard_map/ppermute | solution.py:218
  153.3 2.0 %collective-permute-start.30 = (bf16[8,7168]{1,0:T(8,128)(2,1)S(1)}, bf16[8,7168]{1,0:T(8,128)(2,1)S(1)}, u32[]{:S(2)}, u32[]{:S(2)}) collective-permute-start(bf16[8,7168]{1,0:T(8,128)(2,1)S(1)} %get-tuple-element.60), channel_id=1, source_target_pairs={{0,64},{1,9},{2,66},{3,11},{4,68},{5,13},{6,70},{7,15},{8,72},{9,1... | collective-permute-start | bytes 344072 | tf_op jit(solution)/shard_map/ppermute | solution.py:218
  155.3 1.0 collective-permute-done.28.refs_5_
  156.2 4.4 %collective-permute-done.29.refs_6_ = bf16[8,7168]{1,0:T(8,128)(2,1)S(1)} collective-permute-done((bf16[8,7168]{1,0:T(8,128)(2,1)S(1)}, bf16[8,7168]{1,0:T(8,128)(2,1)S(1)}, u32[]{:S(2)}, u32[]{:S(2)}) %collective-permute-start.29) | collective-permute-done | bytes 114720 | tf_op jit(solution)/shard_map/ppermute | solution.py:218
  160.6 1.4 collective-permute-done.30.refs_7_
  162.0 0.8 shard_map.79
  (22 shorter events, 0.1 us)
Async XLA Ops:
  0.0 78.8 %collective-permute-start.11 = (bf16[1,7168,256]{2,1,0:T(8,128)(2,1)}, bf16[1,7168,256]{2,1,0:T(8,128)(2,1)}, u32[]{:S(2)}, u32[]{:S(2)}) collective-permute-start(bf16[1,7168,256]{2,1,0:T(8,128)(2,1)} %refs_0_.1), channel_id=1, source_target_pairs={{0,1},{1,0},{2,3},{3,2},{4,5},{5,4},{6,7},{7,6},{8,9},{9,8},{10,11... | collective-permute-start | bytes 11010056 | tf_op jit(solution)/shard_map/ppermute | solution.py:228
  0.0 79.5 %collective-permute-start.12 = (bf16[1,7168,256]{2,1,0:T(8,128)(2,1)}, bf16[1,7168,256]{2,1,0:T(8,128)(2,1)}, u32[]{:S(2)}, u32[]{:S(2)}) collective-permute-start(bf16[1,7168,256]{2,1,0:T(8,128)(2,1)} %refs_1_.1), channel_id=1, source_target_pairs={{0,1},{1,0},{2,3},{3,2},{4,5},{5,4},{6,7},{7,6},{8,9},{9,8},{10,11... | collective-permute-start | bytes 11010056 | tf_op jit(solution)/shard_map/ppermute | solution.py:228
  0.5 79.0 %collective-permute-start.13 = (bf16[1,256,7168]{2,1,0:T(8,128)(2,1)}, bf16[1,256,7168]{2,1,0:T(8,128)(2,1)}, u32[]{:S(2)}, u32[]{:S(2)}) collective-permute-start(bf16[1,256,7168]{2,1,0:T(8,128)(2,1)} %refs_2_.1), channel_id=1, source_target_pairs={{0,1},{1,0},{2,3},{3,2},{4,5},{5,4},{6,7},{7,6},{8,9},{9,8},{10,11... | collective-permute-start | bytes 11010056 | tf_op jit(solution)/shard_map/ppermute | solution.py:228
  1.4 14.4 %collective-permute-start.6 = (bf16[8,7424]{1,0:T(8,128)(2,1)S(1)}, bf16[8,7424]{1,0:T(8,128)(2,1)S(1)}, u32[]{:S(2)}, u32[]{:S(2)}) collective-permute-start(bf16[8,7424]{1,0:T(8,128)(2,1)S(1)} %shard_map.73.refs_0_), channel_id=1, source_target_pairs={{0,64},{1,9},{2,66},{3,11},{4,68},{5,13},{6,70},{7,15},{8,72},{9,1... | collective-permute-start | bytes 356360 | tf_op jit(solution)/shard_map/ppermute | solution.py:218
  12.2 11.2 %collective-permute-start.5 = (bf16[8,7424]{1,0:T(8,128)(2,1)S(1)}, bf16[8,7424]{1,0:T(8,128)(2,1)S(1)}, u32[]{:S(2)}, u32[]{:S(2)}) collective-permute-start(bf16[8,7424]{1,0:T(8,128)(2,1)S(1)} %shard_map.73.refs_0_), channel_id=1, source_target_pairs={{0,80},{1,11},{2,82},{3,13},{4,84},{5,15},{6,86},{7,1},{8,88},{9,3... | collective-permute-start | bytes 356360 | tf_op jit(solution)/shard_map/ppermute | solution.py:218
  15.9 8.7 %collective-permute-start.4 = (bf16[8,7424]{1,0:T(8,128)(2,1)S(1)}, bf16[8,7424]{1,0:T(8,128)(2,1)S(1)}, u32[]{:S(2)}, u32[]{:S(2)}) collective-permute-start(bf16[8,7424]{1,0:T(8,128)(2,1)S(1)} %shard_map.73.refs_0_), channel_id=1, source_target_pairs={{0,48},{1,7},{2,50},{3,9},{4,52},{5,11},{6,54},{7,13},{8,56},{9,15... | collective-permute-start | bytes 356360 | tf_op jit(solution)/shard_map/ppermute | solution.py:218
  23.4 5.9 %collective-permute-start.3 = (bf16[8,7424]{1,0:T(8,128)(2,1)S(1)}, bf16[8,7424]{1,0:T(8,128)(2,1)S(1)}, u32[]{:S(2)}, u32[]{:S(2)}) collective-permute-start(bf16[8,7424]{1,0:T(8,128)(2,1)S(1)} %shard_map.73.refs_0_), channel_id=1, source_target_pairs={{0,96},{1,13},{2,98},{3,15},{4,100},{5,1},{6,102},{7,3},{8,104},{9... | collective-permute-start | bytes 356360 | tf_op jit(solution)/shard_map/ppermute | solution.py:218
  24.5 11.7 %collective-permute-start.2 = (bf16[8,7424]{1,0:T(8,128)(2,1)S(1)}, bf16[8,7424]{1,0:T(8,128)(2,1)S(1)}, u32[]{:S(2)}, u32[]{:S(2)}) collective-permute-start(bf16[8,7424]{1,0:T(8,128)(2,1)S(1)} %shard_map.73.refs_0_), channel_id=1, source_target_pairs={{0,32},{1,5},{2,34},{3,7},{4,36},{5,9},{6,38},{7,11},{8,40},{9,13}... | collective-permute-start | bytes 356360 | tf_op jit(solution)/shard_map/ppermute | solution.py:218
  29.4 7.5 %collective-permute-start.1 = (bf16[8,7424]{1,0:T(8,128)(2,1)S(1)}, bf16[8,7424]{1,0:T(8,128)(2,1)S(1)}, u32[]{:S(2)}, u32[]{:S(2)}) collective-permute-start(bf16[8,7424]{1,0:T(8,128)(2,1)S(1)} %shard_map.73.refs_0_), channel_id=1, source_target_pairs={{0,112},{1,15},{2,114},{3,1},{4,116},{5,3},{6,118},{7,5},{8,120},{... | collective-permute-start | bytes 356360 | tf_op jit(solution)/shard_map/ppermute | solution.py:218
  36.2 6.0 %collective-permute-start = (bf16[8,7424]{1,0:T(8,128)(2,1)S(1)}, bf16[8,7424]{1,0:T(8,128)(2,1)S(1)}, u32[]{:S(2)}, u32[]{:S(2)}) collective-permute-start(bf16[8,7424]{1,0:T(8,128)(2,1)S(1)} %shard_map.73.refs_0_), channel_id=1, source_target_pairs={{0,16},{1,3},{2,18},{3,5},{4,20},{5,7},{6,22},{7,9},{8,24},{9,11},... | collective-permute-start | bytes 356360 | tf_op jit(solution)/shard_map/ppermute | solution.py:218
  43.8 17.0 %collective-permute-start.7 = (bf16[24,7168]{1,0:T(8,128)(2,1)S(1)}, bf16[24,7168]{1,0:T(8,128)(2,1)S(1)}, u32[]{:S(2)}, u32[]{:S(2)}) collective-permute-start(bf16[24,7168]{1,0:T(8,128)(2,1)S(1)} %get-tuple-element.35), channel_id=1, source_target_pairs={{0,2},{1,17},{2,4},{3,19},{4,6},{5,21},{6,8},{7,23},{8,10},{9,25},... | collective-permute-start | bytes 1032200 | tf_op jit(solution)/shard_map/ppermute | solution.py:218
  45.6 15.3 %collective-permute-start.8 = (bf16[24,7168]{1,0:T(8,128)(2,1)S(1)}, bf16[24,7168]{1,0:T(8,128)(2,1)S(1)}, u32[]{:S(2)}, u32[]{:S(2)}) collective-permute-start(bf16[24,7168]{1,0:T(8,128)(2,1)S(1)} %get-tuple-element.36), channel_id=1, source_target_pairs={{0,14},{1,113},{2,0},{3,115},{4,2},{5,117},{6,4},{7,119},{8,6},{9,... | collective-permute-start | bytes 1032200 | tf_op jit(solution)/shard_map/ppermute | solution.py:218
  60.8 10.1 %collective-permute-start.9 = (bf16[24,7168]{1,0:T(8,128)(2,1)S(1)}, bf16[24,7168]{1,0:T(8,128)(2,1)S(1)}, u32[]{:S(2)}, u32[]{:S(2)}) collective-permute-start(bf16[24,7168]{1,0:T(8,128)(2,1)S(1)} %get-tuple-element.37), channel_id=1, source_target_pairs={{0,4},{1,33},{2,6},{3,35},{4,8},{5,37},{6,10},{7,39},{8,12},{9,41}... | collective-permute-start | bytes 1032200 | tf_op jit(solution)/shard_map/ppermute | solution.py:218
  60.8 14.3 %collective-permute-start.10 = (bf16[24,7168]{1,0:T(8,128)(2,1)S(1)}, bf16[24,7168]{1,0:T(8,128)(2,1)S(1)}, u32[]{:S(2)}, u32[]{:S(2)}) collective-permute-start(bf16[24,7168]{1,0:T(8,128)(2,1)S(1)} %get-tuple-element.38), channel_id=1, source_target_pairs={{0,12},{1,97},{2,14},{3,99},{4,0},{5,101},{6,2},{7,103},{8,4},{9,1... | collective-permute-start | bytes 1032200 | tf_op jit(solution)/shard_map/ppermute | solution.py:218
  71.0 18.1 %collective-permute-start.18 = (bf16[24,7168]{1,0:T(8,128)(2,1)S(1)}, bf16[24,7168]{1,0:T(8,128)(2,1)S(1)}, u32[]{:S(2)}, u32[]{:S(2)}) collective-permute-start(bf16[24,7168]{1,0:T(8,128)(2,1)S(1)} %get-tuple-element.47), channel_id=1, source_target_pairs={{0,6},{1,49},{2,8},{3,51},{4,10},{5,53},{6,12},{7,55},{8,14},{9,57... | collective-permute-start | bytes 1032200 | tf_op jit(solution)/shard_map/ppermute | solution.py:218
  75.1 22.3 %collective-permute-start.19 = (bf16[24,7168]{1,0:T(8,128)(2,1)S(1)}, bf16[24,7168]{1,0:T(8,128)(2,1)S(1)}, u32[]{:S(2)}, u32[]{:S(2)}) collective-permute-start(bf16[24,7168]{1,0:T(8,128)(2,1)S(1)} %get-tuple-element.48), channel_id=1, source_target_pairs={{0,10},{1,81},{2,12},{3,83},{4,14},{5,85},{6,0},{7,87},{8,2},{9,89... | collective-permute-start | bytes 1032200 | tf_op jit(solution)/shard_map/ppermute | solution.py:218
  78.8 20.6 %collective-permute-start.20 = (bf16[24,7168]{1,0:T(8,128)(2,1)S(1)}, bf16[24,7168]{1,0:T(8,128)(2,1)S(1)}, u32[]{:S(2)}, u32[]{:S(2)}) collective-permute-start(bf16[24,7168]{1,0:T(8,128)(2,1)S(1)} %get-tuple-element.49), channel_id=1, source_target_pairs={{0,8},{1,65},{2,10},{3,67},{4,12},{5,69},{6,14},{7,71},{8,0},{9,73... | collective-permute-start | bytes 1032200 | tf_op jit(solution)/shard_map/ppermute | solution.py:218
  86.8 24.6 %collective-permute-start.14 = (bf16[24,7168]{1,0:T(8,128)(2,1)S(1)}, bf16[24,7168]{1,0:T(8,128)(2,1)S(1)}, u32[]{:S(2)}, u32[]{:S(2)}) collective-permute-start(bf16[24,7168]{1,0:T(8,128)(2,1)S(1)} %get-tuple-element.43), channel_id=1, source_target_pairs={{0,14},{1,113},{2,0},{3,115},{4,2},{5,117},{6,4},{7,119},{8,6},{9,... | collective-permute-start | bytes 1032200 | tf_op jit(solution)/shard_map/ppermute | solution.py:218
  89.1 23.6 %collective-permute-start.15 = (bf16[24,7168]{1,0:T(8,128)(2,1)S(1)}, bf16[24,7168]{1,0:T(8,128)(2,1)S(1)}, u32[]{:S(2)}, u32[]{:S(2)}) collective-permute-start(bf16[24,7168]{1,0:T(8,128)(2,1)S(1)} %get-tuple-element.44), channel_id=1, source_target_pairs={{0,2},{1,17},{2,4},{3,19},{4,6},{5,21},{6,8},{7,23},{8,10},{9,25},... | collective-permute-start | bytes 1032200 | tf_op jit(solution)/shard_map/ppermute | solution.py:218
  89.1 28.7 %collective-permute-start.16 = (bf16[24,7168]{1,0:T(8,128)(2,1)S(1)}, bf16[24,7168]{1,0:T(8,128)(2,1)S(1)}, u32[]{:S(2)}, u32[]{:S(2)}) collective-permute-start(bf16[24,7168]{1,0:T(8,128)(2,1)S(1)} %get-tuple-element.45), channel_id=1, source_target_pairs={{0,12},{1,97},{2,14},{3,99},{4,0},{5,101},{6,2},{7,103},{8,4},{9,1... | collective-permute-start | bytes 1032200 | tf_op jit(solution)/shard_map/ppermute | solution.py:218
  97.4 20.4 %collective-permute-start.17 = (bf16[24,7168]{1,0:T(8,128)(2,1)S(1)}, bf16[24,7168]{1,0:T(8,128)(2,1)S(1)}, u32[]{:S(2)}, u32[]{:S(2)}) collective-permute-start(bf16[24,7168]{1,0:T(8,128)(2,1)S(1)} %get-tuple-element.46), channel_id=1, source_target_pairs={{0,4},{1,33},{2,6},{3,35},{4,8},{5,37},{6,10},{7,39},{8,12},{9,41}... | collective-permute-start | bytes 1032200 | tf_op jit(solution)/shard_map/ppermute | solution.py:218
  107.5 10.6 %collective-permute-start.21 = (bf16[24,7168]{1,0:T(8,128)(2,1)S(1)}, bf16[24,7168]{1,0:T(8,128)(2,1)S(1)}, u32[]{:S(2)}, u32[]{:S(2)}) collective-permute-start(bf16[24,7168]{1,0:T(8,128)(2,1)S(1)} %get-tuple-element.50), channel_id=1, source_target_pairs={{0,10},{1,81},{2,12},{3,83},{4,14},{5,85},{6,0},{7,87},{8,2},{9,89... | collective-permute-start | bytes 1032200 | tf_op jit(solution)/shard_map/ppermute | solution.py:218
  111.4 20.1 %collective-permute-start.22 = (bf16[24,7168]{1,0:T(8,128)(2,1)S(1)}, bf16[24,7168]{1,0:T(8,128)(2,1)S(1)}, u32[]{:S(2)}, u32[]{:S(2)}) collective-permute-start(bf16[24,7168]{1,0:T(8,128)(2,1)S(1)} %get-tuple-element.51), channel_id=1, source_target_pairs={{0,6},{1,49},{2,8},{3,51},{4,10},{5,53},{6,12},{7,55},{8,14},{9,57... | collective-permute-start | bytes 1032200 | tf_op jit(solution)/shard_map/ppermute | solution.py:218
  112.7 30.8 %collective-permute-start.23 = (bf16[24,7168]{1,0:T(8,128)(2,1)S(1)}, bf16[24,7168]{1,0:T(8,128)(2,1)S(1)}, u32[]{:S(2)}, u32[]{:S(2)}) collective-permute-start(bf16[24,7168]{1,0:T(8,128)(2,1)S(1)} %get-tuple-element.52), channel_id=1, source_target_pairs={{0,8},{1,65},{2,10},{3,67},{4,12},{5,69},{6,14},{7,71},{8,0},{9,73... | collective-permute-start | bytes 1032200 | tf_op jit(solution)/shard_map/ppermute | solution.py:218
  144.4 5.9 %collective-permute-start.24 = (bf16[8,7168]{1,0:T(8,128)(2,1)S(1)}, bf16[8,7168]{1,0:T(8,128)(2,1)S(1)}, u32[]{:S(2)}, u32[]{:S(2)}) collective-permute-start(bf16[8,7168]{1,0:T(8,128)(2,1)S(1)} %get-tuple-element.54), channel_id=1, source_target_pairs={{0,112},{1,15},{2,114},{3,1},{4,116},{5,3},{6,118},{7,5},{8,120},{... | collective-permute-start | bytes 344072 | tf_op jit(solution)/shard_map/ppermute | solution.py:218
  144.5 8.8 %collective-permute-start.25 = (bf16[8,7168]{1,0:T(8,128)(2,1)S(1)}, bf16[8,7168]{1,0:T(8,128)(2,1)S(1)}, u32[]{:S(2)}, u32[]{:S(2)}) collective-permute-start(bf16[8,7168]{1,0:T(8,128)(2,1)S(1)} %get-tuple-element.55), channel_id=1, source_target_pairs={{0,16},{1,3},{2,18},{3,5},{4,20},{5,7},{6,22},{7,9},{8,24},{9,11},... | collective-permute-start | bytes 344072 | tf_op jit(solution)/shard_map/ppermute | solution.py:218
  146.5 8.8 %collective-permute-start.26 = (bf16[8,7168]{1,0:T(8,128)(2,1)S(1)}, bf16[8,7168]{1,0:T(8,128)(2,1)S(1)}, u32[]{:S(2)}, u32[]{:S(2)}) collective-permute-start(bf16[8,7168]{1,0:T(8,128)(2,1)S(1)} %get-tuple-element.56), channel_id=1, source_target_pairs={{0,96},{1,13},{2,98},{3,15},{4,100},{5,1},{6,102},{7,3},{8,104},{9... | collective-permute-start | bytes 344072 | tf_op jit(solution)/shard_map/ppermute | solution.py:218
  146.5 8.8 %collective-permute-start.27 = (bf16[8,7168]{1,0:T(8,128)(2,1)S(1)}, bf16[8,7168]{1,0:T(8,128)(2,1)S(1)}, u32[]{:S(2)}, u32[]{:S(2)}) collective-permute-start(bf16[8,7168]{1,0:T(8,128)(2,1)S(1)} %get-tuple-element.57), channel_id=1, source_target_pairs={{0,32},{1,5},{2,34},{3,7},{4,36},{5,9},{6,38},{7,11},{8,40},{9,13}... | collective-permute-start | bytes 344072 | tf_op jit(solution)/shard_map/ppermute | solution.py:218
  149.4 6.8 %collective-permute-start.28 = (bf16[8,7168]{1,0:T(8,128)(2,1)S(1)}, bf16[8,7168]{1,0:T(8,128)(2,1)S(1)}, u32[]{:S(2)}, u32[]{:S(2)}) collective-permute-start(bf16[8,7168]{1,0:T(8,128)(2,1)S(1)} %get-tuple-element.58), channel_id=1, source_target_pairs={{0,80},{1,11},{2,82},{3,13},{4,84},{5,15},{6,86},{7,1},{8,88},{9,3... | collective-permute-start | bytes 344072 | tf_op jit(solution)/shard_map/ppermute | solution.py:218
  150.2 10.4 %collective-permute-start.29 = (bf16[8,7168]{1,0:T(8,128)(2,1)S(1)}, bf16[8,7168]{1,0:T(8,128)(2,1)S(1)}, u32[]{:S(2)}, u32[]{:S(2)}) collective-permute-start(bf16[8,7168]{1,0:T(8,128)(2,1)S(1)} %get-tuple-element.59), channel_id=1, source_target_pairs={{0,48},{1,7},{2,50},{3,9},{4,52},{5,11},{6,54},{7,13},{8,56},{9,15... | collective-permute-start | bytes 344072 | tf_op jit(solution)/shard_map/ppermute | solution.py:218
  153.3 8.7 %collective-permute-start.30 = (bf16[8,7168]{1,0:T(8,128)(2,1)S(1)}, bf16[8,7168]{1,0:T(8,128)(2,1)S(1)}, u32[]{:S(2)}, u32[]{:S(2)}) collective-permute-start(bf16[8,7168]{1,0:T(8,128)(2,1)S(1)} %get-tuple-element.60), channel_id=1, source_target_pairs={{0,64},{1,9},{2,66},{3,11},{4,68},{5,13},{6,70},{7,15},{8,72},{9,1... | collective-permute-start | bytes 344072 | tf_op jit(solution)/shard_map/ppermute | solution.py:218

commit v6 on v5

--- a/solution.py
+++ b/solution.py
@@ -235,11 +235,12 @@
         [V((toks, width + INFO), bf16)],
     )
     rows = [crossed(r, n, 1, 1) for n, r in enumerate(rows)]
-    gate, up, down = call(
+    weights = [gate_proj, gate_peer, up_proj, up_peer, down_proj, down_peer]
+    weights = call(
         load_kernel,
-        [(w, A) for w in (gate_proj, up_proj, down_proj)],
-        [(w.shape, bf16, V) for w in (gate_proj, up_proj, down_proj)],
-        [pltpu.SemaphoreType.DMA((3,))],
+        [(w, A) for w in weights],
+        [(w.shape, bf16, V) for w in weights],
+        [pltpu.SemaphoreType.DMA((len(weights),))],
     )
 
     near = side // 2 + 1
@@ -248,7 +249,7 @@
         done = call(
             functools.partial(expert_kernel, count=count),
             [(rows[n], V) for n in blocks_here]
-            + [(w, V) for w in (gate, gate_peer, up, up_peer, down, down_peer)],
+            + [(w, V) for w in weights],
             [((each, width), bf16, V)] * count,
             [
                 V((count * each, 4 * part), f32),

time: 165 us -> 153 us (0.927); the launches traced: 163 us -> 152 us
  waiting for transfers between devices: 59.1 us -> 51.2 us
  Pallas kernels: 23.9 us -> 18.7 us
  starting transfers between devices: 78.9 us -> 81.9 us
    ppermute x28, waiting for transfers between devices: 59.1 us -> 51.2 us  [crossed(): return lax.ppermute(rows, GROUP, route_pairs(side, sign * order[n], stage))]
    pallas_call x7, Pallas kernels: 23.9 us -> 18.7 us  [call(): pl.pallas_call(kernel, in_specs=[pl.BlockSpec(memory_space=V if space is...]
    ppermute x28, starting transfers between devices: 78.4 us -> 81.4 us  [crossed(): return lax.ppermute(rows, GROUP, route_pairs(side, sign * order[n], stage))]
  transfers between devices with their start and end apart: 31 -> 31, of which waited for: 14 -> 12; matrix products, arithmetic and copies ran while one was open for 0% -> 0% of each run, Pallas kernels for 14% -> 11%
where the time goes in v6:
time: 153 us; the launch traced here: 152 us
  starting transfers between devices  81.9 us (54%)
  waiting for transfers between devices  51.2 us (33%)
  Pallas kernels  18.7 us (12%)
    ppermute x28, starting transfers between devices, crossed(): return lax.ppermute(rows, GROUP, route_pairs(side, sign * order[n], stage))  81.4 us
    ppermute x28, waiting for transfers between devices, crossed(): return lax.ppermute(rows, GROUP, route_pairs(side, sign * order[n], stage))  51.2 us
    pallas_call x7, Pallas kernels, call(): pl.pallas_call(kernel, in_specs=[pl.BlockSpec(memory_space=V if space is...  18.7 us
  transfers between devices with their start and end apart: 31, of which 12 were waited for; matrix products, arithmetic and copies ran while one was open for 0% of the time, Pallas kernels for 11%

profile of v6, /device:TPU:514, one launch (start us, length us, event | category | flops | bytes accessed | tf_op | source)
XLA Modules:
  0.0 152.5 jit_solution(12199354567564930149)
XLA Ops:
  0.0 0.0 collective-permute-start.11
  0.0 0.5 collective-permute-start.12
  0.5 0.9 shard_map.73.refs_0_
  1.4 10.7 %collective-permute-start.6 = (bf16[8,7424]{1,0:T(8,128)(2,1)S(1)}, bf16[8,7424]{1,0:T(8,128)(2,1)S(1)}, u32[]{:S(2)}, u32[]{:S(2)}) collective-permute-start(bf16[8,7424]{1,0:T(8,128)(2,1)S(1)} %shard_map.73.refs_0_), channel_id=1, source_target_pairs={{0,64},{1,9},{2,66},{3,11},{4,68},{5,13},{6,70},{7,15},{8,72},{9,1... | collective-permute-start | bytes 356360 | tf_op jit(solution)/shard_map/ppermute | solution.py:218
  12.2 0.6 collective-permute-start.5
  12.7 3.1 %collective-permute-done.6.refs_7_ = bf16[8,7424]{1,0:T(8,128)(2,1)S(1)} collective-permute-done((bf16[8,7424]{1,0:T(8,128)(2,1)S(1)}, bf16[8,7424]{1,0:T(8,128)(2,1)S(1)}, u32[]{:S(2)}, u32[]{:S(2)}) %collective-permute-start.6) | collective-permute-done | bytes 118816 | tf_op jit(solution)/shard_map/ppermute | solution.py:218
  15.9 3.7 %collective-permute-start.4 = (bf16[8,7424]{1,0:T(8,128)(2,1)S(1)}, bf16[8,7424]{1,0:T(8,128)(2,1)S(1)}, u32[]{:S(2)}, u32[]{:S(2)}) collective-permute-start(bf16[8,7424]{1,0:T(8,128)(2,1)S(1)} %shard_map.73.refs_0_), channel_id=1, source_target_pairs={{0,48},{1,7},{2,50},{3,9},{4,52},{5,11},{6,54},{7,13},{8,56},{9,15... | collective-permute-start | bytes 356360 | tf_op jit(solution)/shard_map/ppermute | solution.py:218
  19.5 3.9 %collective-permute-done.5.refs_6_ = bf16[8,7424]{1,0:T(8,128)(2,1)S(1)} collective-permute-done((bf16[8,7424]{1,0:T(8,128)(2,1)S(1)}, bf16[8,7424]{1,0:T(8,128)(2,1)S(1)}, u32[]{:S(2)}, u32[]{:S(2)}) %collective-permute-start.5) | collective-permute-done | bytes 118816 | tf_op jit(solution)/shard_map/ppermute | solution.py:218
  23.4 1.0 collective-permute-start.3
  24.5 0.0 collective-permute-done.4.refs_5_
  24.5 4.8 %collective-permute-start.2 = (bf16[8,7424]{1,0:T(8,128)(2,1)S(1)}, bf16[8,7424]{1,0:T(8,128)(2,1)S(1)}, u32[]{:S(2)}, u32[]{:S(2)}) collective-permute-start(bf16[8,7424]{1,0:T(8,128)(2,1)S(1)} %shard_map.73.refs_0_), channel_id=1, source_target_pairs={{0,32},{1,5},{2,34},{3,7},{4,36},{5,9},{6,38},{7,11},{8,40},{9,13}... | collective-permute-start | bytes 356360 | tf_op jit(solution)/shard_map/ppermute | solution.py:218
  29.3 0.1 collective-permute-done.3.refs_4_
  29.4 3.4 %collective-permute-start.1 = (bf16[8,7424]{1,0:T(8,128)(2,1)S(1)}, bf16[8,7424]{1,0:T(8,128)(2,1)S(1)}, u32[]{:S(2)}, u32[]{:S(2)}) collective-permute-start(bf16[8,7424]{1,0:T(8,128)(2,1)S(1)} %shard_map.73.refs_0_), channel_id=1, source_target_pairs={{0,112},{1,15},{2,114},{3,1},{4,116},{5,3},{6,118},{7,5},{8,120},{... | collective-permute-start | bytes 356360 | tf_op jit(solution)/shard_map/ppermute | solution.py:218
  32.8 3.4 %collective-permute-done.2.refs_3_ = bf16[8,7424]{1,0:T(8,128)(2,1)S(1)} collective-permute-done((bf16[8,7424]{1,0:T(8,128)(2,1)S(1)}, bf16[8,7424]{1,0:T(8,128)(2,1)S(1)}, u32[]{:S(2)}, u32[]{:S(2)}) %collective-permute-start.2) | collective-permute-done | bytes 118816 | tf_op jit(solution)/shard_map/ppermute | solution.py:218
  36.2 0.7 broadcast_select_fusion.experts_ref
  36.9 5.4 %collective-permute-done.refs_1_ = bf16[8,7424]{1,0:T(8,128)(2,1)S(1)} collective-permute-done((bf16[8,7424]{1,0:T(8,128)(2,1)S(1)}, bf16[8,7424]{1,0:T(8,128)(2,1)S(1)}, u32[]{:S(2)}, u32[]{:S(2)}) %collective-permute-start) | collective-permute-done | bytes 118816 | tf_op jit(solution)/shard_map/ppermute | solution.py:218
  42.2 1.6 %shard_map.74 = (bf16[24,7168]{1,0:T(8,128)(2,1)S(1)}, bf16[24,7168]{1,0:T(8,128)(2,1)S(1)}, bf16[24,7168]{1,0:T(8,128)(2,1)S(1)}, bf16[24,7168]{1,0:T(8,128)(2,...) custom-call(s32[8]{0:T(128)S(1)} %broadcast_select_fusion.experts_re, ...), custom_call_target="tpu_custom_call" | custom-call | tf_op jit(solution)/shard_map/pallas_call | solution.py:52
  43.8 1.7 %collective-permute-start.7 = (bf16[24,7168]{1,0:T(8,128)(2,1)S(1)}, bf16[24,7168]{1,0:T(8,128)(2,1)S(1)}, u32[]{:S(2)}, u32[]{:S(2)}) collective-permute-start(bf16[24,7168]{1,0:T(8,128)(2,1)S(1)} %get-tuple-element.38), channel_id=1, source_target_pairs={{0,2},{1,17},{2,4},{3,19},{4,6},{5,21},{6,8},{7,23},{8,10},{9,25},... | collective-permute-start | bytes 1032200 | tf_op jit(solution)/shard_map/ppermute | solution.py:218
  45.6 10.1 %collective-permute-start.8 = (bf16[24,7168]{1,0:T(8,128)(2,1)S(1)}, bf16[24,7168]{1,0:T(8,128)(2,1)S(1)}, u32[]{:S(2)}, u32[]{:S(2)}) collective-permute-start(bf16[24,7168]{1,0:T(8,128)(2,1)S(1)} %get-tuple-element.39), channel_id=1, source_target_pairs={{0,14},{1,113},{2,0},{3,115},{4,2},{5,117},{6,4},{7,119},{8,6},{9,... | collective-permute-start | bytes 1032200 | tf_op jit(solution)/shard_map/ppermute | solution.py:218
  55.7 4.1 %collective-permute-start.10 = (bf16[24,7168]{1,0:T(8,128)(2,1)S(1)}, bf16[24,7168]{1,0:T(8,128)(2,1)S(1)}, u32[]{:S(2)}, u32[]{:S(2)}) collective-permute-start(bf16[24,7168]{1,0:T(8,128)(2,1)S(1)} %get-tuple-element.41), channel_id=1, source_target_pairs={{0,12},{1,97},{2,14},{3,99},{4,0},{5,101},{6,2},{7,103},{8,4},{9,1... | collective-permute-start | bytes 1032200 | tf_op jit(solution)/shard_map/ppermute | solution.py:218
  59.9 0.0 collective-permute-start.18
  59.9 7.4 %shard_map.75 = (bf16[1,7168,256]{2,1,0:T(8,128)(2,1)S(1)}, bf16[1,7168,256]{2,1,0:T(8,128)(2,1)S(1)}, bf16[1,7168,256]{2,1,0:T(8,128)(2,1)S(1)}, bf16[1,7168,25...) custom-call(bf16[1,7168,256]{2,1,0:T(8,128)(2,1)} %refs_0_.1, ...), custom_call_target="tpu_custom_call" | custom-call | tf_op jit(solution)/shard_map/pallas_call | solution.py:52
  67.3 5.1 %collective-permute-start.19 = (bf16[24,7168]{1,0:T(8,128)(2,1)S(1)}, bf16[24,7168]{1,0:T(8,128)(2,1)S(1)}, u32[]{:S(2)}, u32[]{:S(2)}) collective-permute-start(bf16[24,7168]{1,0:T(8,128)(2,1)S(1)} %get-tuple-element.54), channel_id=1, source_target_pairs={{0,10},{1,81},{2,12},{3,83},{4,14},{5,85},{6,0},{7,87},{8,2},{9,89... | collective-permute-start | bytes 1032200 | tf_op jit(solution)/shard_map/ppermute | solution.py:218
  72.4 2.7 %collective-permute-start.20 = (bf16[24,7168]{1,0:T(8,128)(2,1)S(1)}, bf16[24,7168]{1,0:T(8,128)(2,1)S(1)}, u32[]{:S(2)}, u32[]{:S(2)}) collective-permute-start(bf16[24,7168]{1,0:T(8,128)(2,1)S(1)} %get-tuple-element.55), channel_id=1, source_target_pairs={{0,8},{1,65},{2,10},{3,67},{4,12},{5,69},{6,14},{7,71},{8,0},{9,73... | collective-permute-start | bytes 1032200 | tf_op jit(solution)/shard_map/ppermute | solution.py:218
  75.1 3.1 %shard_map.76 = (bf16[24,7168]{1,0:T(8,128)(2,1)S(1)}, bf16[24,7168]{1,0:T(8,128)(2,1)S(1)}, bf16[24,7168]{1,0:T(8,128)(2,1)S(1)}, bf16[24,7168]{1,0:T(8,128)(2,1)S(1)}, bf16[24,7168]{1,0:T(8,128)(2,1)S(1)}) custom-call(bf16[24,7168]{1,0:T(8,128)(2,1)S(1)} %get-tuple-element.37.refs_0_, bf16[24,7168]{1,0:T(8,128)(2,1)S(1)} %collective-permute-done.7.refs_1_, ...), custom_call_target="tpu_custom_call" | custom-call | tf_op jit(solution)/shard_map/pallas_call | solution.py:52
  78.3 1.4 collective-permute-start.14
  79.7 0.7 collective-permute-start.15
  80.4 0.4 collective-permute-done.18.refs_0_
  80.8 5.7 %collective-permute-start.16 = (bf16[24,7168]{1,0:T(8,128)(2,1)S(1)}, bf16[24,7168]{1,0:T(8,128)(2,1)S(1)}, u32[]{:S(2)}, u32[]{:S(2)}) collective-permute-start(bf16[24,7168]{1,0:T(8,128)(2,1)S(1)} %get-tuple-element.51), channel_id=1, source_target_pairs={{0,12},{1,97},{2,14},{3,99},{4,0},{5,101},{6,2},{7,103},{8,4},{9,1... | collective-permute-start | bytes 1032200 | tf_op jit(solution)/shard_map/ppermute | solution.py:218
  86.5 1.9 %collective-permute-done.19.refs_1_ = bf16[24,7168]{1,0:T(8,128)(2,1)S(1)} collective-permute-done((bf16[24,7168]{1,0:T(8,128)(2,1)S(1)}, bf16[24,7168]{1,0:T(8,128)(2,1)S(1)}, u32[]{:S(2)}, u32[]{:S(2)}) %collective-permute-start.19) | collective-permute-done | bytes 344096 | tf_op jit(solution)/shard_map/ppermute | solution.py:218
  88.3 3.0 %collective-permute-start.17 = (bf16[24,7168]{1,0:T(8,128)(2,1)S(1)}, bf16[24,7168]{1,0:T(8,128)(2,1)S(1)}, u32[]{:S(2)}, u32[]{:S(2)}) collective-permute-start(bf16[24,7168]{1,0:T(8,128)(2,1)S(1)} %get-tuple-element.52), channel_id=1, source_target_pairs={{0,4},{1,33},{2,6},{3,35},{4,8},{5,37},{6,10},{7,39},{8,12},{9,41}... | collective-permute-start | bytes 1032200 | tf_op jit(solution)/shard_map/ppermute | solution.py:218
  91.3 3.1 %collective-permute-done.20.refs_2_ = bf16[24,7168]{1,0:T(8,128)(2,1)S(1)} collective-permute-done((bf16[24,7168]{1,0:T(8,128)(2,1)S(1)}, bf16[24,7168]{1,0:T(8,128)(2,1)S(1)}, u32[]{:S(2)}, u32[]{:S(2)}) %collective-permute-start.20) | collective-permute-done | bytes 344096 | tf_op jit(solution)/shard_map/ppermute | solution.py:218
  94.4 4.0 %shard_map.77 = (bf16[24,7168]{1,0:T(8,128)(2,1)S(1)}, bf16[24,7168]{1,0:T(8,128)(2,1)S(1)}, bf16[24,7168]{1,0:T(8,128)(2,1)S(1)}) custom-call(bf16[24,7168]{1,0:T(8,128)(2,1)S(1)} %collective-permute-done.18.refs_0_, bf16[24,7168]{1,0:T(8,128)(2,1)S(1)} %collective-permute-done.19.refs_1_, bf16[24,7168]{1,0:T(8,128)(2,1)S(1)} %collective-permute-done.20.refs_2_, ...), custom_call_target="tpu_custom_call" | custom-call | tf_op jit(solution)/shard_map/pallas_call | solution.py:52
  98.4 0.1 collective-permute-start.21
  98.6 5.0 %collective-permute-start.22 = (bf16[24,7168]{1,0:T(8,128)(2,1)S(1)}, bf16[24,7168]{1,0:T(8,128)(2,1)S(1)}, u32[]{:S(2)}, u32[]{:S(2)}) collective-permute-start(bf16[24,7168]{1,0:T(8,128)(2,1)S(1)} %get-tuple-element.57), channel_id=1, source_target_pairs={{0,6},{1,49},{2,8},{3,51},{4,10},{5,53},{6,12},{7,55},{8,14},{9,57... | collective-permute-start | bytes 1032200 | tf_op jit(solution)/shard_map/ppermute | solution.py:218
  103.6 4.2 %collective-permute-start.23 = (bf16[24,7168]{1,0:T(8,128)(2,1)S(1)}, bf16[24,7168]{1,0:T(8,128)(2,1)S(1)}, u32[]{:S(2)}, u32[]{:S(2)}) collective-permute-start(bf16[24,7168]{1,0:T(8,128)(2,1)S(1)} %get-tuple-element.58), channel_id=1, source_target_pairs={{0,8},{1,65},{2,10},{3,67},{4,12},{5,69},{6,14},{7,71},{8,0},{9,73... | collective-permute-start | bytes 1032200 | tf_op jit(solution)/shard_map/ppermute | solution.py:218
  107.8 11.8 %collective-permute-done.21.refs_5_ = bf16[24,7168]{1,0:T(8,128)(2,1)S(1)} collective-permute-done((bf16[24,7168]{1,0:T(8,128)(2,1)S(1)}, bf16[24,7168]{1,0:T(8,128)(2,1)S(1)}, u32[]{:S(2)}, u32[]{:S(2)}) %collective-permute-start.21) | collective-permute-done | bytes 344096 | tf_op jit(solution)/shard_map/ppermute | solution.py:218
  119.5 13.1 %collective-permute-done.23.refs_7_ = bf16[24,7168]{1,0:T(8,128)(2,1)S(1)} collective-permute-done((bf16[24,7168]{1,0:T(8,128)(2,1)S(1)}, bf16[24,7168]{1,0:T(8,128)(2,1)S(1)}, u32[]{:S(2)}, u32[]{:S(2)}) %collective-permute-start.23) | collective-permute-done | bytes 344096 | tf_op jit(solution)/shard_map/ppermute | solution.py:218
  132.6 0.9 shard_map.78
  133.5 0.1 collective-permute-start.24
  133.6 2.0 %collective-permute-start.25 = (bf16[8,7168]{1,0:T(8,128)(2,1)S(1)}, bf16[8,7168]{1,0:T(8,128)(2,1)S(1)}, u32[]{:S(2)}, u32[]{:S(2)}) collective-permute-start(bf16[8,7168]{1,0:T(8,128)(2,1)S(1)} %get-tuple-element.61), channel_id=1, source_target_pairs={{0,16},{1,3},{2,18},{3,5},{4,20},{5,7},{6,22},{7,9},{8,24},{9,11},... | collective-permute-start | bytes 344072 | tf_op jit(solution)/shard_map/ppermute | solution.py:218
  135.6 2.9 %collective-permute-start.27 = (bf16[8,7168]{1,0:T(8,128)(2,1)S(1)}, bf16[8,7168]{1,0:T(8,128)(2,1)S(1)}, u32[]{:S(2)}, u32[]{:S(2)}) collective-permute-start(bf16[8,7168]{1,0:T(8,128)(2,1)S(1)} %get-tuple-element.63), channel_id=1, source_target_pairs={{0,32},{1,5},{2,34},{3,7},{4,36},{5,9},{6,38},{7,11},{8,40},{9,13}... | collective-permute-start | bytes 344072 | tf_op jit(solution)/shard_map/ppermute | solution.py:218
  138.6 2.8 %collective-permute-start.28 = (bf16[8,7168]{1,0:T(8,128)(2,1)S(1)}, bf16[8,7168]{1,0:T(8,128)(2,1)S(1)}, u32[]{:S(2)}, u32[]{:S(2)}) collective-permute-start(bf16[8,7168]{1,0:T(8,128)(2,1)S(1)} %get-tuple-element.64), channel_id=1, source_target_pairs={{0,80},{1,11},{2,82},{3,13},{4,84},{5,15},{6,86},{7,1},{8,88},{9,3... | collective-permute-start | bytes 344072 | tf_op jit(solution)/shard_map/ppermute | solution.py:218
  141.4 1.4 collective-permute-start.29
  142.7 3.9 %collective-permute-start.30 = (bf16[8,7168]{1,0:T(8,128)(2,1)S(1)}, bf16[8,7168]{1,0:T(8,128)(2,1)S(1)}, u32[]{:S(2)}, u32[]{:S(2)}) collective-permute-start(bf16[8,7168]{1,0:T(8,128)(2,1)S(1)} %get-tuple-element.66), channel_id=1, source_target_pairs={{0,64},{1,9},{2,66},{3,11},{4,68},{5,13},{6,70},{7,15},{8,72},{9,1... | collective-permute-start | bytes 344072 | tf_op jit(solution)/shard_map/ppermute | solution.py:218
  146.7 1.3 collective-permute-done.28.refs_5_
  148.0 3.8 %collective-permute-done.29.refs_6_ = bf16[8,7168]{1,0:T(8,128)(2,1)S(1)} collective-permute-done((bf16[8,7168]{1,0:T(8,128)(2,1)S(1)}, bf16[8,7168]{1,0:T(8,128)(2,1)S(1)}, u32[]{:S(2)}, u32[]{:S(2)}) %collective-permute-start.29) | collective-permute-done | bytes 114720 | tf_op jit(solution)/shard_map/ppermute | solution.py:218
  151.7 0.8 shard_map.79
  (22 shorter events, 0.1 us)
Async XLA Ops:
  0.0 55.7 %collective-permute-start.11 = (bf16[1,7168,256]{2,1,0:T(8,128)(2,1)}, bf16[1,7168,256]{2,1,0:T(8,128)(2,1)}, u32[]{:S(2)}, u32[]{:S(2)}) collective-permute-start(bf16[1,7168,256]{2,1,0:T(8,128)(2,1)} %refs_0_.1), channel_id=1, source_target_pairs={{0,1},{1,0},{2,3},{3,2},{4,5},{5,4},{6,7},{7,6},{8,9},{9,8},{10,11... | collective-permute-start | bytes 11010056 | tf_op jit(solution)/shard_map/ppermute | solution.py:228
  0.0 55.7 %collective-permute-start.12 = (bf16[1,7168,256]{2,1,0:T(8,128)(2,1)}, bf16[1,7168,256]{2,1,0:T(8,128)(2,1)}, u32[]{:S(2)}, u32[]{:S(2)}) collective-permute-start(bf16[1,7168,256]{2,1,0:T(8,128)(2,1)} %refs_2_.1), channel_id=1, source_target_pairs={{0,1},{1,0},{2,3},{3,2},{4,5},{5,4},{6,7},{7,6},{8,9},{9,8},{10,11... | collective-permute-start | bytes 11010056 | tf_op jit(solution)/shard_map/ppermute | solution.py:228
  0.5 59.3 %collective-permute-start.13 = (bf16[1,256,7168]{2,1,0:T(8,128)(2,1)}, bf16[1,256,7168]{2,1,0:T(8,128)(2,1)}, u32[]{:S(2)}, u32[]{:S(2)}) collective-permute-start(bf16[1,256,7168]{2,1,0:T(8,128)(2,1)} %refs_4_.1), channel_id=1, source_target_pairs={{0,1},{1,0},{2,3},{3,2},{4,5},{5,4},{6,7},{7,6},{8,9},{9,8},{10,11... | collective-permute-start | bytes 11010056 | tf_op jit(solution)/shard_map/ppermute | solution.py:228
  1.4 14.4 %collective-permute-start.6 = (bf16[8,7424]{1,0:T(8,128)(2,1)S(1)}, bf16[8,7424]{1,0:T(8,128)(2,1)S(1)}, u32[]{:S(2)}, u32[]{:S(2)}) collective-permute-start(bf16[8,7424]{1,0:T(8,128)(2,1)S(1)} %shard_map.73.refs_0_), channel_id=1, source_target_pairs={{0,64},{1,9},{2,66},{3,11},{4,68},{5,13},{6,70},{7,15},{8,72},{9,1... | collective-permute-start | bytes 356360 | tf_op jit(solution)/shard_map/ppermute | solution.py:218
  12.2 11.2 %collective-permute-start.5 = (bf16[8,7424]{1,0:T(8,128)(2,1)S(1)}, bf16[8,7424]{1,0:T(8,128)(2,1)S(1)}, u32[]{:S(2)}, u32[]{:S(2)}) collective-permute-start(bf16[8,7424]{1,0:T(8,128)(2,1)S(1)} %shard_map.73.refs_0_), channel_id=1, source_target_pairs={{0,80},{1,11},{2,82},{3,13},{4,84},{5,15},{6,86},{7,1},{8,88},{9,3... | collective-permute-start | bytes 356360 | tf_op jit(solution)/shard_map/ppermute | solution.py:218
  15.9 8.7 %collective-permute-start.4 = (bf16[8,7424]{1,0:T(8,128)(2,1)S(1)}, bf16[8,7424]{1,0:T(8,128)(2,1)S(1)}, u32[]{:S(2)}, u32[]{:S(2)}) collective-permute-start(bf16[8,7424]{1,0:T(8,128)(2,1)S(1)} %shard_map.73.refs_0_), channel_id=1, source_target_pairs={{0,48},{1,7},{2,50},{3,9},{4,52},{5,11},{6,54},{7,13},{8,56},{9,15... | collective-permute-start | bytes 356360 | tf_op jit(solution)/shard_map/ppermute | solution.py:218
  23.4 5.9 %collective-permute-start.3 = (bf16[8,7424]{1,0:T(8,128)(2,1)S(1)}, bf16[8,7424]{1,0:T(8,128)(2,1)S(1)}, u32[]{:S(2)}, u32[]{:S(2)}) collective-permute-start(bf16[8,7424]{1,0:T(8,128)(2,1)S(1)} %shard_map.73.refs_0_), channel_id=1, source_target_pairs={{0,96},{1,13},{2,98},{3,15},{4,100},{5,1},{6,102},{7,3},{8,104},{9... | collective-permute-start | bytes 356360 | tf_op jit(solution)/shard_map/ppermute | solution.py:218
  24.5 11.7 %collective-permute-start.2 = (bf16[8,7424]{1,0:T(8,128)(2,1)S(1)}, bf16[8,7424]{1,0:T(8,128)(2,1)S(1)}, u32[]{:S(2)}, u32[]{:S(2)}) collective-permute-start(bf16[8,7424]{1,0:T(8,128)(2,1)S(1)} %shard_map.73.refs_0_), channel_id=1, source_target_pairs={{0,32},{1,5},{2,34},{3,7},{4,36},{5,9},{6,38},{7,11},{8,40},{9,13}... | collective-permute-start | bytes 356360 | tf_op jit(solution)/shard_map/ppermute | solution.py:218
  29.4 7.5 %collective-permute-start.1 = (bf16[8,7424]{1,0:T(8,128)(2,1)S(1)}, bf16[8,7424]{1,0:T(8,128)(2,1)S(1)}, u32[]{:S(2)}, u32[]{:S(2)}) collective-permute-start(bf16[8,7424]{1,0:T(8,128)(2,1)S(1)} %shard_map.73.refs_0_), channel_id=1, source_target_pairs={{0,112},{1,15},{2,114},{3,1},{4,116},{5,3},{6,118},{7,5},{8,120},{... | collective-permute-start | bytes 356360 | tf_op jit(solution)/shard_map/ppermute | solution.py:218
  36.2 6.0 %collective-permute-start = (bf16[8,7424]{1,0:T(8,128)(2,1)S(1)}, bf16[8,7424]{1,0:T(8,128)(2,1)S(1)}, u32[]{:S(2)}, u32[]{:S(2)}) collective-permute-start(bf16[8,7424]{1,0:T(8,128)(2,1)S(1)} %shard_map.73.refs_0_), channel_id=1, source_target_pairs={{0,16},{1,3},{2,18},{3,5},{4,20},{5,7},{6,22},{7,9},{8,24},{9,11},... | collective-permute-start | bytes 356360 | tf_op jit(solution)/shard_map/ppermute | solution.py:218
  43.8 23.4 %collective-permute-start.7 = (bf16[24,7168]{1,0:T(8,128)(2,1)S(1)}, bf16[24,7168]{1,0:T(8,128)(2,1)S(1)}, u32[]{:S(2)}, u32[]{:S(2)}) collective-permute-start(bf16[24,7168]{1,0:T(8,128)(2,1)S(1)} %get-tuple-element.38), channel_id=1, source_target_pairs={{0,2},{1,17},{2,4},{3,19},{4,6},{5,21},{6,8},{7,23},{8,10},{9,25},... | collective-permute-start | bytes 1032200 | tf_op jit(solution)/shard_map/ppermute | solution.py:218
  45.6 26.8 %collective-permute-start.8 = (bf16[24,7168]{1,0:T(8,128)(2,1)S(1)}, bf16[24,7168]{1,0:T(8,128)(2,1)S(1)}, u32[]{:S(2)}, u32[]{:S(2)}) collective-permute-start(bf16[24,7168]{1,0:T(8,128)(2,1)S(1)} %get-tuple-element.39), channel_id=1, source_target_pairs={{0,14},{1,113},{2,0},{3,115},{4,2},{5,117},{6,4},{7,119},{8,6},{9,... | collective-permute-start | bytes 1032200 | tf_op jit(solution)/shard_map/ppermute | solution.py:218
  55.7 19.4 %collective-permute-start.9 = (bf16[24,7168]{1,0:T(8,128)(2,1)S(1)}, bf16[24,7168]{1,0:T(8,128)(2,1)S(1)}, u32[]{:S(2)}, u32[]{:S(2)}) collective-permute-start(bf16[24,7168]{1,0:T(8,128)(2,1)S(1)} %get-tuple-element.40), channel_id=1, source_target_pairs={{0,4},{1,33},{2,6},{3,35},{4,8},{5,37},{6,10},{7,39},{8,12},{9,41}... | collective-permute-start | bytes 1032200 | tf_op jit(solution)/shard_map/ppermute | solution.py:218
  55.7 19.4 %collective-permute-start.10 = (bf16[24,7168]{1,0:T(8,128)(2,1)S(1)}, bf16[24,7168]{1,0:T(8,128)(2,1)S(1)}, u32[]{:S(2)}, u32[]{:S(2)}) collective-permute-start(bf16[24,7168]{1,0:T(8,128)(2,1)S(1)} %get-tuple-element.41), channel_id=1, source_target_pairs={{0,12},{1,97},{2,14},{3,99},{4,0},{5,101},{6,2},{7,103},{8,4},{9,1... | collective-permute-start | bytes 1032200 | tf_op jit(solution)/shard_map/ppermute | solution.py:218
  59.9 20.9 %collective-permute-start.18 = (bf16[24,7168]{1,0:T(8,128)(2,1)S(1)}, bf16[24,7168]{1,0:T(8,128)(2,1)S(1)}, u32[]{:S(2)}, u32[]{:S(2)}) collective-permute-start(bf16[24,7168]{1,0:T(8,128)(2,1)S(1)} %get-tuple-element.53), channel_id=1, source_target_pairs={{0,6},{1,49},{2,8},{3,51},{4,10},{5,53},{6,12},{7,55},{8,14},{9,57... | collective-permute-start | bytes 1032200 | tf_op jit(solution)/shard_map/ppermute | solution.py:218
  67.3 21.1 %collective-permute-start.19 = (bf16[24,7168]{1,0:T(8,128)(2,1)S(1)}, bf16[24,7168]{1,0:T(8,128)(2,1)S(1)}, u32[]{:S(2)}, u32[]{:S(2)}) collective-permute-start(bf16[24,7168]{1,0:T(8,128)(2,1)S(1)} %get-tuple-element.54), channel_id=1, source_target_pairs={{0,10},{1,81},{2,12},{3,83},{4,14},{5,85},{6,0},{7,87},{8,2},{9,89... | collective-permute-start | bytes 1032200 | tf_op jit(solution)/shard_map/ppermute | solution.py:218
  72.4 22.0 %collective-permute-start.20 = (bf16[24,7168]{1,0:T(8,128)(2,1)S(1)}, bf16[24,7168]{1,0:T(8,128)(2,1)S(1)}, u32[]{:S(2)}, u32[]{:S(2)}) collective-permute-start(bf16[24,7168]{1,0:T(8,128)(2,1)S(1)} %get-tuple-element.55), channel_id=1, source_target_pairs={{0,8},{1,65},{2,10},{3,67},{4,12},{5,69},{6,14},{7,71},{8,0},{9,73... | collective-permute-start | bytes 1032200 | tf_op jit(solution)/shard_map/ppermute | solution.py:218
  78.3 20.3 %collective-permute-start.14 = (bf16[24,7168]{1,0:T(8,128)(2,1)S(1)}, bf16[24,7168]{1,0:T(8,128)(2,1)S(1)}, u32[]{:S(2)}, u32[]{:S(2)}) collective-permute-start(bf16[24,7168]{1,0:T(8,128)(2,1)S(1)} %get-tuple-element.49), channel_id=1, source_target_pairs={{0,14},{1,113},{2,0},{3,115},{4,2},{5,117},{6,4},{7,119},{8,6},{9,... | collective-permute-start | bytes 1032200 | tf_op jit(solution)/shard_map/ppermute | solution.py:218
  79.7 23.9 %collective-permute-start.15 = (bf16[24,7168]{1,0:T(8,128)(2,1)S(1)}, bf16[24,7168]{1,0:T(8,128)(2,1)S(1)}, u32[]{:S(2)}, u32[]{:S(2)}) collective-permute-start(bf16[24,7168]{1,0:T(8,128)(2,1)S(1)} %get-tuple-element.50), channel_id=1, source_target_pairs={{0,2},{1,17},{2,4},{3,19},{4,6},{5,21},{6,8},{7,23},{8,10},{9,25},... | collective-permute-start | bytes 1032200 | tf_op jit(solution)/shard_map/ppermute | solution.py:218
  80.8 27.0 %collective-permute-start.16 = (bf16[24,7168]{1,0:T(8,128)(2,1)S(1)}, bf16[24,7168]{1,0:T(8,128)(2,1)S(1)}, u32[]{:S(2)}, u32[]{:S(2)}) collective-permute-start(bf16[24,7168]{1,0:T(8,128)(2,1)S(1)} %get-tuple-element.51), channel_id=1, source_target_pairs={{0,12},{1,97},{2,14},{3,99},{4,0},{5,101},{6,2},{7,103},{8,4},{9,1... | collective-permute-start | bytes 1032200 | tf_op jit(solution)/shard_map/ppermute | solution.py:218
  88.3 19.4 %collective-permute-start.17 = (bf16[24,7168]{1,0:T(8,128)(2,1)S(1)}, bf16[24,7168]{1,0:T(8,128)(2,1)S(1)}, u32[]{:S(2)}, u32[]{:S(2)}) collective-permute-start(bf16[24,7168]{1,0:T(8,128)(2,1)S(1)} %get-tuple-element.52), channel_id=1, source_target_pairs={{0,4},{1,33},{2,6},{3,35},{4,8},{5,37},{6,10},{7,39},{8,12},{9,41}... | collective-permute-start | bytes 1032200 | tf_op jit(solution)/shard_map/ppermute | solution.py:218
  98.4 21.1 %collective-permute-start.21 = (bf16[24,7168]{1,0:T(8,128)(2,1)S(1)}, bf16[24,7168]{1,0:T(8,128)(2,1)S(1)}, u32[]{:S(2)}, u32[]{:S(2)}) collective-permute-start(bf16[24,7168]{1,0:T(8,128)(2,1)S(1)} %get-tuple-element.56), channel_id=1, source_target_pairs={{0,10},{1,81},{2,12},{3,83},{4,14},{5,85},{6,0},{7,87},{8,2},{9,89... | collective-permute-start | bytes 1032200 | tf_op jit(solution)/shard_map/ppermute | solution.py:218
  98.6 21.0 %collective-permute-start.22 = (bf16[24,7168]{1,0:T(8,128)(2,1)S(1)}, bf16[24,7168]{1,0:T(8,128)(2,1)S(1)}, u32[]{:S(2)}, u32[]{:S(2)}) collective-permute-start(bf16[24,7168]{1,0:T(8,128)(2,1)S(1)} %get-tuple-element.57), channel_id=1, source_target_pairs={{0,6},{1,49},{2,8},{3,51},{4,10},{5,53},{6,12},{7,55},{8,14},{9,57... | collective-permute-start | bytes 1032200 | tf_op jit(solution)/shard_map/ppermute | solution.py:218
  103.6 29.1 %collective-permute-start.23 = (bf16[24,7168]{1,0:T(8,128)(2,1)S(1)}, bf16[24,7168]{1,0:T(8,128)(2,1)S(1)}, u32[]{:S(2)}, u32[]{:S(2)}) collective-permute-start(bf16[24,7168]{1,0:T(8,128)(2,1)S(1)} %get-tuple-element.58), channel_id=1, source_target_pairs={{0,8},{1,65},{2,10},{3,67},{4,12},{5,69},{6,14},{7,71},{8,0},{9,73... | collective-permute-start | bytes 1032200 | tf_op jit(solution)/shard_map/ppermute | solution.py:218
  133.5 7.9 %collective-permute-start.24 = (bf16[8,7168]{1,0:T(8,128)(2,1)S(1)}, bf16[8,7168]{1,0:T(8,128)(2,1)S(1)}, u32[]{:S(2)}, u32[]{:S(2)}) collective-permute-start(bf16[8,7168]{1,0:T(8,128)(2,1)S(1)} %get-tuple-element.60), channel_id=1, source_target_pairs={{0,112},{1,15},{2,114},{3,1},{4,116},{5,3},{6,118},{7,5},{8,120},{... | collective-permute-start | bytes 344072 | tf_op jit(solution)/shard_map/ppermute | solution.py:218
  133.6 9.1 %collective-permute-start.25 = (bf16[8,7168]{1,0:T(8,128)(2,1)S(1)}, bf16[8,7168]{1,0:T(8,128)(2,1)S(1)}, u32[]{:S(2)}, u32[]{:S(2)}) collective-permute-start(bf16[8,7168]{1,0:T(8,128)(2,1)S(1)} %get-tuple-element.61), channel_id=1, source_target_pairs={{0,16},{1,3},{2,18},{3,5},{4,20},{5,7},{6,22},{7,9},{8,24},{9,11},... | collective-permute-start | bytes 344072 | tf_op jit(solution)/shard_map/ppermute | solution.py:218
  135.6 11.0 %collective-permute-start.26 = (bf16[8,7168]{1,0:T(8,128)(2,1)S(1)}, bf16[8,7168]{1,0:T(8,128)(2,1)S(1)}, u32[]{:S(2)}, u32[]{:S(2)}) collective-permute-start(bf16[8,7168]{1,0:T(8,128)(2,1)S(1)} %get-tuple-element.62), channel_id=1, source_target_pairs={{0,96},{1,13},{2,98},{3,15},{4,100},{5,1},{6,102},{7,3},{8,104},{9... | collective-permute-start | bytes 344072 | tf_op jit(solution)/shard_map/ppermute | solution.py:218
  135.6 11.0 %collective-permute-start.27 = (bf16[8,7168]{1,0:T(8,128)(2,1)S(1)}, bf16[8,7168]{1,0:T(8,128)(2,1)S(1)}, u32[]{:S(2)}, u32[]{:S(2)}) collective-permute-start(bf16[8,7168]{1,0:T(8,128)(2,1)S(1)} %get-tuple-element.63), channel_id=1, source_target_pairs={{0,32},{1,5},{2,34},{3,7},{4,36},{5,9},{6,38},{7,11},{8,40},{9,13}... | collective-permute-start | bytes 344072 | tf_op jit(solution)/shard_map/ppermute | solution.py:218
  138.6 9.4 %collective-permute-start.28 = (bf16[8,7168]{1,0:T(8,128)(2,1)S(1)}, bf16[8,7168]{1,0:T(8,128)(2,1)S(1)}, u32[]{:S(2)}, u32[]{:S(2)}) collective-permute-start(bf16[8,7168]{1,0:T(8,128)(2,1)S(1)} %get-tuple-element.64), channel_id=1, source_target_pairs={{0,80},{1,11},{2,82},{3,13},{4,84},{5,15},{6,86},{7,1},{8,88},{9,3... | collective-permute-start | bytes 344072 | tf_op jit(solution)/shard_map/ppermute | solution.py:218
  141.4 10.4 %collective-permute-start.29 = (bf16[8,7168]{1,0:T(8,128)(2,1)S(1)}, bf16[8,7168]{1,0:T(8,128)(2,1)S(1)}, u32[]{:S(2)}, u32[]{:S(2)}) collective-permute-start(bf16[8,7168]{1,0:T(8,128)(2,1)S(1)} %get-tuple-element.65), channel_id=1, source_target_pairs={{0,48},{1,7},{2,50},{3,9},{4,52},{5,11},{6,54},{7,13},{8,56},{9,15... | collective-permute-start | bytes 344072 | tf_op jit(solution)/shard_map/ppermute | solution.py:218
  142.7 9.0 %collective-permute-start.30 = (bf16[8,7168]{1,0:T(8,128)(2,1)S(1)}, bf16[8,7168]{1,0:T(8,128)(2,1)S(1)}, u32[]{:S(2)}, u32[]{:S(2)}) collective-permute-start(bf16[8,7168]{1,0:T(8,128)(2,1)S(1)} %get-tuple-element.66), channel_id=1, source_target_pairs={{0,64},{1,9},{2,66},{3,11},{4,68},{5,13},{6,70},{7,15},{8,72},{9,1... | collective-permute-start | bytes 344072 | tf_op jit(solution)/shard_map/ppermute | solution.py:218
